TPU v7x, 128 devices: a whole 4x4x4 slice. The times are simulated.
128 devices in a mesh: section: 2 (over core), dev: 64 (over x, z, y).
Axes of the slice: x: 4, y: 4, z: 4, core: 2. Of those that a mesh axis runs over, the one named last changes fastest.
Arguments:
- indices: int32 [8192, 32, 8], P(('section', 'dev')), may hold values from 0 to 131071
- pool_len: int32 [32], replicated, may hold values from 1 to 8
- tables: bfloat16 [4194304, 128], P(('section', 'dev')), may hold values from -3 to 3
- w_first: bfloat16 [4096, 4096], P('dev', 'section'), may hold values from -0.09375 to 0.09375
- b_first: bfloat16 [4096], P('section'), may hold values from -3 to 3
- w_out: bfloat16 [4096], P('section'), may hold values from -0.09375 to 0.09375
Outputs:
- logits: float32 [8192], P('dev')
Inputs may be any that keep to these rules, and one draw needn't show every extreme that they name: `indices`: ids of rows of the table named by the second index.
All inputs are finite; a program needn't handle non-finite values.
Results may differ from a plain program's by a relative error of at most 0.0095.
Values may be sent and summed in bfloat16 or wider, within the bound.
No kernel may reach another device: no remote copies, remote signals or barrier semaphores. Data moves between devices by JAX's collectives and lax.ppermute only.
A program may use at most 128 MiB of HBM per device.

v0:
```python
import jax
import jax.numpy as jnp
from jax import lax
from jax.sharding import PartitionSpec as P


def sent_to_all(shard, axis):
    devices = lax.axis_size(axis)
    return lax.all_to_all(
        jnp.broadcast_to(shard[None], (devices, *shard.shape)), axis, 0, 0, tiled=True
    )


def in_order(tiles, dim):
    shape = list(tiles.shape[1:])
    shape[dim] *= tiles.shape[0]
    return jnp.moveaxis(tiles, 0, dim).reshape(shape)


def collect(shard, axis, dim):
    tiles = sent_to_all(shard, axis)
    return in_order(tiles, dim)


def gathered_total(shard, axis):
    return lax.all_gather(shard, axis).sum(0)


def body(indices, pool_len, tables, w_first, b_first, w_out):
    sec_count = lax.axis_size("section")
    dev_count = lax.axis_size("dev")
    devices = sec_count * dev_count
    dev_rows, n_tables, pool_size = indices.shape
    rows_dev, emb_width = tables.shape
    row_split = devices // n_tables
    position = lax.axis_index("section") * dev_count + lax.axis_index("dev")
    table_id = position // row_split
    first_row = position % row_split * rows_dev
    outgoing = jnp.repeat(indices, row_split, axis=1)
    arrived = lax.all_to_all(outgoing, ("section", "dev"), split_axis=1, concat_axis=0, tiled=True)
    all_rows = devices * dev_rows
    wanted = arrived.reshape(all_rows, pool_size) - first_row
    live_slots = jnp.sum(jnp.where(jnp.arange(n_tables) == table_id, pool_len, 0))
    usable = (wanted >= 0) & (wanted < rows_dev) & (jnp.arange(pool_size)[None, :] < live_slots)
    safe_rows = jnp.where(usable, wanted, 0)
    looked = jnp.take(tables, safe_rows, axis=0)
    picked = jnp.where(usable[:, :, None], looked, jnp.zeros((), jnp.bfloat16))
    partial_value = jnp.sum(picked.astype(jnp.float32), axis=1).astype(jnp.bfloat16)
    ordered = jnp.transpose(
        partial_value.reshape(dev_count, sec_count, dev_rows, emb_width), (1, 0, 2, 3)
    )
    received = lax.all_to_all(
        ordered.reshape(devices, dev_rows, emb_width),
        ("section", "dev"),
        split_axis=0,
        concat_axis=0,
        tiled=True,
    )
    summed = jnp.sum(
        received.reshape(n_tables, row_split, dev_rows, emb_width).astype(jnp.float32), axis=1
    )
    features = jnp.transpose(summed.astype(jnp.bfloat16), (1, 0, 2)).reshape(
        dev_rows, n_tables * emb_width
    )
    samples = collect(features, "section", 0)
    whole_weights = lax.all_gather(w_first, "dev", axis=0, tiled=True)
    pre_act = jnp.dot(samples, whole_weights, preferred_element_type=jnp.float32)
    hidden = jnp.maximum(pre_act + b_first.astype(jnp.float32)[None, :], 0.0)
    logit_part = jnp.sum(hidden * w_out.astype(jnp.float32)[None, :], axis=1)
    return gathered_total(logit_part, "section")


def solution(mesh):
    placed = (
        P(("section", "dev"), None, None),
        P(),
        P(("section", "dev"), None),
        P("dev", "section"),
        P("section"),
        P("section"),
    )
    return jax.shard_map(body, mesh=mesh, in_specs=placed, out_specs=P("dev"), check_vma=False)
```

profile of v0, /device:TPU:1, one launch (start us, length us, event | category | flops | bytes accessed | tf_op | source)
XLA Modules:
  0.0 371.6 jit_solution(8074114564195128807)
XLA Ops:
  6.5 0.7 all-gather.4.cloned.1.call-update
  7.3 0.9 broadcast_in_dim.42
  8.2 1.0 reshape.131
  9.2 11.5 %all-to-all-start = ((s32[128,1,512]{2,1,0:T(1,128)}), s32[128,1,512]{2,1,0:T(1,128)S(1)}, u32[]{:S(2)}, u32[]{:S(2)}) async-start(s32[128,1,512]{2,1,0:T(1,128)} %reshape.131), calls=%async_computation | async-start | bytes 524288 | tf_op jit(solution)/shard_map/all_to_all | solution.py:40
  20.7 1.3 fusion.5
  22.0 0.6 iota_compare_fusion
  22.7 8.8 %all-to-all-done = s32[128,1,512]{2,1,0:T(1,128)S(1)} async-done(((s32[128,1,512]{2,1,0:T(1,128)}), s32[128,1,512]{2,1,0:T(1,128)S(1)}, u32[]{:S(2)}, u32[]{:S(2)}) %all-to-all-start) | async-done | bytes 262176 | tf_op jit(solution)/shard_map/all_to_all | solution.py:40
  31.5 0.5 broadcast.117
  32.0 1.3 reduce.3
  34.1 2.6 copy.17
  36.6 3.6 reshape.120
  40.3 0.2 and_and_fusion
  40.5 1.7 copy.14
  42.2 1.7 copy.15
  43.9 222.4 %gather_fusion = bf16[65536,128]{1,0:T(8,128)(2,1)} fusion(bf16[32768,128]{1,0:T(8,128)(2,1)} %param.8, s32[65536]{0:T(1024)S(1)} %broadcast_clamp_fusion), kind=kCustom, calls=%fused_computation | custom fusion | bytes 33816576 | tf_op jit(solution)/shard_map/jit(_take)/gather | solution.py:46
  266.3 46.4 %fusion.1 = bf16[8192,128]{1,0:T(8,128)(2,1)S(1)} fusion(bf16[65536,128]{1,0:T(8,128)(2,1)} %gather_fusion, pred[8192,8]{1,0:T(8,128)(4,1)S(1)} %copy.15, pred[8192,8]{1,0:T(8,128)(4,1)S(1)} %copy.14), kind=kLoop, calls=%fused_computation.3 | loop fusion | flops 24117248 | bytes 19005440 | tf_op jit(solution)/shard_map/reduce_sum | solution.py:48
  312.7 1.5 copy.18
  314.2 4.2 %all-to-all-start.1 = ((bf16[128,64,128]{2,1,0:T(8,128)(2,1)}), bf16[128,64,128]{2,1,0:T(8,128)(2,1)S(1)}, u32[]{:S(2)}, u32[]{:S(2)}) async-start(bf16[128,64,128]{2,1,0:T(8,128)(2,1)} %bitcast.41), calls=%async_computation.1 | async-start | bytes 4194304 | tf_op jit(solution)/shard_map/all_to_all | solution.py:52
  318.4 30.1 %all-to-all-done.1 = bf16[128,64,128]{2,1,0:T(8,128)(2,1)S(1)} async-done(((bf16[128,64,128]{2,1,0:T(8,128)(2,1)}), bf16[128,64,128]{2,1,0:T(8,128)(2,1)S(1)}, u32[]{:S(2)}, u32[]{:S(2)}) %all-to-all-start.1) | async-done | bytes 2097184 | tf_op jit(solution)/shard_map/all_to_all | solution.py:52
  348.5 0.4 bitcast_reduce_fusion
  349.1 5.1 %all_to_all.19 = bf16[2,64,4096]{2,1,0:T(8,128)(2,1)S(1)} all-to-all(bf16[2,64,4096]{2,1,0:T(8,128)(2,1)S(1)} %broadcast_in_dim.49), channel_id=1, replica_groups=mesh['section'=2,'dev'=64] {'section'}, dimensions={0} | all-to-all | bytes 2097152 | tf_op jit(solution)/shard_map/all_to_all | solution.py:9
  354.2 8.2 %fusion.4 = f32[128]{0:T(128)S(1)} fusion(bf16[128,4096]{1,0:T(8,128)(2,1)S(1)} %bitcast.42, bf16[4096,2048]{1,0:T(8,128)(2,1)} %all-gather.4.cloned.1.call-done, f32[2048]{0:T(1024)S(1)} %convert_element_type.5, f32[2048]{0:T(1024)S(1)} %convert_element_type.4), kind=kOutput, calls=%fused_computation.8 | convolution fusion | flops 2148532224 | bytes 17842688 | tf_op jit(solution)/shard_map/dot_general | solution.py:67
  362.4 1.8 all-gather.1
  364.2 0.5 reduce_sum.55
  (17 shorter events, 1.0 us)
Async XLA Ops:
  6.5 347.7 %all-gather.4.cloned.1.call-start = ((), (), s32[]{:S(2)}) async-start(), calls=%async_computation.3 | async-start | bytes 17039360 | tf_op jit(solution)/shard_map/all_gather | solution.py:66
  9.2 22.3 %all-to-all-start = ((s32[128,1,512]{2,1,0:T(1,128)}), s32[128,1,512]{2,1,0:T(1,128)S(1)}, u32[]{:S(2)}, u32[]{:S(2)}) async-start(s32[128,1,512]{2,1,0:T(1,128)} %reshape.131), calls=%async_computation | async-start | bytes 524288 | tf_op jit(solution)/shard_map/all_to_all | solution.py:40
  266.3 52.1 %copy-start = (bf16[2048]{0:T(1024)(128)(2,1)S(1)}, bf16[2048]{0:T(1024)(128)(2,1)}, u32[]{:S(2)}) copy-start(bf16[2048]{0:T(1024)(128)(2,1)} %param.10) | copy-start | bytes 12292
  266.3 52.1 %copy-start.1 = (bf16[2048]{0:T(1024)(128)(2,1)S(1)}, bf16[2048]{0:T(1024)(128)(2,1)}, u32[]{:S(2)}) copy-start(bf16[2048]{0:T(1024)(128)(2,1)} %param.11) | copy-start | bytes 12292
  314.2 34.3 %all-to-all-start.1 = ((bf16[128,64,128]{2,1,0:T(8,128)(2,1)}), bf16[128,64,128]{2,1,0:T(8,128)(2,1)S(1)}, u32[]{:S(2)}, u32[]{:S(2)}) async-start(bf16[128,64,128]{2,1,0:T(8,128)(2,1)} %bitcast.41), calls=%async_computation.1 | async-start | bytes 4194304 | tf_op jit(solution)/shard_map/all_to_all | solution.py:52
Sparse Core Ops, SparseCore 0:
  10.2 107.0 all-gather.3
where the time goes:
time: 372 us
  local copies, waits for them, and re-layouts  237 us (64%)
  other arithmetic  50.9 us (14%)
  waiting for transfers between devices  39.6 us (11%)
  starting transfers between devices  15.7 us (4%)
  between operations  13.6 us (4%)
  matrix products  8.24 us (2%)
  blocking collectives  6.93 us (2%)
    gather x1, local copies, waits for them, and re-layouts, body(): looked = jnp.take(tables, safe_rows, axis=0)  222 us
    reduce_sum x1, other arithmetic, body(): jnp.sum(picked.astype(jnp.float32), axis=1).astype(jnp.bfloat16)  46.4 us
    all_to_all x1, waiting for transfers between devices, body(): lax.all_to_all(ordered.reshape(devices, dev_rows, emb_width), ('section',...  30.1 us
    all_to_all x1, starting transfers between devices, body(): lax.all_to_all(outgoing, ('section', 'dev'), split_axis=1, concat_axis=0,...  11.5 us
    all_to_all x1, waiting for transfers between devices, body(): lax.all_to_all(outgoing, ('section', 'dev'), split_axis=1, concat_axis=0,...  8.81 us
    dot_general x1, matrix products, body(): jnp.dot(samples, whole_weights, preferred_element_type=jnp.float32)  8.24 us
  transfers between devices with their start and end apart: 3, of which 2 were waited for; matrix products, arithmetic and copies ran while one was open for 77% of the time, Pallas kernels for 0%

commit v1 on v0

v1 whole, which is shorter than its diff:
```python
import functools

import jax
import jax.numpy as jnp
from jax import lax
from jax.experimental import pallas as pl
from jax.experimental.pallas import tpu as pltpu
from jax.sharding import PartitionSpec as P

E = 128
ROWS_DEV = 32768
POOL = 8
CHUNK = 64
SLOTS = POOL * CHUNK
DEAD = ROWS_DEV | (8 << 16)
PIECES = 8
TBLK = 4096
SORT8 = (
    (0, 2), (1, 3), (4, 6), (5, 7), (0, 4), (1, 5), (2, 6), (3, 7), (0, 1), (2, 3),
    (4, 5), (6, 7), (2, 4), (3, 5), (1, 4), (3, 6), (1, 2), (3, 4), (5, 6),
)


def prep_body(x_ref, live_ref, list_ref, bag_ref):
    shape = (CHUNK, 128)
    lane = lax.broadcasted_iota(jnp.int32, shape, 1)
    bag = lax.broadcasted_iota(jnp.int32, shape, 0)
    first = ((lane >> 1) & 3) * ROWS_DEV
    live = jnp.broadcast_to(live_ref[...], shape)
    v = []
    for p in range(POOL):
        row = x_ref[p] - first
        ok = (row >= 0) & (row < ROWS_DEV) & (live > p)
        v.append(jnp.where(ok, row, ROWS_DEV))
    for a, b in SORT8:
        v[a], v[b] = jnp.minimum(v[a], v[b]), jnp.maximum(v[a], v[b])
    kept = sum((w < ROWS_DEV).astype(jnp.int32) for w in v)
    cols = [(POOL - kept) * CHUNK + bag]
    cols += [v[2 * k] | (v[2 * k + 1] << 16) for k in range(POOL // 2)]
    size = 2
    while size <= CHUNK:
        step = size // 2
        while step:
            upper = (bag & step) != 0
            small = ((bag & size) == 0) != upper
            other = [
                jnp.where(upper, pltpu.roll(c, step, 0), pltpu.roll(c, CHUNK - step, 0)) for c in cols
            ]
            take = jnp.where(small, other[0] - cols[0], cols[0] - other[0]) < 0
            cols = [jnp.where(take, o, c) for o, c in zip(other, cols)]
            step //= 2
        size *= 2
    key = cols[0]
    bag_ref[...] = (key & (CHUNK - 1)).T
    kept = POOL - (key >> 6)
    v = []
    for w in cols[1:]:
        v += [w & 0xFFFF, lax.shift_right_logical(w, 16)]
    tile = (8, 128)
    groups = []
    total = jnp.zeros((1, 128), jnp.int32)
    for g in range(CHUNK // 8):
        n = kept[8 * g : 8 * g + 1]
        shift = jnp.broadcast_to((8 * g - total) << 20, tile)
        n_all = jnp.broadcast_to(n, tile)
        for p in range(POOL):
            word = v[p][8 * g : 8 * g + 8] | (g << 16) | shift
            groups.append(jnp.where(n_all > p, word, DEAD))
        total = total + n
    for k in range(6):
        gap = 1 << k
        moves = [((w >> (20 + k)) & 1) != 0 for w in groups]
        new = []
        for i in range(64):
            stay = jnp.where(moves[i], DEAD, groups[i])
            if i + gap < 64:
                stay = jnp.where(moves[i + gap], groups[i + gap], stay)
            new.append(stay)
        groups = new
    head = lax.broadcasted_iota(jnp.int32, tile, 0) == 0
    mask = jnp.where(head, 0xFFFFF, 0xFFFF)
    groups = [w & mask for w in groups]
    groups[0] = groups[0] | jnp.where(head, jnp.broadcast_to(total << 20, tile), 0)
    for i in range(4):
        block = jnp.concatenate(groups[16 * i : 16 * i + 16], axis=0)
        list_ref[:, 128 * i : 128 * i + 128] = block.T


def prep(x, live):
    return pl.pallas_call(
        prep_body,
        out_shape=(
            jax.ShapeDtypeStruct((128, SLOTS), jnp.int32),
            jax.ShapeDtypeStruct((128, CHUNK), jnp.int32),
        ),
        name="bag_lists",
    )(x, live)


def gather_body(lists_ref, table_ref, out_ref, tab, tbuf, smem, acc, tsem, lsem, *, unroll):
    chunks = out_ref.shape[0]
    piece = chunks * SLOTS // PIECES

    def list_copy(i):
        part = pl.ds(i * piece, piece)
        return pltpu.make_async_copy(lists_ref.at[part], smem.at[part], lsem.at[i])

    def table_copy(b):
        return pltpu.make_async_copy(
            table_ref.at[pl.ds(b * TBLK, TBLK)], tbuf.at[b % 2], tsem.at[b % 2]
        )

    blocks = ROWS_DEV // TBLK
    table_copy(0).start()
    for i in range(PIECES):
        list_copy(i).start()
    tab[pl.ds(ROWS_DEV, 8), :] = jnp.zeros((8, E), jnp.float32)
    for b in range(blocks):
        if b + 1 < blocks:
            table_copy(b + 1).start()
        table_copy(b).wait()
        tab[pl.ds(b * TBLK, TBLK), :] = tbuf[b % 2].astype(jnp.float32)

    def level(base):
        head = smem[base]
        rows = [head & 0xFFFF] + [smem[base + i] for i in range(1, 8)]
        return (head >> 16) & 15, jnp.concatenate([tab[pl.ds(r, 1), :] for r in rows], axis=0)

    def chunk(c, carry):
        base = c * SLOTS
        acc[...] = jnp.zeros(acc.shape, jnp.float32)
        levels = smem[base] >> 20

        def step(k, carry):
            at = base + k * (8 * unroll)
            for g, rows in [level(at + 8 * u) for u in range(unroll)]:
                acc[pl.ds(pl.multiple_of(g * 8, 8), 8), :] += rows
            return carry

        lax.fori_loop(0, (levels + unroll - 1) // unroll, step, 0)
        out_ref[c] = acc[pl.ds(0, CHUNK), :].astype(jnp.bfloat16)
        return carry

    per = chunks // PIECES
    for i in range(PIECES):
        list_copy(i).wait()
        lax.fori_loop(i * per, (i + 1) * per, chunk, 0)


def gather(lists, table, chunks, unroll=4):
    return pl.pallas_call(
        functools.partial(gather_body, unroll=unroll),
        out_shape=jax.ShapeDtypeStruct((chunks, CHUNK, E), jnp.bfloat16),
        in_specs=[pl.BlockSpec(memory_space=pl.ANY), pl.BlockSpec(memory_space=pl.ANY)],
        out_specs=pl.BlockSpec(memory_space=pltpu.VMEM),
        scratch_shapes=[
            pltpu.VMEM((ROWS_DEV + 8, E), jnp.float32),
            pltpu.VMEM((2, TBLK, E), jnp.bfloat16),
            pltpu.SMEM((chunks * SLOTS,), jnp.int32),
            pltpu.VMEM((CHUNK + 8, E), jnp.float32),
            pltpu.SemaphoreType.DMA((2,)),
            pltpu.SemaphoreType.DMA((PIECES,)),
        ],
        compiler_params=pltpu.CompilerParams(vmem_limit_bytes=32 * 2**20),
        name="bag_gather",
    )(lists, table)


def unsort_body(part_ref, bag_ref, out_ref):
    tables = out_ref.shape[1] // E
    bag = lax.broadcasted_iota(jnp.int32, (CHUNK, 4 * CHUNK), 0)
    for t in range(tables):
        for h in range(2):
            where = bag_ref[2 * t + h : 2 * t + h + 1, :]
            pick = (bag == where).astype(jnp.float32).astype(jnp.bfloat16)
            rows = part_ref[4 * t : 4 * t + 4, h].reshape(4 * CHUNK, E)
            total = jnp.dot(pick, rows, preferred_element_type=jnp.float32)
            out_ref[h * CHUNK : (h + 1) * CHUNK, t * E : (t + 1) * E] = total.astype(jnp.bfloat16)


def unsort(parts, bags):
    return pl.pallas_call(
        unsort_body,
        out_shape=jax.ShapeDtypeStruct((2 * CHUNK, parts.shape[0] // 4 * E), jnp.bfloat16),
        name="bag_unsort",
    )(parts, bags)


def swap(x, axis):
    return lax.all_to_all(jnp.broadcast_to(x[None], (2, *x.shape)), axis, 0, 0, tiled=True)


def body(indices, pool_len, tables, w_first, b_first, w_out):
    n_dev = lax.axis_size("dev")
    n_sec = lax.axis_size("section")
    n_tables = indices.shape[1]
    half = n_tables // n_sec
    section = lax.axis_index("section")
    dev = lax.axis_index("dev")
    ids = jnp.transpose(indices, (1, 2, 0)).reshape(n_sec, half, POOL, CHUNK)
    odd = dev % 2
    own = lax.dynamic_index_in_dim(ids, odd, 0, keepdims=False)
    other = lax.dynamic_index_in_dim(ids, 1 - odd, 0, keepdims=False)
    blocks = range(n_sec * n_dev)
    straight = [(b, (b % 2) * n_dev + b // 2) for b in blocks]
    crossed = [(b, (1 - b % 2) * n_dev + b // 2) for b in blocks]
    same = lax.ppermute(own, ("section", "dev"), straight)
    cross = lax.ppermute(other, ("section", "dev"), crossed)
    low = jnp.where(section == 0, same, cross)
    high = jnp.where(section == 0, cross, same)
    x = jnp.transpose(jnp.stack([low, high]), (2, 3, 1, 0))
    x = jnp.broadcast_to(x[:, :, :, None, :], (POOL, CHUNK, half, 4, 2)).reshape(POOL, CHUNK, 128)
    live = jnp.repeat(lax.dynamic_slice(pool_len, (section * half,), (half,)), 8).reshape(1, 128)
    lists, bags = prep(x, live)
    bags = jnp.transpose(bags.reshape(half, 4, 2, CHUNK), (0, 2, 1, 3)).reshape(2 * half, 4 * CHUNK)
    arrived = lax.all_to_all(lists.reshape(n_dev, 2 * SLOTS), "dev", 0, 0, tiled=True)
    parts = gather(arrived.reshape(-1), tables, 2 * n_dev)
    parts = lax.all_to_all(parts.reshape(n_dev, 2 * CHUNK, E), "dev", 0, 0, tiled=True)
    features = unsort(parts.reshape(n_dev, 2, CHUNK, E), bags)
    both = swap(features, "section")
    samples = jnp.moveaxis(both, 0, 1).reshape(2 * CHUNK, n_tables * E)
    whole_weights = lax.all_gather(w_first, "dev", axis=0, tiled=True)
    pre_act = jnp.dot(samples, whole_weights, preferred_element_type=jnp.float32)
    hidden = jnp.maximum(pre_act + b_first.astype(jnp.float32)[None, :], 0.0)
    logit_part = jnp.sum(hidden * w_out.astype(jnp.float32)[None, :], axis=1)
    return lax.all_gather(logit_part, "section").sum(0)


def solution(mesh):
    placed = (
        P(("section", "dev"), None, None),
        P(),
        P(("section", "dev"), None),
        P("dev", "section"),
        P("section"),
        P("section"),
    )
    return jax.shard_map(body, mesh=mesh, in_specs=placed, out_specs=P("dev"), check_vma=False)
```

time: 372 us -> 166 us (0.45)
  local copies, waits for them, and re-layouts: 237 us -> 12.3 us
  other arithmetic: 50.9 us -> 0.56 us
  blocking collectives: 6.93 us -> 34 us
  Pallas kernels: 0 us -> 20.1 us
  starting transfers between devices: 15.7 us -> 28.2 us
  waiting for transfers between devices: 39.6 us -> 48.8 us
    gather x1 -> x0, local copies, waits for them, and re-layouts: 222 us -> none  [body(): looked = jnp.take(tables, safe_rows, axis=0)]
    reduce_sum x4 -> x1, other arithmetic: 48.6 us -> 0.53 us  [body(): return lax.all_gather(logit_part, 'section').sum(0)]
    all_to_all x1 -> x2, blocking collectives: 5.13 us -> 32.1 us  [the longest x1 25.5 us: body(): lax.all_to_all(lists.reshape(n_dev, 2 * SLOTS), 'dev', 0, 0, tiled=True)]
    pallas_call x0 -> x3, Pallas kernels: none -> 20.1 us  [the longest x1 14.2 us: gather(): pl.pallas_call(functools.partial(gather_body, unroll=unroll), out_shape=j...]
    all_to_all x2 -> x1, waiting for transfers between devices: 38.9 us -> 48.1 us  [body(): lax.all_to_all(parts.reshape(n_dev, 2 * CHUNK, E), 'dev', 0, 0, tiled=True)]
    ppermute x0 -> x2, starting transfers between devices: none -> 7.02 us  [the longest x1 6.03 us: body(): same = lax.ppermute(own, ('section', 'dev'), straight)]
    select_n x2 -> x0, local copies, waits for them, and re-layouts: 6.22 us -> none  [body(): looked = jnp.take(tables, safe_rows, axis=0)]
    all_to_all x2 -> x1, starting transfers between devices: 15.7 us -> 21.2 us  [body(): lax.all_to_all(parts.reshape(n_dev, 2 * CHUNK, E), 'dev', 0, 0, tiled=True)]
  transfers between devices with their start and end apart: 3 -> 4, of which waited for: 2 -> 1; matrix products, arithmetic and copies ran while one was open for 77% -> 4% of each run, Pallas kernels for 0% -> 12%
where the time goes in v1:
time: 166 us
  waiting for transfers between devices  48.8 us (29%)
  blocking collectives  34 us (20%)
  starting transfers between devices  28.2 us (17%)
  Pallas kernels  20.1 us (12%)
  between operations  13.5 us (8%)
  local copies, waits for them, and re-layouts  12.3 us (7%)
  matrix products  8.21 us (5%)
    all_to_all x1, waiting for transfers between devices, body(): lax.all_to_all(parts.reshape(n_dev, 2 * CHUNK, E), 'dev', 0, 0, tiled=True)  48.1 us
    all_to_all x1, blocking collectives, body(): lax.all_to_all(lists.reshape(n_dev, 2 * SLOTS), 'dev', 0, 0, tiled=True)  25.5 us
    all_to_all x1, starting transfers between devices, body(): lax.all_to_all(parts.reshape(n_dev, 2 * CHUNK, E), 'dev', 0, 0, tiled=True)  21.2 us
    pallas_call x1, Pallas kernels, gather(): pl.pallas_call(functools.partial(gather_body, unroll=unroll), out_shape=j...  14.2 us
    dot_general x1, matrix products, body(): jnp.dot(samples, whole_weights, preferred_element_type=jnp.float32)  8.21 us
    all_to_all x1, blocking collectives, swap(): lax.all_to_all(jnp.broadcast_to(x[None], (2, *x.shape)), axis, 0, 0, tile...  6.63 us
    ppermute x1, starting transfers between devices, body(): same = lax.ppermute(own, ('section', 'dev'), straight)  6.03 us
    unnamed x8, local copies, waits for them, and re-layouts  4.84 us
  transfers between devices with their start and end apart: 4, of which 1 were waited for; matrix products, arithmetic and copies ran while one was open for 4% of the time, Pallas kernels for 12%

profile of v1, /device:TPU:1, one launch (start us, length us, event | category | flops | bytes accessed | tf_op | source)
XLA Modules:
  0.0 165.7 jit_solution(10163753051767497100)
XLA Ops:
  6.5 0.7 all-gather.4.cloned.1.call-update
  7.3 0.9 dynamic-slice_bitcast_fusion.1
  8.2 6.0 %collective-permute-start = (s32[16,8,64]{2,1,0:T(8,128)S(1)}, s32[16,8,64]{2,1,0:T(8,128)S(1)}, u32[]{:S(2)}, u32[]{:S(2)}) collective-permute-start(s32[16,8,64]{2,1,0:T(8,128)S(1)} %get-tuple-element.11), channel_id=1, source_target_pairs={{0,0},{1,64},{2,1},{3,65},{4,2},{5,66},{6,3},{7,67},{8,4},{9,68},{... | collective-permute-start | bytes 98312 | tf_op jit(solution)/shard_map/ppermute | solution.py:207
  14.2 1.0 collective-permute-start.1
  15.2 0.7 dynamic_slice.12
  15.9 0.1 broadcast_in_dim.7
  16.0 0.6 reshape_reshape.3.live_ref
  16.7 0.9 copy.14.x_ref
  17.6 3.0 %bag_lists.1 = (s32[128,512]{1,0:T(8,128)}, s32[128,64]{1,0:T(8,128)}) custom-call(s32[8,64,128]{2,1,0:T(8,128)} %copy.14.x_ref, s32[1,128]{1,0:T(1,128)} %reshape_reshape.3.live_ref), custom_call_target="tpu_custom_call" | custom-call | tf_op jit(solution)/shard_map/bag_lists/pallas_call | solution.py:90
  20.7 1.3 all_to_all.16
  21.9 25.5 %all_to_all.20 = s32[64,1,1024]{2,1,0:T(1,128)S(1)} all-to-all(s32[64,1,1024]{2,1,0:T(1,128)S(1)} %all_to_all.16), channel_id=1, replica_groups=mesh['section'=2,'dev'=64] {'dev'}, dimensions={0} | all-to-all | bytes 524288 | tf_op jit(solution)/shard_map/all_to_all | solution.py:216
  47.4 3.5 %copy-done = bf16[32768,128]{1,0:T(8,128)(2,1)S(1)} copy-done((bf16[32768,128]{1,0:T(8,128)(2,1)S(1)}, bf16[32768,128]{1,0:T(8,128)(2,1)}, u32[]{:S(2)}) %copy-start) | copy-done | bytes 8388632
  50.9 14.2 %bag_gather.1 = bf16[128,64,128]{2,1,0:T(8,128)(2,1)} custom-call(s32[65536]{0:T(1024)S(1)} %bitcast.27, bf16[32768,128]{1,0:T(8,128)(2,1)S(1)} %copy-done), custom_call_target="tpu_custom_call" | custom-call | tf_op jit(solution)/shard_map/bag_gather/pallas_call | solution.py:151
  65.2 21.2 %all-to-all-start.1 = ((bf16[64,128,128]{2,1,0:T(8,128)(2,1)}), bf16[64,128,128]{2,1,0:T(8,128)(2,1)S(1)}, u32[]{:S(2)}, u32[]{:S(2)}) async-start(bf16[64,128,128]{2,1,0:T(8,128)(2,1)} %bitcast.10), calls=%async_computation.1 | async-start | bytes 4194304 | tf_op jit(solution)/shard_map/all_to_all | solution.py:218
  86.4 0.9 copy.19
  87.3 0.7 reshape.39.bag_ref
  88.0 48.1 %all-to-all-done.1 = bf16[64,128,128]{2,1,0:T(8,128)(2,1)S(1)} async-done(((bf16[64,128,128]{2,1,0:T(8,128)(2,1)}), bf16[64,128,128]{2,1,0:T(8,128)(2,1)S(1)}, u32[]{:S(2)}, u32[]{:S(2)}) %all-to-all-start.1) | async-done | bytes 2097184 | tf_op jit(solution)/shard_map/all_to_all | solution.py:218
  136.1 1.3 copy-done.1
  137.4 2.9 %bag_unsort.1 = bf16[128,2048]{1,0:T(8,128)(2,1)} custom-call(bf16[64,2,64,128]{3,2,1,0:T(8,128)(2,1)} %bitcast.28, s32[32,256]{1,0:T(8,128)} %reshape.39.bag_ref), custom_call_target="tpu_custom_call" | custom-call | tf_op jit(solution)/shard_map/bag_unsort/pallas_call | solution.py:182
  140.3 1.3 copy.17
  141.7 6.6 %all_to_all.21 = bf16[2,128,2048]{1,2,0:T(8,128)(2,1)S(1)} all-to-all(bf16[2,128,2048]{1,2,0:T(8,128)(2,1)S(1)} %broadcast_in_dim.8), channel_id=1, replica_groups=mesh['section'=2,'dev'=64] {'section'}, dimensions={0} | all-to-all | bytes 2097152 | tf_op jit(solution)/shard_map/all_to_all | solution.py:190
  148.3 8.2 %fusion.2 = f32[128]{0:T(128)S(1)} fusion(bf16[128,4096]{0,1:T(8,128)(2,1)S(1)} %bitcast.29, bf16[4096,2048]{1,0:T(8,128)(2,1)} %all-gather.4.cloned.1.call-done, f32[2048]{0:T(1024)S(1)} %convert_element_type.7, f32[2048]{0:T(1024)S(1)} %convert_element_type.6), kind=kOutput, calls=%fused_computation.3 | convolution fusion | flops 2148532224 | bytes 17842688 | tf_op jit(solution)/shard_map/dot_general | solution.py:223
  156.5 1.8 %all-gather.1 = f32[2,1,128]{2,1,0:T(1,128)S(1)} all-gather(f32[1,1,128]{2,1,0:T(1,128)S(1)} %bitcast.34), channel_id=2, replica_groups=mesh['section'=2,'dev'=64] {'section'}, dimensions={0}, use_global_device_ids=true | all-gather | bytes 1536 | tf_op jit(solution)/shard_map/all_gather | solution.py:226
  158.3 0.5 reduce_sum.19
  (17 shorter events, 0.2 us)
Async XLA Ops:
  6.5 79.8 %copy-start.2 = (bf16[2048]{0:T(1024)(128)(2,1)S(1)}, bf16[2048]{0:T(1024)(128)(2,1)}, u32[]{:S(2)}) copy-start(bf16[2048]{0:T(1024)(128)(2,1)} %param.10) | copy-start | bytes 12292
  6.5 79.8 %copy-start.3 = (bf16[2048]{0:T(1024)(128)(2,1)S(1)}, bf16[2048]{0:T(1024)(128)(2,1)}, u32[]{:S(2)}) copy-start(bf16[2048]{0:T(1024)(128)(2,1)} %param.11) | copy-start | bytes 12292
  6.5 141.7 %all-gather.4.cloned.1.call-start = ((), (), s32[]{:S(2)}) async-start(), calls=%async_computation.3 | async-start | bytes 17039360 | tf_op jit(solution)/shard_map/all_gather | solution.py:222
  8.2 8.4 %collective-permute-start = (s32[16,8,64]{2,1,0:T(8,128)S(1)}, s32[16,8,64]{2,1,0:T(8,128)S(1)}, u32[]{:S(2)}, u32[]{:S(2)}) collective-permute-start(s32[16,8,64]{2,1,0:T(8,128)S(1)} %get-tuple-element.11), channel_id=1, source_target_pairs={{0,0},{1,64},{2,1},{3,65},{4,2},{5,66},{6,3},{7,67},{8,4},{9,68},{... | collective-permute-start | bytes 98312 | tf_op jit(solution)/shard_map/ppermute | solution.py:207
  14.2 2.4 %collective-permute-start.1 = (s32[16,8,64]{2,1,0:T(8,128)S(1)}, s32[16,8,64]{2,1,0:T(8,128)S(1)}, u32[]{:S(2)}, u32[]{:S(2)}) collective-permute-start(s32[16,8,64]{2,1,0:T(8,128)S(1)} %get-tuple-element.12), channel_id=1, source_target_pairs={{0,64},{1,0},{2,65},{3,1},{4,66},{5,2},{6,67},{7,3},{8,68},{9,4},{... | collective-permute-start | bytes 98312 | tf_op jit(solution)/shard_map/ppermute | solution.py:208
  47.4 3.5 %copy-start = (bf16[32768,128]{1,0:T(8,128)(2,1)S(1)}, bf16[32768,128]{1,0:T(8,128)(2,1)}, u32[]{:S(2)}) copy-start(bf16[32768,128]{1,0:T(8,128)(2,1)} %table_ref.1) | copy-start | bytes 25165828
  65.2 70.9 %all-to-all-start.1 = ((bf16[64,128,128]{2,1,0:T(8,128)(2,1)}), bf16[64,128,128]{2,1,0:T(8,128)(2,1)S(1)}, u32[]{:S(2)}, u32[]{:S(2)}) async-start(bf16[64,128,128]{2,1,0:T(8,128)(2,1)} %bitcast.10), calls=%async_computation.1 | async-start | bytes 4194304 | tf_op jit(solution)/shard_map/all_to_all | solution.py:218
  136.1 1.3 copy-start.1
Sparse Core Ops, SparseCore 0:
  10.2 129.4 all-gather.3

commit v2 on v1

--- a/solution.py
+++ b/solution.py
@@ -15,6 +15,7 @@
 DEAD = ROWS_DEV | (8 << 16)
 PIECES = 8
 TBLK = 4096
+HID_SPLIT = 2
 SORT8 = (
     (0, 2), (1, 3), (4, 6), (5, 7), (0, 4), (1, 5), (2, 6), (3, 7), (0, 1), (2, 3),
     (4, 5), (6, 7), (2, 4), (3, 5), (1, 4), (3, 6), (1, 2), (3, 4), (5, 6),
@@ -217,13 +218,28 @@
     parts = gather(arrived.reshape(-1), tables, 2 * n_dev)
     parts = lax.all_to_all(parts.reshape(n_dev, 2 * CHUNK, E), "dev", 0, 0, tiled=True)
     features = unsort(parts.reshape(n_dev, 2, CHUNK, E), bags)
-    both = swap(features, "section")
-    samples = jnp.moveaxis(both, 0, 1).reshape(2 * CHUNK, n_tables * E)
-    whole_weights = lax.all_gather(w_first, "dev", axis=0, tiled=True)
-    pre_act = jnp.dot(samples, whole_weights, preferred_element_type=jnp.float32)
-    hidden = jnp.maximum(pre_act + b_first.astype(jnp.float32)[None, :], 0.0)
-    logit_part = jnp.sum(hidden * w_out.astype(jnp.float32)[None, :], axis=1)
-    return lax.all_gather(logit_part, "section").sum(0)
+    ring = 4
+    rows, cols = w_first.shape
+    part = cols // HID_SPLIT
+    planes = n_dev // ring
+    rings = [[ring * p + y for y in range(ring)] for p in range(planes)]
+    levels = [[ring * p + y for p in range(planes)] for y in range(ring)]
+    pieces = jnp.moveaxis(w_first.reshape(rows, HID_SPLIT, part), 1, 0)
+    pieces = jnp.concatenate([pieces] * (ring // HID_SPLIT))
+    mine = lax.all_to_all(pieces, "dev", 0, 0, axis_index_groups=rings, tiled=True)
+    whole = lax.all_gather(mine.reshape(ring * rows, part), "dev", axis_index_groups=levels, tiled=True)
+    q = dev % HID_SPLIT
+    bias = lax.dynamic_slice(b_first, (q * part,), (part,)).astype(jnp.float32)
+    scale = lax.dynamic_slice(w_out, (q * part,), (part,)).astype(jnp.float32)
+    pairs = [(d, d ^ 1) for d in range(n_dev)]
+    shared = jnp.stack([features, lax.ppermute(features, "dev", pairs)])
+    both = swap(shared, "section")
+    samples = jnp.moveaxis(both, 0, 2).reshape(HID_SPLIT * 2 * CHUNK, n_tables * E)
+    pre_act = jnp.dot(samples, whole, preferred_element_type=jnp.float32)
+    hidden = jnp.maximum(pre_act + bias[None, :], 0.0)
+    logit_part = jnp.sum(hidden * scale[None, :], axis=1).reshape(HID_SPLIT, 2 * CHUNK)
+    total = logit_part[0] + lax.ppermute(logit_part[1], "dev", pairs)
+    return lax.all_gather(total, "section").sum(0)
 
 
 def solution(mesh):

time: 166 us -> 174 us (1.048)
  Pallas kernels: 20.1 us -> 36.6 us
  blocking collectives: 34 us -> 49.9 us
  starting transfers between devices: 28.2 us -> 14.1 us
  waiting for transfers between devices: 48.8 us -> 37.9 us
  matrix products: 8.21 us -> 5.85 us
    all_to_all x1, waiting for transfers between devices: 48.1 us -> 26.3 us  [body(): lax.all_to_all(parts.reshape(n_dev, 2 * CHUNK, E), 'dev', 0, 0, tiled=True)]
    pallas_call x1, Pallas kernels: 14.2 us -> 30.7 us  [gather(): pl.pallas_call(functools.partial(gather_body, unroll=unroll), out_shape=j...]
    all_to_all x1, starting transfers between devices: 21.2 us -> 5.14 us  [body(): lax.all_to_all(parts.reshape(n_dev, 2 * CHUNK, E), 'dev', 0, 0, tiled=True)]
    all_to_all x0 -> x1, blocking collectives: none -> 13.5 us  [body(): lax.all_to_all(pieces, 'dev', 0, 0, axis_index_groups=rings, tiled=True)]
    ppermute x0 -> x2, waiting for transfers between devices: none -> 11 us  [the longest x1 9.4 us: body(): shared = jnp.stack([features, lax.ppermute(features, 'dev', pairs)])]
    all_to_all x1, blocking collectives: 6.63 us -> 9.46 us  [swap(): lax.all_to_all(jnp.broadcast_to(x[None], (2, *x.shape)), axis, 0, 0, tile...]
    dot_general x1, matrix products: 8.21 us -> 5.85 us  [body(): pre_act = jnp.dot(samples, whole, preferred_element_type=jnp.float32)]
    transpose x0 -> x1, local copies, waits for them, and re-layouts: none -> 2.16 us  [body(): jnp.moveaxis(both, 0, 2).reshape(HID_SPLIT * 2 * CHUNK, n_tables * E)]
  transfers between devices with their start and end apart: 4 -> 6, of which waited for: 1 -> 4; matrix products, arithmetic and copies ran while one was open for 4% -> 4% of each run, Pallas kernels for 12% -> 21%
where the time goes in v2:
time: 174 us; the launch traced here: 173 us
  blocking collectives  49.9 us (29%)
  waiting for transfers between devices  37.9 us (22%)
  Pallas kernels  36.6 us (21%)
  starting transfers between devices  14.1 us (8%)
  between operations  13.6 us (8%)
  local copies, waits for them, and re-layouts  13.2 us (8%)
  matrix products  5.85 us (3%)
  other arithmetic  2.18 us (1%)
    pallas_call x1, Pallas kernels, gather(): pl.pallas_call(functools.partial(gather_body, unroll=unroll), out_shape=j...  30.7 us
    all_to_all x1, waiting for transfers between devices, body(): lax.all_to_all(parts.reshape(n_dev, 2 * CHUNK, E), 'dev', 0, 0, tiled=True)  26.3 us
    all_to_all x1, blocking collectives, body(): lax.all_to_all(lists.reshape(n_dev, 2 * SLOTS), 'dev', 0, 0, tiled=True)  24 us
    all_to_all x1, blocking collectives, body(): lax.all_to_all(pieces, 'dev', 0, 0, axis_index_groups=rings, tiled=True)  13.5 us
    all_to_all x1, blocking collectives, swap(): lax.all_to_all(jnp.broadcast_to(x[None], (2, *x.shape)), axis, 0, 0, tile...  9.46 us
    ppermute x1, waiting for transfers between devices, body(): shared = jnp.stack([features, lax.ppermute(features, 'dev', pairs)])  9.4 us
    ppermute x1, starting transfers between devices, body(): same = lax.ppermute(own, ('section', 'dev'), straight)  6.35 us
    dot_general x1, matrix products, body(): pre_act = jnp.dot(samples, whole, preferred_element_type=jnp.float32)  5.85 us
  transfers between devices with their start and end apart: 6, of which 4 were waited for; matrix products, arithmetic and copies ran while one was open for 4% of the time, Pallas kernels for 21%

profile of v2, /device:TPU:1, one launch (start us, length us, event | category | flops | bytes accessed | tf_op | source)
XLA Modules:
  0.0 173.4 jit_solution(13603793754517187699)
XLA Ops:
  6.5 1.2 reshape.52
  8.4 13.5 %all_to_all.25 = bf16[4,64,1024]{2,1,0:T(8,128)(2,1)} all-to-all(bf16[4,64,1024]{2,1,0:T(8,128)(2,1)S(1)} %copy.21), channel_id=1, replica_groups={{0,1,2,3},{4,5,6,7},{8,9,10,11},{12,13,14,15},{16,17,18,19},{20,21,22,2..., dimensions={0} | all-to-all | bytes 1048576 | tf_op jit(solution)/shard_map/all_to_all | solution.py:229
  22.0 6.3 %collective-permute-start = (s32[16,8,64]{2,1,0:T(8,128)S(1)}, s32[16,8,64]{2,1,0:T(8,128)S(1)}, u32[]{:S(2)}, u32[]{:S(2)}) collective-permute-start(s32[16,8,64]{2,1,0:T(8,128)S(1)} %get-tuple-element.11), channel_id=1, source_target_pairs={{0,0},{1,64},{2,1},{3,65},{4,2},{5,66},{6,3},{7,67},{8,4},{9,68},{... | collective-permute-start | bytes 98312 | tf_op jit(solution)/shard_map/ppermute | solution.py:208
  28.3 1.0 collective-permute-start.1
  30.8 0.9 copy.17.x_ref
  31.7 3.0 %bag_lists.1 = (s32[128,512]{1,0:T(8,128)}, s32[128,64]{1,0:T(8,128)}) custom-call(s32[8,64,128]{2,1,0:T(8,128)} %copy.17.x_ref, s32[1,128]{1,0:T(1,128)} %reshape_reshape.3.live_ref), custom_call_target="tpu_custom_call" | custom-call | tf_op jit(solution)/shard_map/bag_lists/pallas_call | solution.py:91
  34.8 1.3 all_to_all.20
  36.0 24.0 %all_to_all.26 = s32[64,1,1024]{2,1,0:T(1,128)S(1)} all-to-all(s32[64,1,1024]{2,1,0:T(1,128)S(1)} %all_to_all.20), channel_id=1, replica_groups=mesh['section'=2,'dev'=64] {'dev'}, dimensions={0} | all-to-all | bytes 524288 | tf_op jit(solution)/shard_map/all_to_all | solution.py:217
  60.1 3.4 %copy-done = bf16[32768,128]{1,0:T(8,128)(2,1)S(1)} copy-done((bf16[32768,128]{1,0:T(8,128)(2,1)S(1)}, bf16[32768,128]{1,0:T(8,128)(2,1)}, u32[]{:S(2)}) %copy-start) | copy-done | bytes 8388632
  63.4 30.7 %bag_gather.1 = bf16[128,64,128]{2,1,0:T(8,128)(2,1)} custom-call(s32[65536]{0:T(1024)S(1)} %bitcast.33, bf16[32768,128]{1,0:T(8,128)(2,1)S(1)} %copy-done), custom_call_target="tpu_custom_call" | custom-call | tf_op jit(solution)/shard_map/bag_gather/pallas_call | solution.py:152
  94.2 5.1 %all-to-all-start.1 = ((bf16[64,128,128]{2,1,0:T(8,128)(2,1)}), bf16[64,128,128]{2,1,0:T(8,128)(2,1)S(1)}, u32[]{:S(2)}, u32[]{:S(2)}) async-start(bf16[64,128,128]{2,1,0:T(8,128)(2,1)} %bitcast.10), calls=%async_computation.1 | async-start | bytes 4194304 | tf_op jit(solution)/shard_map/all_to_all | solution.py:219
  100.1 26.3 %all-to-all-done.1 = bf16[64,128,128]{2,1,0:T(8,128)(2,1)S(1)} async-done(((bf16[64,128,128]{2,1,0:T(8,128)(2,1)}), bf16[64,128,128]{2,1,0:T(8,128)(2,1)S(1)}, u32[]{:S(2)}, u32[]{:S(2)}) %all-to-all-start.1) | async-done | bytes 2097184 | tf_op jit(solution)/shard_map/all_to_all | solution.py:219
  126.4 1.4 copy-done.1
  127.8 2.8 %bag_unsort.1 = bf16[128,2048]{1,0:T(8,128)(2,1)} custom-call(bf16[64,2,64,128]{3,2,1,0:T(8,128)(2,1)} %bitcast.34, s32[32,256]{1,0:T(8,128)} %reshape.50.bag_ref), custom_call_target="tpu_custom_call" | custom-call | tf_op jit(solution)/shard_map/bag_unsort/pallas_call | solution.py:183
  130.6 0.8 collective-permute-start.2
  131.4 9.4 %collective-permute-done.2 = bf16[128,2048]{1,0:T(8,128)(2,1)S(1)} collective-permute-done((bf16[128,2048]{1,0:T(8,128)(2,1)}, bf16[128,2048]{1,0:T(8,128)(2,1)S(1)}, u32[]{:S(2)}, u32[]{:S(2)}) %collective-permute-start.2) | collective-permute-done | bytes 524320 | tf_op jit(solution)/shard_map/ppermute | solution.py:235
  140.8 1.1 pad_maximum_fusion
  142.2 9.5 %all_to_all.27 = bf16[2,2,128,2048]{3,2,1,0:T(8,128)(2,1)S(1)} all-to-all(bf16[2,2,128,2048]{3,2,1,0:T(8,128)(2,1)S(1)} %broadcast_in_dim.8), channel_id=1, replica_groups=mesh['section'=2,'dev'=64] {'section'}, dimensions={0} | all-to-all | bytes 4194304 | tf_op jit(solution)/shard_map/all_to_all | solution.py:191
  151.7 2.2 %copy.20 = bf16[2,128,2,2048]{3,2,1,0:T(2,128)(2,1)S(1)} copy(bf16[2,128,2,2048]{3,1,0,2:T(8,128)(2,1)S(1)} %bitcast.35) | data formatting | bytes 4194304 | tf_op jit(solution)/shard_map/transpose | solution.py:237
  153.8 0.9 copy.22
  154.7 5.9 %fusion.2 = f32[256]{0:T(256)S(1)} fusion(bf16[256,4096]{1,0:T(8,128)(2,1)S(1)} %bitcast.38, bf16[4096,1024]{1,0:T(8,128)(2,1)} %all-gather.4.cloned.1.call-done, f32[1024]{0:T(1024)S(1)} %get-tuple-element.13, f32[1024]{0:T(1024)S(1)} %get-tuple-element.14), kind=kOutput, calls=%fused_computation.3 | convolution fusion | flops 2148531968 | bytes 10494976 | tf_op jit(solution)/shard_map/dot_general | solution.py:238
  160.6 0.9 collective-permute-start.3
  161.5 1.6 collective-permute-done.3
  163.1 2.9 %all-gather.1 = f32[2,1,128]{2,1,0:T(1,128)S(1)} all-gather(f32[1,1,128]{2,1,0:T(1,128)S(1)} %add_bitcast_fusion.1), channel_id=2, replica_groups=mesh['section'=2,'dev'=64] {'section'}, dimensions={0}, use_global_device_ids=true | all-gather | bytes 1536 | tf_op jit(solution)/shard_map/all_gather | solution.py:242
  (34 shorter events, 3.7 us)
Async XLA Ops:
  6.5 15.4 %copy-start.2 = (s32[64,32,8]{0,2,1:T(8,128)S(1)}, s32[64,32,8]{0,2,1:T(8,128)}, u32[]{:S(2)}) copy-start(s32[64,32,8]{0,2,1:T(8,128)} %param.6) | copy-start | bytes 196612
  6.5 22.8 %copy-start.6 = (s32[32]{0:T(128)S(1)}, s32[32]{0:T(128)}, u32[]{:S(2)}) copy-start(s32[32]{0:T(128)} %param.7) | copy-start | bytes 388
  6.5 148.2 %all-gather.4.cloned.1.call-start = ((), (), s32[]{:S(2)}) async-start(), calls=%async_computation.4 | async-start | bytes 8912896 | tf_op jit(solution)/shard_map/all_gather | solution.py:230
  22.0 8.1 %collective-permute-start = (s32[16,8,64]{2,1,0:T(8,128)S(1)}, s32[16,8,64]{2,1,0:T(8,128)S(1)}, u32[]{:S(2)}, u32[]{:S(2)}) collective-permute-start(s32[16,8,64]{2,1,0:T(8,128)S(1)} %get-tuple-element.11), channel_id=1, source_target_pairs={{0,0},{1,64},{2,1},{3,65},{4,2},{5,66},{6,3},{7,67},{8,4},{9,68},{... | collective-permute-start | bytes 98312 | tf_op jit(solution)/shard_map/ppermute | solution.py:208
  28.3 2.3 %collective-permute-start.1 = (s32[16,8,64]{2,1,0:T(8,128)S(1)}, s32[16,8,64]{2,1,0:T(8,128)S(1)}, u32[]{:S(2)}, u32[]{:S(2)}) collective-permute-start(s32[16,8,64]{2,1,0:T(8,128)S(1)} %get-tuple-element.12), channel_id=1, source_target_pairs={{0,64},{1,0},{2,65},{3,1},{4,66},{5,2},{6,67},{7,3},{8,68},{9,4},{... | collective-permute-start | bytes 98312 | tf_op jit(solution)/shard_map/ppermute | solution.py:209
  60.1 3.4 %copy-start = (bf16[32768,128]{1,0:T(8,128)(2,1)S(1)}, bf16[32768,128]{1,0:T(8,128)(2,1)}, u32[]{:S(2)}) copy-start(bf16[32768,128]{1,0:T(8,128)(2,1)} %table_ref.1) | copy-start | bytes 25165828
  94.2 5.2 %copy-start.3 = (s32[128,64]{1,0:T(8,128)S(1)}, s32[128,64]{1,0:T(8,128)}, u32[]{:S(2)}) copy-start(s32[128,64]{1,0:T(8,128)} %get-tuple-element.8) | copy-start | bytes 98308
  94.2 32.2 %all-to-all-start.1 = ((bf16[64,128,128]{2,1,0:T(8,128)(2,1)}), bf16[64,128,128]{2,1,0:T(8,128)(2,1)S(1)}, u32[]{:S(2)}, u32[]{:S(2)}) async-start(bf16[64,128,128]{2,1,0:T(8,128)(2,1)} %bitcast.10), calls=%async_computation.1 | async-start | bytes 4194304 | tf_op jit(solution)/shard_map/all_to_all | solution.py:219
  99.3 32.1 %copy-start.4 = (bf16[2048]{0:T(1024)(128)(2,1)S(1)}, bf16[2048]{0:T(1024)(128)(2,1)}, u32[]{:S(2)}) copy-start(bf16[2048]{0:T(1024)(128)(2,1)} %param.11) | copy-start | bytes 12292
  99.3 32.1 %copy-start.5 = (bf16[2048]{0:T(1024)(128)(2,1)S(1)}, bf16[2048]{0:T(1024)(128)(2,1)}, u32[]{:S(2)}) copy-start(bf16[2048]{0:T(1024)(128)(2,1)} %param.10) | copy-start | bytes 12292
  126.4 1.4 copy-start.1
  130.6 10.2 %collective-permute-start.2 = (bf16[128,2048]{1,0:T(8,128)(2,1)}, bf16[128,2048]{1,0:T(8,128)(2,1)S(1)}, u32[]{:S(2)}, u32[]{:S(2)}) collective-permute-start(bf16[128,2048]{1,0:T(8,128)(2,1)} %bag_unsort.1), channel_id=1, source_target_pairs={{0,1},{1,0},{2,3},{3,2},{4,5},{5,4},{6,7},{7,6},{8,9},{9,8},{10,11... | collective-permute-start | bytes 1572872 | tf_op jit(solution)/shard_map/ppermute | solution.py:235
  160.6 2.5 %collective-permute-start.3 = (f32[128]{0:T(128)S(1)}, f32[128]{0:T(128)S(1)}, u32[]{:S(2)}, u32[]{:S(2)}) collective-permute-start(f32[128]{0:T(128)S(1)} %slice.9), channel_id=1, source_target_pairs={{0,1},{1,0},{2,3},{3,2},{4,5},{5,4},{6,7},{7,6},{8,9},{9,8},{10,11... | collective-permute-start | bytes 1544 | tf_op jit(solution)/shard_map/ppermute | solution.py:241
Sparse Core Ops, SparseCore 0:
  22.0 72.3 all-gather.3

commit v3 on v1

v3 whole, which is shorter than its diff:
```python
import functools

import jax
import jax.numpy as jnp
from jax import lax
from jax.experimental import pallas as pl
from jax.experimental.pallas import tpu as pltpu
from jax.sharding import PartitionSpec as P

E = 128
ROWS_DEV = 32768
POOL = 8
CHUNK = 64
SLOTS = POOL * CHUNK
DEAD = ROWS_DEV | (8 << 16)
PIECES = 8
TBLK = 2048
TSLOTS = 4
HID_SPLIT = 2
SORT8 = (
    (0, 2), (1, 3), (4, 6), (5, 7), (0, 4), (1, 5), (2, 6), (3, 7), (0, 1), (2, 3),
    (4, 5), (6, 7), (2, 4), (3, 5), (1, 4), (3, 6), (1, 2), (3, 4), (5, 6),
)


def prep_body(x_ref, pool_ref, list_ref, bag_ref):
    shape = (CHUNK, 128)
    tables = x_ref.shape[0]
    lane = lax.broadcasted_iota(jnp.int32, shape, 1)
    bag = lax.broadcasted_iota(jnp.int32, shape, 0)
    table = lax.broadcasted_iota(jnp.int32, (8, 128), 1) & (tables - 1)
    live = jnp.zeros((8, 128), jnp.int32)
    for t in range(tables):
        live = jnp.where(table == t, pool_ref[t], live)
    live = jnp.concatenate([live] * (CHUNK // 8), axis=0)
    first = (lane // tables) * ROWS_DEV
    v = []
    for p in range(POOL):
        row = jnp.concatenate([x_ref[:, p, :]] * 4, axis=0).T - first
        ok = (row >= 0) & (row < ROWS_DEV) & (live > p)
        v.append(jnp.where(ok, row, ROWS_DEV))
    for a, b in SORT8:
        v[a], v[b] = jnp.minimum(v[a], v[b]), jnp.maximum(v[a], v[b])
    kept = sum((w < ROWS_DEV).astype(jnp.int32) for w in v)
    cols = [(POOL - kept) * CHUNK + bag]
    cols += [v[2 * k] | (v[2 * k + 1] << 16) for k in range(POOL // 2)]
    size = 2
    while size <= CHUNK:
        step = size // 2
        while step:
            upper = (bag & step) != 0
            small = ((bag & size) == 0) != upper
            other = [
                jnp.where(upper, pltpu.roll(c, step, 0), pltpu.roll(c, CHUNK - step, 0)) for c in cols
            ]
            take = jnp.where(small, other[0] - cols[0], cols[0] - other[0]) < 0
            cols = [jnp.where(take, o, c) for o, c in zip(other, cols)]
            step //= 2
        size *= 2
    key = cols[0]
    order = (key & (CHUNK - 1)).T
    for j in range(4):
        bag_ref[:, j * CHUNK : (j + 1) * CHUNK] = order[j * tables : (j + 1) * tables, :]
    kept = POOL - (key >> 6)
    v = []
    for w in cols[1:]:
        v += [w & 0xFFFF, lax.shift_right_logical(w, 16)]
    tile = (8, 128)
    groups = []
    total = jnp.zeros((1, 128), jnp.int32)
    for g in range(CHUNK // 8):
        n = kept[8 * g : 8 * g + 1]
        shift = jnp.broadcast_to((8 * g - total) << 20, tile)
        n_all = jnp.broadcast_to(n, tile)
        for p in range(POOL):
            word = v[p][8 * g : 8 * g + 8] | (g << 16) | shift
            groups.append(jnp.where(n_all > p, word, DEAD))
        total = total + n
    for k in range(6):
        gap = 1 << k
        moves = [((w >> (20 + k)) & 1) != 0 for w in groups]
        new = []
        for i in range(64):
            stay = jnp.where(moves[i], DEAD, groups[i])
            if i + gap < 64:
                stay = jnp.where(moves[i + gap], groups[i + gap], stay)
            new.append(stay)
        groups = new
    head = lax.broadcasted_iota(jnp.int32, tile, 0) == 0
    mask = jnp.where(head, 0xFFFFF, 0xFFFF)
    groups = [w & mask for w in groups]
    groups[0] = groups[0] | jnp.where(head, jnp.broadcast_to(total << 20, tile), 0)
    for i in range(4):
        block = jnp.concatenate(groups[16 * i : 16 * i + 16], axis=0)
        block = block.T
        for j in range(4):
            list_ref[pl.ds(4 * j + i, tables, stride=16), :] = block[j * tables : (j + 1) * tables, :]


def prep(ids, pool_len):
    tables = ids.shape[0]
    return pl.pallas_call(
        prep_body,
        out_shape=(
            pltpu.VMEM((128 * 4, 128), jnp.int32),
            pltpu.VMEM((tables, 4 * CHUNK), jnp.int32),
        ),
        out_specs=(pl.BlockSpec(memory_space=pltpu.VMEM), pl.BlockSpec(memory_space=pltpu.VMEM)),
        in_specs=[pl.BlockSpec(memory_space=pltpu.VMEM), pl.BlockSpec(memory_space=pltpu.SMEM)],
        name="bag_lists",
    )(ids, pool_len)


def gather_body(lists_ref, table_ref, out_ref, tab, tbuf, smem, acc, obuf, tsem, lsem, osem, *, unroll):
    chunks = out_ref.shape[0]
    per = chunks // PIECES
    piece = chunks * SLOTS // PIECES

    def list_copy(i):
        part = pl.ds(i * piece, piece)
        return pltpu.make_async_copy(lists_ref.at[part], smem.at[part], lsem.at[i])

    def table_copy(b):
        slot = b % TSLOTS
        return pltpu.make_async_copy(
            table_ref.at[pl.ds(b * TBLK, TBLK)], tbuf.at[slot], tsem.at[slot]
        )

    def out_copy(i):
        return pltpu.make_async_copy(obuf.at[i % 2], out_ref.at[pl.ds(i * per, per)], osem.at[i % 2])

    blocks = ROWS_DEV // TBLK
    for b in range(TSLOTS):
        table_copy(b).start()
    for i in range(PIECES):
        list_copy(i).start()
    tab[pl.ds(ROWS_DEV, 8), :] = jnp.zeros((8, E), jnp.float32)
    for b in range(blocks):
        table_copy(b).wait()
        tab[pl.ds(b * TBLK, TBLK), :] = tbuf[b % TSLOTS].astype(jnp.float32)
        if b + TSLOTS < blocks:
            table_copy(b + TSLOTS).start()

    def level(base):
        head = smem[base]
        rows = [head & 0xFFFF] + [smem[base + i] for i in range(1, 8)]
        return (head >> 16) & 15, jnp.concatenate([tab[pl.ds(r, 1), :] for r in rows], axis=0)

    def chunk(c, piece):
        base = (piece * per + c) * SLOTS
        acc[...] = jnp.zeros(acc.shape, jnp.float32)
        levels = smem[base] >> 20

        def step(k, carry):
            at = base + k * (8 * unroll)
            for g, rows in [level(at + 8 * u) for u in range(unroll)]:
                acc[pl.ds(pl.multiple_of(g * 8, 8), 8), :] += rows
            return carry

        lax.fori_loop(0, (levels + unroll - 1) // unroll, step, 0)
        obuf[piece % 2, c] = acc[pl.ds(0, CHUNK), :].astype(jnp.bfloat16)

    for i in range(PIECES):
        list_copy(i).wait()
        if i >= 2:
            out_copy(i - 2).wait()
        lax.fori_loop(0, per, lambda c, carry: (chunk(c, i), carry)[1], 0)
        out_copy(i).start()
    out_copy(PIECES - 2).wait()
    out_copy(PIECES - 1).wait()


def gather(lists, table, chunks, unroll=4):
    return pl.pallas_call(
        functools.partial(gather_body, unroll=unroll),
        out_shape=pltpu.HBM((chunks, CHUNK, E), jnp.bfloat16),
        in_specs=[pl.BlockSpec(memory_space=pl.ANY), pl.BlockSpec(memory_space=pltpu.HBM)],
        out_specs=pl.BlockSpec(memory_space=pltpu.HBM),
        scratch_shapes=[
            pltpu.VMEM((ROWS_DEV + 8, E), jnp.float32),
            pltpu.VMEM((TSLOTS, TBLK, E), jnp.bfloat16),
            pltpu.SMEM((chunks * SLOTS,), jnp.int32),
            pltpu.VMEM((CHUNK + 8, E), jnp.float32),
            pltpu.VMEM((2, chunks // PIECES, CHUNK, E), jnp.bfloat16),
            pltpu.SemaphoreType.DMA((TSLOTS,)),
            pltpu.SemaphoreType.DMA((PIECES,)),
            pltpu.SemaphoreType.DMA((2,)),
        ],
        compiler_params=pltpu.CompilerParams(vmem_limit_bytes=32 * 2**20),
        name="bag_gather",
    )(lists, pltpu.with_memory_space_constraint(table, pltpu.HBM))


def unsort_body(part_ref, low_ref, high_ref, out_ref):
    tables = out_ref.shape[1] // E
    bag = lax.broadcasted_iota(jnp.int32, (CHUNK, 4 * CHUNK), 0)
    for t in range(tables):
        for h in range(2):
            where = (low_ref, high_ref)[h][t : t + 1, :]
            pick = (bag == where).astype(jnp.float32).astype(jnp.bfloat16)
            rows = part_ref[4 * t : 4 * t + 4, h].reshape(4 * CHUNK, E)
            total = jnp.dot(pick, rows, preferred_element_type=jnp.float32)
            out_ref[h * CHUNK : (h + 1) * CHUNK, t * E : (t + 1) * E] = total.astype(jnp.bfloat16)


def unsort(parts, low, high):
    return pl.pallas_call(
        unsort_body,
        out_shape=pltpu.VMEM((2 * CHUNK, parts.shape[0] // 4 * E), jnp.bfloat16),
        in_specs=[pl.BlockSpec(memory_space=pltpu.VMEM)] * 3,
        out_specs=pl.BlockSpec(memory_space=pltpu.VMEM),
        name="bag_unsort",
    )(pltpu.with_memory_space_constraint(parts, pltpu.VMEM), low, high)


def swap(x, axis):
    return lax.all_to_all(jnp.broadcast_to(x[None], (2, *x.shape)), axis, 0, 0, tiled=True)


def body(indices, pool_len, tables, w_first, b_first, w_out):
    n_dev = lax.axis_size("dev")
    n_sec = lax.axis_size("section")
    n_tables = indices.shape[1]
    half = n_tables // n_sec
    section = lax.axis_index("section")
    dev = lax.axis_index("dev")
    lists, order = prep(jnp.transpose(indices, (1, 2, 0)), pool_len)
    ring = 4
    rows, cols = w_first.shape
    part = cols // HID_SPLIT
    planes = n_dev // ring
    levels = [[ring * p + y for p in range(planes)] for y in range(ring)]
    y = dev % ring
    q = dev % HID_SPLIT
    keep = lax.dynamic_slice(w_first, (0, q * part), (rows, part))
    give = lax.dynamic_slice(w_first, (0, (1 - q) * part), (rows, part))

    def along(x, k):
        return lax.ppermute(x, "dev", [(d, d // ring * ring + (d + k) % ring) for d in range(n_dev)])

    pieces = [keep, along(give, 1), along(keep, 2), along(give, 3)]
    pieces, lists = lax.optimization_barrier((pieces, lists))
    pieces = jnp.stack(pieces)
    pieces = [lax.dynamic_index_in_dim(pieces, (y - k) % ring, 0, False) for k in range(ring)]
    whole = lax.all_gather(jnp.concatenate(pieces), "dev", axis_index_groups=levels, tiled=True)
    both_axes = ("section", "dev")
    blocks = range(n_sec * n_dev)
    arrived = lax.all_to_all(lists.reshape(n_sec * n_dev, 4, 128), both_axes, 0, 0, tiled=True)
    order = order.reshape(n_sec, half, 4 * CHUNK)
    odd = dev % 2
    straight = [(b, (b % 2) * n_dev + b // 2) for b in blocks]
    crossed = [(b, (1 - b % 2) * n_dev + b // 2) for b in blocks]
    same = lax.ppermute(lax.dynamic_index_in_dim(order, odd, 0, False), both_axes, straight)
    cross = lax.ppermute(lax.dynamic_index_in_dim(order, 1 - odd, 0, False), both_axes, crossed)
    low = jnp.where(section == 0, same, cross)
    high = jnp.where(section == 0, cross, same)
    parts = gather(arrived.reshape(-1), tables, n_sec * n_dev)
    parts = lax.all_to_all(parts.reshape(n_dev, 2 * CHUNK, E), "dev", 0, 0, tiled=True)
    features = unsort(parts.reshape(n_dev, 2, CHUNK, E), low, high)
    bias = lax.dynamic_slice(b_first, (q * part,), (part,)).astype(jnp.float32)
    scale = lax.dynamic_slice(w_out, (q * part,), (part,)).astype(jnp.float32)
    far = lax.ppermute(features, "dev", [(d, d ^ 1) for d in range(n_dev)])
    k_half = half * E

    def logits_of(mine):
        both = swap(mine, "section")
        pre_act = jnp.dot(both[0], whole[:k_half], preferred_element_type=jnp.float32)
        pre_act += jnp.dot(both[1], whole[k_half:], preferred_element_type=jnp.float32)
        hidden = jnp.maximum(pre_act + bias[None, :], 0.0)
        return jnp.sum(hidden * scale[None, :], axis=1)

    near_part = logits_of(features)
    far, near_part = lax.optimization_barrier((far, near_part))
    far_part = logits_of(far)
    by_chip = jnp.stack([jnp.where(q == 0, near_part, far_part), jnp.where(q == 0, far_part, near_part)])
    quads = [[s * n_dev + 2 * p + i for s in range(n_sec) for i in range(2)] for p in range(n_dev // 2)]
    quarters = lax.all_gather(by_chip, both_axes, axis_index_groups=quads)
    return lax.dynamic_index_in_dim(quarters.sum(0), q, 0, False)


def solution(mesh):
    placed = (
        P(("section", "dev"), None, None),
        P(),
        P(("section", "dev"), None),
        P("dev", "section"),
        P("section"),
        P("section"),
    )
    return jax.shard_map(body, mesh=mesh, in_specs=placed, out_specs=P("dev"), check_vma=False)
```

time: 166 us -> 154 us (0.928)
  waiting for transfers between devices: 48.8 us -> 33.1 us
  local copies, waits for them, and re-layouts: 12.3 us -> 1.82 us
  Pallas kernels: 20.1 us -> 27.4 us
  blocking collectives: 34 us -> 39.3 us
    all_to_all x1, waiting for transfers between devices: 48.1 us -> 5.2 us  [body(): lax.all_to_all(parts.reshape(n_dev, 2 * CHUNK, E), 'dev', 0, 0, tiled=True)]
    ppermute x2 -> x6, waiting for transfers between devices: 0.01 us -> 27.9 us  [the longest x1 25.4 us: body(): lax.ppermute(lax.dynamic_index_in_dim(order, 1 - odd, 0, False), both_axe...]
    pallas_call x3, Pallas kernels: 20.1 us -> 27.4 us  [the longest x1 23.7 us: gather(): pl.pallas_call(functools.partial(gather_body, unroll=unroll), out_shape=p...]
    ppermute x2 -> x6, starting transfers between devices: 7.02 us -> 13.8 us  [the longest x3 5.87 us: along(): lax.ppermute(x, 'dev', [(d, d // ring * ring + (d + k) % ring) for d in r...]
    all_to_all x1, starting transfers between devices: 21.2 us -> 15 us  [body(): lax.all_to_all(parts.reshape(n_dev, 2 * CHUNK, E), 'dev', 0, 0, tiled=True)]
    all_gather x1, blocking collectives: 1.84 us -> 6.8 us  [body(): quarters = lax.all_gather(by_chip, both_axes, axis_index_groups=quads)]
    unnamed x8, local copies, waits for them, and re-layouts: 4.84 us -> 0.02 us
    all_to_all x1 -> x2, blocking collectives: 6.63 us -> 11.1 us  [swap(): lax.all_to_all(jnp.broadcast_to(x[None], (2, *x.shape)), axis, 0, 0, tile...]
  transfers between devices with their start and end apart: 4 -> 8, of which waited for: 1 -> 4; matrix products, arithmetic and copies ran while one was open for 4% -> 5% of each run, Pallas kernels for 12% -> 18%
where the time goes in v3:
time: 154 us; the launch traced here: 153 us
  blocking collectives  39.3 us (26%)
  waiting for transfers between devices  33.1 us (21%)
  starting transfers between devices  28.8 us (19%)
  Pallas kernels  27.4 us (18%)
  between operations  13.6 us (9%)
  matrix products  7.86 us (5%)
  local copies, waits for them, and re-layouts  1.82 us (1%)
  other arithmetic  1.55 us (1%)
    ppermute x1, waiting for transfers between devices, body(): lax.ppermute(lax.dynamic_index_in_dim(order, 1 - odd, 0, False), both_axe...  25.4 us
    pallas_call x1, Pallas kernels, gather(): pl.pallas_call(functools.partial(gather_body, unroll=unroll), out_shape=p...  23.7 us
    all_to_all x1, blocking collectives, body(): lax.all_to_all(lists.reshape(n_sec * n_dev, 4, 128), both_axes, 0, 0, til...  21.5 us
    all_to_all x1, starting transfers between devices, body(): lax.all_to_all(parts.reshape(n_dev, 2 * CHUNK, E), 'dev', 0, 0, tiled=True)  15 us
    all_to_all x2, blocking collectives, swap(): lax.all_to_all(jnp.broadcast_to(x[None], (2, *x.shape)), axis, 0, 0, tile...  11.1 us
    all_gather x1, blocking collectives, body(): quarters = lax.all_gather(by_chip, both_axes, axis_index_groups=quads)  6.8 us
    ppermute x3, starting transfers between devices, along(): lax.ppermute(x, 'dev', [(d, d // ring * ring + (d + k) % ring) for d in r...  5.87 us
    all_to_all x1, waiting for transfers between devices, body(): lax.all_to_all(parts.reshape(n_dev, 2 * CHUNK, E), 'dev', 0, 0, tiled=True)  5.2 us
  transfers between devices with their start and end apart: 8, of which 4 were waited for; matrix products, arithmetic and copies ran while one was open for 5% of the time, Pallas kernels for 18%

profile of v3, /device:TPU:1, one launch (start us, length us, event | category | flops | bytes accessed | tf_op | source)
XLA Modules:
  0.0 153.5 jit_solution(15730474147881033307)
XLA Ops:
  6.5 1.0 constant_dynamic-slice_fusion.1
  7.5 2.2 %collective-permute-start = (bf16[64,1024]{1,0:T(8,128)(2,1)S(1)}, bf16[64,1024]{1,0:T(8,128)(2,1)S(1)}, u32[]{:S(2)}, u32[]{:S(2)}) collective-permute-start(bf16[64,1024]{1,0:T(8,128)(2,1)S(1)} %get-tuple-element.27), channel_id=1, source_target_pairs={{0,1},{1,2},{2,3},{3,0},{4,5},{5,6},{6,7},{7,4},{8,9},{9,10},{10,1... | collective-permute-start | bytes 393224 | tf_op jit(solution)/shard_map/ppermute | solution.py:239
  9.7 2.6 %collective-permute-start.1 = (bf16[64,1024]{1,0:T(8,128)(2,1)S(1)}, bf16[64,1024]{1,0:T(8,128)(2,1)S(1)}, u32[]{:S(2)}, u32[]{:S(2)}) collective-permute-start(bf16[64,1024]{1,0:T(8,128)(2,1)S(1)} %get-tuple-element.17), channel_id=1, source_target_pairs={{0,2},{1,3},{2,0},{3,1},{4,6},{5,7},{6,4},{7,5},{8,10},{9,11},{10,... | collective-permute-start | bytes 393224 | tf_op jit(solution)/shard_map/ppermute | solution.py:239
  12.3 1.1 collective-permute-start.2
  13.4 2.5 %bag_lists.1 = (s32[512,128]{1,0:T(8,128)S(1)}, s32[32,256]{1,0:T(8,128)S(1)}) custom-call(s32[32,8,64]{2,1,0:T(8,128)} %bitcast.48, s32[32]{0:T(128)} %pool_ref.1), custom_call_target="tpu_custom_call" | custom-call | tf_op jit(solution)/shard_map/bag_lists/pallas_call | solution.py:102
  15.9 2.1 %collective-permute-done.1 = bf16[64,1024]{1,0:T(8,128)(2,1)S(1)} collective-permute-done((bf16[64,1024]{1,0:T(8,128)(2,1)S(1)}, bf16[64,1024]{1,0:T(8,128)(2,1)S(1)}, u32[]{:S(2)}, u32[]{:S(2)}) %collective-permute-start.1) | collective-permute-done | bytes 131104 | tf_op jit(solution)/shard_map/ppermute | solution.py:239
  18.2 0.8 pad_maximum_fusion.1
  19.1 21.5 %all_to_all.20 = s32[128,4,128]{2,1,0:T(4,128)S(1)} all-to-all(s32[128,4,128]{2,1,0:T(4,128)S(1)} %bitcast.44), channel_id=1, replica_groups=mesh['section'=2,'dev'=64] {'section','dev'}, dimensions={0} | all-to-all | bytes 524288 | tf_op jit(solution)/shard_map/all_to_all | solution.py:248
  40.6 23.7 %bag_gather.1 = bf16[128,64,128]{2,1,0:T(8,128)(2,1)} custom-call(s32[65536]{0:T(1024)S(1)} %bitcast.43, bf16[32768,128]{1,0:T(8,128)(2,1)} %table_ref.1), custom_call_target="tpu_custom_call" | custom-call | tf_op jit(solution)/shard_map/bag_gather/pallas_call | solution.py:174
  64.3 15.0 %all-to-all-start.1 = ((bf16[64,128,128]{2,1,0:T(8,128)(2,1)}), bf16[64,128,128]{2,1,0:T(8,128)(2,1)S(1)}, u32[]{:S(2)}, u32[]{:S(2)}) async-start(bf16[64,128,128]{2,1,0:T(8,128)(2,1)} %bitcast.46), calls=%async_computation.1 | async-start | bytes 4194304 | tf_op jit(solution)/shard_map/all_to_all | solution.py:258
  79.3 2.7 %collective-permute-start.4 = (s32[16,256]{1,0:T(8,128)S(1)}, s32[16,256]{1,0:T(8,128)S(1)}, u32[]{:S(2)}, u32[]{:S(2)}) collective-permute-start(s32[16,256]{1,0:T(8,128)S(1)} %get-tuple-element.31), channel_id=1, source_target_pairs={{0,64},{1,0},{2,65},{3,1},{4,66},{5,2},{6,67},{7,3},{8,68},{9,4},{... | collective-permute-start | bytes 49160 | tf_op jit(solution)/shard_map/ppermute | solution.py:254
  82.0 4.0 %collective-permute-start.3 = (s32[16,256]{1,0:T(8,128)S(1)}, s32[16,256]{1,0:T(8,128)S(1)}, u32[]{:S(2)}, u32[]{:S(2)}) collective-permute-start(s32[16,256]{1,0:T(8,128)S(1)} %get-tuple-element.32), channel_id=1, source_target_pairs={{0,0},{1,64},{2,1},{3,65},{4,2},{5,66},{6,3},{7,67},{8,4},{9,68},{... | collective-permute-start | bytes 49160 | tf_op jit(solution)/shard_map/ppermute | solution.py:253
  86.1 25.4 %collective-permute-done.4 = s32[16,256]{1,0:T(8,128)S(1)} collective-permute-done((s32[16,256]{1,0:T(8,128)S(1)}, s32[16,256]{1,0:T(8,128)S(1)}, u32[]{:S(2)}, u32[]{:S(2)}) %collective-permute-start.4) | collective-permute-done | bytes 16416 | tf_op jit(solution)/shard_map/ppermute | solution.py:254
  111.8 0.6 broadcast_select_fusion
  112.4 5.2 %all-to-all-done.1 = bf16[64,128,128]{2,1,0:T(8,128)(2,1)S(1)} async-done(((bf16[64,128,128]{2,1,0:T(8,128)(2,1)}), bf16[64,128,128]{2,1,0:T(8,128)(2,1)S(1)}, u32[]{:S(2)}, u32[]{:S(2)}) %all-to-all-start.1) | async-done | bytes 2097184 | tf_op jit(solution)/shard_map/all_to_all | solution.py:258
  117.6 1.2 bag_unsort.1
  118.8 1.2 collective-permute-start.5
  120.2 6.5 %all_to_all.21 = bf16[2,128,2048]{2,1,0:T(8,128)(2,1)S(1)} all-to-all(bf16[2,128,2048]{2,1,0:T(8,128)(2,1)S(1)} %broadcast_in_dim.4), channel_id=1, replica_groups=mesh['section'=2,'dev'=64] {'section'}, dimensions={0} | all-to-all | bytes 2097152 | tf_op jit(solution)/shard_map/all_to_all | solution.py:217
  126.7 3.0 %fusion.2 = f32[128,1024]{1,0:T(8,128)S(1)} fusion(bf16[4096,1024]{1,0:T(8,128)(2,1)} %all-gather.4.cloned.1.call-done, bf16[2,128,2048]{2,1,0:T(8,128)(2,1)S(1)} %all_to_all.21), kind=kOutput, calls=%fused_computation.2 | convolution fusion | flops 536870912 | bytes 5242880 | tf_op jit(solution)/shard_map/dot_general | solution.py:268
  129.7 3.2 %fusion.32 = f32[128]{0:T(128)S(1)} fusion(f32[128,1024]{1,0:T(8,128)S(1)} %fusion.2, bf16[4096,1024]{1,0:T(8,128)(2,1)} %all-gather.4.cloned.1.call-done, bf16[2,128,2048]{2,1,0:T(8,128)(2,1)S(1)} %all_to_all.21, f32[1024]{0:T(1024)S(1)} %get-tuple-element.35, f32[1024]{0:T(1024)S(1)} %get-tuple-element.36), kind=kOutput, calls=%fused_computation.16 | convolution fusion | flops 537526144 | bytes 5251584 | tf_op jit(solution)/shard_map/dot_general | solution.py:267
  133.1 4.6 %all_to_all.22 = bf16[2,128,2048]{2,1,0:T(8,128)(2,1)S(1)} all-to-all(bf16[2,128,2048]{2,1,0:T(8,128)(2,1)S(1)} %broadcast_in_dim.5), channel_id=1, replica_groups=mesh['section'=2,'dev'=64] {'section'}, dimensions={0} | all-to-all | bytes 2097152 | tf_op jit(solution)/shard_map/all_to_all | solution.py:217
  137.7 0.7 fusion
  138.4 0.9 fusion.35
  139.3 6.8 %all-gather.1 = f32[4,2,128]{2,1,0:T(2,128)S(1)} all-gather(f32[1,2,128]{2,1,0:T(2,128)S(1)} %maximum_bitcast_fusion), channel_id=2, replica_groups={{0,1,64,65},{2,3,66,67},{4,5,68,69},{6,7,70,71},{8,9,72,73},{10,11,74,7..., dimensions={0}, use_global_device_ids=true | all-gather | bytes 5120 | tf_op jit(solution)/shard_map/all_gather | solution.py:277
  (26 shorter events, 1.3 us)
Async XLA Ops:
  6.5 120.1 %all-gather.4.cloned.1.call-start = ((), (), s32[]{:S(2)}) async-start(), calls=%async_computation.4 | async-start | bytes 8912896 | tf_op jit(solution)/shard_map/all_gather | solution.py:245
  7.5 8.4 %collective-permute-start = (bf16[64,1024]{1,0:T(8,128)(2,1)S(1)}, bf16[64,1024]{1,0:T(8,128)(2,1)S(1)}, u32[]{:S(2)}, u32[]{:S(2)}) collective-permute-start(bf16[64,1024]{1,0:T(8,128)(2,1)S(1)} %get-tuple-element.27), channel_id=1, source_target_pairs={{0,1},{1,2},{2,3},{3,0},{4,5},{5,6},{6,7},{7,4},{8,9},{9,10},{10,1... | collective-permute-start | bytes 393224 | tf_op jit(solution)/shard_map/ppermute | solution.py:239
  9.7 8.3 %collective-permute-start.1 = (bf16[64,1024]{1,0:T(8,128)(2,1)S(1)}, bf16[64,1024]{1,0:T(8,128)(2,1)S(1)}, u32[]{:S(2)}, u32[]{:S(2)}) collective-permute-start(bf16[64,1024]{1,0:T(8,128)(2,1)S(1)} %get-tuple-element.17), channel_id=1, source_target_pairs={{0,2},{1,3},{2,0},{3,1},{4,6},{5,7},{6,4},{7,5},{8,10},{9,11},{10,... | collective-permute-start | bytes 393224 | tf_op jit(solution)/shard_map/ppermute | solution.py:239
  12.3 5.7 %collective-permute-start.2 = (bf16[64,1024]{1,0:T(8,128)(2,1)S(1)}, bf16[64,1024]{1,0:T(8,128)(2,1)S(1)}, u32[]{:S(2)}, u32[]{:S(2)}) collective-permute-start(bf16[64,1024]{1,0:T(8,128)(2,1)S(1)} %get-tuple-element.27), channel_id=1, source_target_pairs={{0,3},{1,0},{2,1},{3,2},{4,7},{5,4},{6,5},{7,6},{8,11},{9,8},{10,9... | collective-permute-start | bytes 393224 | tf_op jit(solution)/shard_map/ppermute | solution.py:239
  18.2 67.8 %copy-start = (bf16[2048]{0:T(1024)(128)(2,1)S(1)}, bf16[2048]{0:T(1024)(128)(2,1)}, u32[]{:S(2)}) copy-start(bf16[2048]{0:T(1024)(128)(2,1)} %param.11) | copy-start | bytes 12292
  18.2 67.8 %copy-start.1 = (bf16[2048]{0:T(1024)(128)(2,1)S(1)}, bf16[2048]{0:T(1024)(128)(2,1)}, u32[]{:S(2)}) copy-start(bf16[2048]{0:T(1024)(128)(2,1)} %param.10) | copy-start | bytes 12292
  64.3 53.4 %all-to-all-start.1 = ((bf16[64,128,128]{2,1,0:T(8,128)(2,1)}), bf16[64,128,128]{2,1,0:T(8,128)(2,1)S(1)}, u32[]{:S(2)}, u32[]{:S(2)}) async-start(bf16[64,128,128]{2,1,0:T(8,128)(2,1)} %bitcast.46), calls=%async_computation.1 | async-start | bytes 4194304 | tf_op jit(solution)/shard_map/all_to_all | solution.py:258
  79.3 32.2 %collective-permute-start.4 = (s32[16,256]{1,0:T(8,128)S(1)}, s32[16,256]{1,0:T(8,128)S(1)}, u32[]{:S(2)}, u32[]{:S(2)}) collective-permute-start(s32[16,256]{1,0:T(8,128)S(1)} %get-tuple-element.31), channel_id=1, source_target_pairs={{0,64},{1,0},{2,65},{3,1},{4,66},{5,2},{6,67},{7,3},{8,68},{9,4},{... | collective-permute-start | bytes 49160 | tf_op jit(solution)/shard_map/ppermute | solution.py:254
  82.0 29.8 %collective-permute-start.3 = (s32[16,256]{1,0:T(8,128)S(1)}, s32[16,256]{1,0:T(8,128)S(1)}, u32[]{:S(2)}, u32[]{:S(2)}) collective-permute-start(s32[16,256]{1,0:T(8,128)S(1)} %get-tuple-element.32), channel_id=1, source_target_pairs={{0,0},{1,64},{2,1},{3,65},{4,2},{5,66},{6,3},{7,67},{8,4},{9,68},{... | collective-permute-start | bytes 49160 | tf_op jit(solution)/shard_map/ppermute | solution.py:253
  118.8 14.1 %collective-permute-start.5 = (bf16[128,2048]{1,0:T(8,128)(2,1)S(1)}, bf16[128,2048]{1,0:T(8,128)(2,1)S(1)}, u32[]{:S(2)}, u32[]{:S(2)}) collective-permute-start(bf16[128,2048]{1,0:T(8,128)(2,1)S(1)} %bag_unsort.1), channel_id=1, source_target_pairs={{0,1},{1,0},{2,3},{3,2},{4,5},{5,4},{6,7},{7,6},{8,9},{9,8},{10,11... | collective-permute-start | bytes 1572872 | tf_op jit(solution)/shard_map/ppermute | solution.py:262
  126.7 11.0 %slice-start = ((s8[8388608]{0:T(1024)(128)(4,1)}), s8[4194304]{0:T(1024)(128)(4,1)S(1)}, s32[]{:S(2)}) async-start(s8[8388608]{0:T(1024)(128)(4,1)} %bitcast.52), calls=%async_computation.5 | async-start | bytes 8388608
  129.7 7.9 %slice-start.1 = ((s8[8388608]{0:T(1024)(128)(4,1)}), s8[4194304]{0:T(1024)(128)(4,1)S(1)}, s32[]{:S(2)}) async-start(s8[8388608]{0:T(1024)(128)(4,1)} %bitcast.52), calls=%async_computation.6 | async-start | bytes 8388608
Sparse Core Ops, SparseCore 0:
  19.2 92.8 all-gather.3

commit v4 on v3

--- a/solution.py
+++ b/solution.py
@@ -16,7 +16,7 @@
 PIECES = 8
 TBLK = 2048
 TSLOTS = 4
-HID_SPLIT = 2
+HID_SPLIT = 4
 SORT8 = (
     (0, 2), (1, 3), (4, 6), (5, 7), (0, 4), (1, 5), (2, 6), (3, 7), (0, 1), (2, 3),
     (4, 5), (6, 7), (2, 4), (3, 5), (1, 4), (3, 6), (1, 2), (3, 4), (5, 6),
@@ -225,24 +225,7 @@
     section = lax.axis_index("section")
     dev = lax.axis_index("dev")
     lists, order = prep(jnp.transpose(indices, (1, 2, 0)), pool_len)
-    ring = 4
-    rows, cols = w_first.shape
-    part = cols // HID_SPLIT
-    planes = n_dev // ring
-    levels = [[ring * p + y for p in range(planes)] for y in range(ring)]
-    y = dev % ring
-    q = dev % HID_SPLIT
-    keep = lax.dynamic_slice(w_first, (0, q * part), (rows, part))
-    give = lax.dynamic_slice(w_first, (0, (1 - q) * part), (rows, part))
-
-    def along(x, k):
-        return lax.ppermute(x, "dev", [(d, d // ring * ring + (d + k) % ring) for d in range(n_dev)])
-
-    pieces = [keep, along(give, 1), along(keep, 2), along(give, 3)]
-    pieces, lists = lax.optimization_barrier((pieces, lists))
-    pieces = jnp.stack(pieces)
-    pieces = [lax.dynamic_index_in_dim(pieces, (y - k) % ring, 0, False) for k in range(ring)]
-    whole = lax.all_gather(jnp.concatenate(pieces), "dev", axis_index_groups=levels, tiled=True)
+    lists, order, w_first = lax.optimization_barrier((lists, order, w_first))
     both_axes = ("section", "dev")
     blocks = range(n_sec * n_dev)
     arrived = lax.all_to_all(lists.reshape(n_sec * n_dev, 4, 128), both_axes, 0, 0, tiled=True)
@@ -254,12 +237,29 @@
     cross = lax.ppermute(lax.dynamic_index_in_dim(order, 1 - odd, 0, False), both_axes, crossed)
     low = jnp.where(section == 0, same, cross)
     high = jnp.where(section == 0, cross, same)
+    ring = HID_SPLIT
+    rows, cols = w_first.shape
+    part = cols // ring
+    planes = n_dev // ring
+    levels = [[ring * p + y for p in range(planes)] for y in range(ring)]
+    y = dev % ring
+
+    def along(x, k):
+        return lax.ppermute(x, "dev", [(d, d // ring * ring + (d + k) % ring) for d in range(n_dev)])
+
+    def slab(k):
+        return lax.dynamic_slice(w_first, (0, (y + k) % ring * part), (rows, part))
+
+    pieces = jnp.stack([slab(0)] + [along(slab(k), k) for k in range(1, ring)])
+    pieces = [lax.dynamic_index_in_dim(pieces, (y - k) % ring, 0, False) for k in range(ring)]
+    mine = jnp.concatenate(pieces)
+    arrived, low, high = lax.optimization_barrier((arrived, low, high))
+    whole = lax.all_gather(mine, "dev", axis_index_groups=levels, tiled=True)
+    bias = lax.dynamic_slice(b_first, (y * part,), (part,)).astype(jnp.float32)
+    scale = lax.dynamic_slice(w_out, (y * part,), (part,)).astype(jnp.float32)
     parts = gather(arrived.reshape(-1), tables, n_sec * n_dev)
     parts = lax.all_to_all(parts.reshape(n_dev, 2 * CHUNK, E), "dev", 0, 0, tiled=True)
     features = unsort(parts.reshape(n_dev, 2, CHUNK, E), low, high)
-    bias = lax.dynamic_slice(b_first, (q * part,), (part,)).astype(jnp.float32)
-    scale = lax.dynamic_slice(w_out, (q * part,), (part,)).astype(jnp.float32)
-    far = lax.ppermute(features, "dev", [(d, d ^ 1) for d in range(n_dev)])
     k_half = half * E
 
     def logits_of(mine):
@@ -269,13 +269,17 @@
         hidden = jnp.maximum(pre_act + bias[None, :], 0.0)
         return jnp.sum(hidden * scale[None, :], axis=1)
 
-    near_part = logits_of(features)
-    far, near_part = lax.optimization_barrier((far, near_part))
-    far_part = logits_of(far)
-    by_chip = jnp.stack([jnp.where(q == 0, near_part, far_part), jnp.where(q == 0, far_part, near_part)])
-    quads = [[s * n_dev + 2 * p + i for s in range(n_sec) for i in range(2)] for p in range(n_dev // 2)]
-    quarters = lax.all_gather(by_chip, both_axes, axis_index_groups=quads)
-    return lax.dynamic_index_in_dim(quarters.sum(0), q, 0, False)
+    after, before, far = along(features, 1), along(features, 3), along(features, 2)
+    part_0 = logits_of(features)
+    after, before, part_0 = lax.optimization_barrier((after, before, part_0))
+    part_13 = logits_of(jnp.concatenate([after, before]))
+    far, part_13 = lax.optimization_barrier((far, part_13))
+    part_2 = logits_of(far)
+    shifts = jnp.stack([part_0, part_13[: 2 * CHUNK], part_2, part_13[2 * CHUNK :]])
+    by_chip = jnp.stack([lax.dynamic_index_in_dim(shifts, (y - k) % ring, 0, False) for k in range(ring)])
+    rings = [[s * n_dev + ring * p + i for s in range(n_sec) for i in range(ring)] for p in range(planes)]
+    eighths = lax.all_gather(by_chip, both_axes, axis_index_groups=rings)
+    return lax.dynamic_index_in_dim(eighths.sum(0), y, 0, False)
 
 
 def solution(mesh):

time: 154 us -> 178 us (1.16)
  the two profiles are of different devices: /device:TPU:1 before, /device:TPU:7 now
where the time goes in v4:
time: 178 us; the launch traced here: 179 us
  starting transfers between devices  57.2 us (32%)
  waiting for transfers between devices  41.7 us (23%)
  blocking collectives  37.4 us (21%)
  Pallas kernels  18.2 us (10%)
  between operations  13.6 us (8%)
  matrix products  6.66 us (4%)
  other arithmetic  2.27 us (1%)
  local copies, waits for them, and re-layouts  2.02 us (1%)
    all_to_all x1, starting transfers between devices, body(): lax.all_to_all(parts.reshape(n_dev, 2 * CHUNK, E), 'dev', 0, 0, tiled=True)  31.1 us
    all_to_all x1, waiting for transfers between devices, body(): lax.all_to_all(parts.reshape(n_dev, 2 * CHUNK, E), 'dev', 0, 0, tiled=True)  24.8 us
    all_gather x1, blocking collectives, body(): eighths = lax.all_gather(by_chip, both_axes, axis_index_groups=rings)  20.2 us
    all_to_all x3, blocking collectives, swap(): lax.all_to_all(jnp.broadcast_to(x[None], (2, *x.shape)), axis, 0, 0, tile...  17.2 us
    ppermute x6, waiting for transfers between devices, along(): lax.ppermute(x, 'dev', [(d, d // ring * ring + (d + k) % ring) for d in r...  15.3 us
    pallas_call x1, Pallas kernels, gather(): pl.pallas_call(functools.partial(gather_body, unroll=unroll), out_shape=p...  13.8 us
    all_to_all x1, starting transfers between devices, body(): lax.all_to_all(lists.reshape(n_sec * n_dev, 4, 128), both_axes, 0, 0, til...  10.3 us
    ppermute x6, starting transfers between devices, along(): lax.ppermute(x, 'dev', [(d, d // ring * ring + (d + k) % ring) for d in r...  8.36 us
  transfers between devices with their start and end apart: 11, of which 7 were waited for; matrix products, arithmetic and copies ran while one was open for 4% of the time, Pallas kernels for 8%

profile of v4, /device:TPU:7, one launch (start us, length us, event | category | flops | bytes accessed | tf_op | source)
XLA Modules:
  0.0 179.0 jit_solution(17642157491426324713)
XLA Ops:
  6.5 3.2 %bag_lists.1 = (s32[512,128]{1,0:T(8,128)}, s32[32,256]{1,0:T(8,128)S(1)}) custom-call(s32[32,8,64]{2,1,0:T(8,128)} %bitcast.55, s32[32]{0:T(128)} %pool_ref.1), custom_call_target="tpu_custom_call" | custom-call | tf_op jit(solution)/shard_map/bag_lists/pallas_call | solution.py:102
  9.7 1.0 dynamic-slice_bitcast_fusion.4
  10.7 2.8 %collective-permute-start.6 = (bf16[64,512]{1,0:T(8,128)(2,1)S(1)}, bf16[64,512]{1,0:T(8,128)(2,1)S(1)}, u32[]{:S(2)}, u32[]{:S(2)}) collective-permute-start(bf16[64,512]{1,0:T(8,128)(2,1)S(1)} %get-tuple-element.36), channel_id=1, source_target_pairs={{0,3},{1,0},{2,1},{3,2},{4,7},{5,4},{6,5},{7,6},{8,11},{9,8},{10,9... | collective-permute-start | bytes 196616 | tf_op jit(solution)/shard_map/ppermute | solution.py:248
  14.8 3.4 %collective-permute-done.5 = bf16[64,512]{1,0:T(8,128)(2,1)S(1)} collective-permute-done((bf16[64,512]{1,0:T(8,128)(2,1)S(1)}, bf16[64,512]{1,0:T(8,128)(2,1)S(1)}, u32[]{:S(2)}, u32[]{:S(2)}) %collective-permute-start.5) | collective-permute-done | bytes 65568 | tf_op jit(solution)/shard_map/ppermute | solution.py:248
  19.6 10.3 %all-to-all-start = ((s32[128,4,128]{2,1,0:T(4,128)}), s32[128,4,128]{2,1,0:T(4,128)S(1)}, u32[]{:S(2)}, u32[]{:S(2)}) async-start(s32[128,4,128]{2,1,0:T(4,128)} %bitcast.1), calls=%async_computation | async-start | bytes 524288 | tf_op jit(solution)/shard_map/all_to_all | solution.py:231
  30.0 3.2 %collective-permute-start.1 = (s32[16,256]{1,0:T(8,128)S(1)}, s32[16,256]{1,0:T(8,128)S(1)}, u32[]{:S(2)}, u32[]{:S(2)}) collective-permute-start(s32[16,256]{1,0:T(8,128)S(1)} %get-tuple-element.41), channel_id=1, source_target_pairs={{0,64},{1,0},{2,65},{3,1},{4,66},{5,2},{6,67},{7,3},{8,68},{9,4},{... | collective-permute-start | bytes 49160 | tf_op jit(solution)/shard_map/ppermute | solution.py:237
  33.2 4.2 %collective-permute-start = (s32[16,256]{1,0:T(8,128)S(1)}, s32[16,256]{1,0:T(8,128)S(1)}, u32[]{:S(2)}, u32[]{:S(2)}) collective-permute-start(s32[16,256]{1,0:T(8,128)S(1)} %get-tuple-element.42), channel_id=1, source_target_pairs={{0,0},{1,64},{2,1},{3,65},{4,2},{5,66},{6,3},{7,67},{8,4},{9,68},{... | collective-permute-start | bytes 49160 | tf_op jit(solution)/shard_map/ppermute | solution.py:236
  37.4 1.5 collective-permute-done
  39.6 13.8 %bag_gather.1 = bf16[128,64,128]{2,1,0:T(8,128)(2,1)} custom-call(s32[65536]{0:T(1024)S(1)} %bitcast.52, bf16[32768,128]{1,0:T(8,128)(2,1)} %table_ref.1), custom_call_target="tpu_custom_call" | custom-call | tf_op jit(solution)/shard_map/bag_gather/pallas_call | solution.py:174
  53.4 31.1 %all-to-all-start.1 = ((bf16[64,128,128]{2,1,0:T(8,128)(2,1)}), bf16[64,128,128]{2,1,0:T(8,128)(2,1)S(1)}, u32[]{:S(2)}, u32[]{:S(2)}) async-start(bf16[64,128,128]{2,1,0:T(8,128)(2,1)} %bitcast.54), calls=%async_computation.1 | async-start | bytes 4194304 | tf_op jit(solution)/shard_map/all_to_all | solution.py:261
  84.5 0.8 dynamic-slice_convert_fusion
  85.3 24.8 %all-to-all-done.1 = bf16[64,128,128]{2,1,0:T(8,128)(2,1)S(1)} async-done(((bf16[64,128,128]{2,1,0:T(8,128)(2,1)}), bf16[64,128,128]{2,1,0:T(8,128)(2,1)S(1)}, u32[]{:S(2)}, u32[]{:S(2)}) %all-to-all-start.1) | async-done | bytes 2097184 | tf_op jit(solution)/shard_map/all_to_all | solution.py:261
  110.1 1.2 bag_unsort.1
  111.3 3.1 %collective-permute-start.7 = (bf16[128,2048]{1,0:T(8,128)(2,1)S(1)}, bf16[128,2048]{1,0:T(8,128)(2,1)S(1)}, u32[]{:S(2)}, u32[]{:S(2)}) collective-permute-start(bf16[128,2048]{1,0:T(8,128)(2,1)S(1)} %bag_unsort.1), channel_id=1, source_target_pairs={{0,2},{1,3},{2,0},{3,1},{4,6},{5,7},{6,4},{7,5},{8,10},{9,11},{10,... | collective-permute-start | bytes 1572872 | tf_op jit(solution)/shard_map/ppermute | solution.py:248
  114.3 0.9 collective-permute-start.3
  115.9 6.8 %all_to_all.25 = bf16[2,128,2048]{2,1,0:T(8,128)(2,1)S(1)} all-to-all(bf16[2,128,2048]{2,1,0:T(8,128)(2,1)S(1)} %broadcast_in_dim.6), channel_id=1, replica_groups=mesh['section'=2,'dev'=64] {'section'}, dimensions={0} | all-to-all | bytes 2097152 | tf_op jit(solution)/shard_map/all_to_all | solution.py:217
  122.7 2.0 %fusion.4 = f32[128,512]{1,0:T(8,128)S(1)} fusion(bf16[4096,512]{1,0:T(8,128)(2,1)} %all-gather.4.cloned.1.call-done, bf16[2,128,2048]{2,1,0:T(8,128)(2,1)S(1)} %all_to_all.25), kind=kOutput, calls=%fused_computation.4 | convolution fusion | flops 268435456 | bytes 2883584 | tf_op jit(solution)/shard_map/dot_general | solution.py:268
  124.8 2.1 %fusion.51 = f32[128]{0:T(128)S(1)} fusion(f32[128,512]{1,0:T(8,128)S(1)} %fusion.4, bf16[4096,512]{1,0:T(8,128)(2,1)} %all-gather.4.cloned.1.call-done, bf16[2,128,2048]{2,1,0:T(8,128)(2,1)S(1)} %all_to_all.25, f32[512]{0:T(512)S(1)} %get-tuple-element.49, f32[512]{0:T(512)S(1)} %get-tuple-element.50), kind=kOutput, calls=%fused_computation.25 | convolution fusion | flops 268763008 | bytes 2888192 | tf_op jit(solution)/shard_map/dot_general | solution.py:267
  126.9 8.6 %collective-permute-done.3 = bf16[128,2048]{1,0:T(8,128)(2,1)S(1)} collective-permute-done((bf16[128,2048]{1,0:T(8,128)(2,1)S(1)}, bf16[128,2048]{1,0:T(8,128)(2,1)S(1)}, u32[]{:S(2)}, u32[]{:S(2)}) %collective-permute-start.3) | collective-permute-done | bytes 524320 | tf_op jit(solution)/shard_map/ppermute | solution.py:248
  135.5 2.4 %collective-permute-done.2 = bf16[128,2048]{1,0:T(8,128)(2,1)S(1)} collective-permute-done((bf16[128,2048]{1,0:T(8,128)(2,1)S(1)}, bf16[128,2048]{1,0:T(8,128)(2,1)S(1)}, u32[]{:S(2)}, u32[]{:S(2)}) %collective-permute-start.2) | collective-permute-done | bytes 524320 | tf_op jit(solution)/shard_map/ppermute | solution.py:248
  138.3 5.8 %all_to_all.26 = bf16[2,256,2048]{2,1,0:T(8,128)(2,1)S(1)} all-to-all(bf16[2,256,2048]{2,1,0:T(8,128)(2,1)S(1)} %broadcast_in_dim.7), channel_id=1, replica_groups=mesh['section'=2,'dev'=64] {'section'}, dimensions={0} | all-to-all | bytes 4194304 | tf_op jit(solution)/shard_map/all_to_all | solution.py:217
  144.8 0.8 fusion.24
  145.7 4.6 %all_to_all.27 = bf16[2,128,2048]{2,1,0:T(8,128)(2,1)S(1)} all-to-all(bf16[2,128,2048]{2,1,0:T(8,128)(2,1)S(1)} %broadcast_in_dim.8), channel_id=1, replica_groups=mesh['section'=2,'dev'=64] {'section'}, dimensions={0} | all-to-all | bytes 2097152 | tf_op jit(solution)/shard_map/all_to_all | solution.py:217
  151.4 20.2 %all-gather.1 = f32[8,4,128]{2,1,0:T(4,128)S(1)} all-gather(f32[1,4,128]{2,1,0:T(4,128)S(1)} %maximum_bitcast_fusion), channel_id=2, replica_groups={{0,1,2,3,64,65,66,67},{4,5,6,7,68,69,70,71},{8,9,10,11,72,73,74,75},{12..., dimensions={0}, use_global_device_ids=true | all-gather | bytes 18432 | tf_op jit(solution)/shard_map/all_gather | solution.py:281
  (31 shorter events, 6.9 us)
Async XLA Ops:
  6.5 116.2 %all-gather.4.cloned.1.call-start = ((), (), s32[]{:S(2)}) async-start(), calls=%async_computation.5 | async-start | bytes 4456448 | tf_op jit(solution)/shard_map/all_gather | solution.py:257
  10.7 4.1 %collective-permute-start.6 = (bf16[64,512]{1,0:T(8,128)(2,1)S(1)}, bf16[64,512]{1,0:T(8,128)(2,1)S(1)}, u32[]{:S(2)}, u32[]{:S(2)}) collective-permute-start(bf16[64,512]{1,0:T(8,128)(2,1)S(1)} %get-tuple-element.36), channel_id=1, source_target_pairs={{0,3},{1,0},{2,1},{3,2},{4,7},{5,4},{6,5},{7,6},{8,11},{9,8},{10,9... | collective-permute-start | bytes 196616 | tf_op jit(solution)/shard_map/ppermute | solution.py:248
  13.5 4.7 %collective-permute-start.5 = (bf16[64,512]{1,0:T(8,128)(2,1)S(1)}, bf16[64,512]{1,0:T(8,128)(2,1)S(1)}, u32[]{:S(2)}, u32[]{:S(2)}) collective-permute-start(bf16[64,512]{1,0:T(8,128)(2,1)S(1)} %get-tuple-element.37), channel_id=1, source_target_pairs={{0,2},{1,3},{2,0},{3,1},{4,6},{5,7},{6,4},{7,5},{8,10},{9,11},{10,... | collective-permute-start | bytes 196616 | tf_op jit(solution)/shard_map/ppermute | solution.py:248
  13.8 5.0 %collective-permute-start.4 = (bf16[64,512]{1,0:T(8,128)(2,1)S(1)}, bf16[64,512]{1,0:T(8,128)(2,1)S(1)}, u32[]{:S(2)}, u32[]{:S(2)}) collective-permute-start(bf16[64,512]{1,0:T(8,128)(2,1)S(1)} %get-tuple-element.38), channel_id=1, source_target_pairs={{0,1},{1,2},{2,3},{3,0},{4,5},{5,6},{6,7},{7,4},{8,9},{9,10},{10,1... | collective-permute-start | bytes 196616 | tf_op jit(solution)/shard_map/ppermute | solution.py:248
  19.6 20.0 %all-to-all-start = ((s32[128,4,128]{2,1,0:T(4,128)}), s32[128,4,128]{2,1,0:T(4,128)S(1)}, u32[]{:S(2)}, u32[]{:S(2)}) async-start(s32[128,4,128]{2,1,0:T(4,128)} %bitcast.1), calls=%async_computation | async-start | bytes 524288 | tf_op jit(solution)/shard_map/all_to_all | solution.py:231
  30.0 7.4 %collective-permute-start.1 = (s32[16,256]{1,0:T(8,128)S(1)}, s32[16,256]{1,0:T(8,128)S(1)}, u32[]{:S(2)}, u32[]{:S(2)}) collective-permute-start(s32[16,256]{1,0:T(8,128)S(1)} %get-tuple-element.41), channel_id=1, source_target_pairs={{0,64},{1,0},{2,65},{3,1},{4,66},{5,2},{6,67},{7,3},{8,68},{9,4},{... | collective-permute-start | bytes 49160 | tf_op jit(solution)/shard_map/ppermute | solution.py:237
  33.2 5.8 %collective-permute-start = (s32[16,256]{1,0:T(8,128)S(1)}, s32[16,256]{1,0:T(8,128)S(1)}, u32[]{:S(2)}, u32[]{:S(2)}) collective-permute-start(s32[16,256]{1,0:T(8,128)S(1)} %get-tuple-element.42), channel_id=1, source_target_pairs={{0,0},{1,64},{2,1},{3,65},{4,2},{5,66},{6,3},{7,67},{8,4},{9,68},{... | collective-permute-start | bytes 49160 | tf_op jit(solution)/shard_map/ppermute | solution.py:236
  53.4 56.7 %all-to-all-start.1 = ((bf16[64,128,128]{2,1,0:T(8,128)(2,1)}), bf16[64,128,128]{2,1,0:T(8,128)(2,1)S(1)}, u32[]{:S(2)}, u32[]{:S(2)}) async-start(bf16[64,128,128]{2,1,0:T(8,128)(2,1)} %bitcast.54), calls=%async_computation.1 | async-start | bytes 4194304 | tf_op jit(solution)/shard_map/all_to_all | solution.py:261
  111.3 34.3 %collective-permute-start.7 = (bf16[128,2048]{1,0:T(8,128)(2,1)S(1)}, bf16[128,2048]{1,0:T(8,128)(2,1)S(1)}, u32[]{:S(2)}, u32[]{:S(2)}) collective-permute-start(bf16[128,2048]{1,0:T(8,128)(2,1)S(1)} %bag_unsort.1), channel_id=1, source_target_pairs={{0,2},{1,3},{2,0},{3,1},{4,6},{5,7},{6,4},{7,5},{8,10},{9,11},{10,... | collective-permute-start | bytes 1572872 | tf_op jit(solution)/shard_map/ppermute | solution.py:248
  114.3 21.2 %collective-permute-start.3 = (bf16[128,2048]{1,0:T(8,128)(2,1)S(1)}, bf16[128,2048]{1,0:T(8,128)(2,1)S(1)}, u32[]{:S(2)}, u32[]{:S(2)}) collective-permute-start(bf16[128,2048]{1,0:T(8,128)(2,1)S(1)} %bag_unsort.1), channel_id=1, source_target_pairs={{0,3},{1,0},{2,1},{3,2},{4,7},{5,4},{6,5},{7,6},{8,11},{9,8},{10,9... | collective-permute-start | bytes 1572872 | tf_op jit(solution)/shard_map/ppermute | solution.py:248
  115.2 22.8 %collective-permute-start.2 = (bf16[128,2048]{1,0:T(8,128)(2,1)S(1)}, bf16[128,2048]{1,0:T(8,128)(2,1)S(1)}, u32[]{:S(2)}, u32[]{:S(2)}) collective-permute-start(bf16[128,2048]{1,0:T(8,128)(2,1)S(1)} %bag_unsort.1), channel_id=1, source_target_pairs={{0,1},{1,2},{2,3},{3,0},{4,5},{5,6},{6,7},{7,4},{8,9},{9,10},{10,1... | collective-permute-start | bytes 1572872 | tf_op jit(solution)/shard_map/ppermute | solution.py:248
  138.3 5.8 %copy-start = (bf16[4096,512]{1,0:T(8,128)(2,1)S(1)}, bf16[4096,512]{1,0:T(8,128)(2,1)}, u32[]{:S(2)}) copy-start(bf16[4096,512]{1,0:T(8,128)(2,1)} %all-gather.4.cloned.1.call-done) | copy-start | bytes 12582916
Sparse Core Ops, SparseCore 0:
  19.8 54.1 all-gather.3

commit v5 on v3

--- a/solution.py
+++ b/solution.py
@@ -13,7 +13,6 @@
 CHUNK = 64
 SLOTS = POOL * CHUNK
 DEAD = ROWS_DEV | (8 << 16)
-PIECES = 8
 TBLK = 2048
 TSLOTS = 4
 HID_SPLIT = 2
@@ -23,7 +22,7 @@
 )
 
 
-def prep_body(x_ref, pool_ref, list_ref, bag_ref):
+def prep_body(x_ref, pool_ref, list_ref, order_ref):
     shape = (CHUNK, 128)
     tables = x_ref.shape[0]
     lane = lax.broadcasted_iota(jnp.int32, shape, 1)
@@ -58,9 +57,9 @@
             step //= 2
         size *= 2
     key = cols[0]
-    order = (key & (CHUNK - 1)).T
+    order = (((key & (CHUNK - 1)) | CHUNK) << 20).T
     for j in range(4):
-        bag_ref[:, j * CHUNK : (j + 1) * CHUNK] = order[j * tables : (j + 1) * tables, :]
+        order_ref[:, j * CHUNK : (j + 1) * CHUNK] = order[j * tables : (j + 1) * tables, :]
     kept = POOL - (key >> 6)
     v = []
     for w in cols[1:]:
@@ -94,46 +93,33 @@
         block = jnp.concatenate(groups[16 * i : 16 * i + 16], axis=0)
         block = block.T
         for j in range(4):
-            list_ref[pl.ds(4 * j + i, tables, stride=16), :] = block[j * tables : (j + 1) * tables, :]
+            rows = block[j * tables : (j + 1) * tables, :]
+            if i >= 2:
+                rows = rows | order_ref[:, (i - 2) * 128 : (i - 1) * 128]
+            list_ref[pl.ds(4 * j + i, tables, stride=16), :] = rows
 
 
 def prep(ids, pool_len):
-    tables = ids.shape[0]
     return pl.pallas_call(
         prep_body,
-        out_shape=(
-            pltpu.VMEM((128 * 4, 128), jnp.int32),
-            pltpu.VMEM((tables, 4 * CHUNK), jnp.int32),
-        ),
-        out_specs=(pl.BlockSpec(memory_space=pltpu.VMEM), pl.BlockSpec(memory_space=pltpu.VMEM)),
+        out_shape=pltpu.VMEM((128 * 4, 128), jnp.int32),
+        out_specs=pl.BlockSpec(memory_space=pltpu.VMEM),
         in_specs=[pl.BlockSpec(memory_space=pltpu.VMEM), pl.BlockSpec(memory_space=pltpu.SMEM)],
+        scratch_shapes=[pltpu.VMEM((ids.shape[0], 4 * CHUNK), jnp.int32)],
         name="bag_lists",
     )(ids, pool_len)
 
 
-def gather_body(lists_ref, table_ref, out_ref, tab, tbuf, smem, acc, obuf, tsem, lsem, osem, *, unroll):
-    chunks = out_ref.shape[0]
-    per = chunks // PIECES
-    piece = chunks * SLOTS // PIECES
-
-    def list_copy(i):
-        part = pl.ds(i * piece, piece)
-        return pltpu.make_async_copy(lists_ref.at[part], smem.at[part], lsem.at[i])
-
+def widen_body(table_ref, tab, tbuf, tsem):
     def table_copy(b):
         slot = b % TSLOTS
         return pltpu.make_async_copy(
             table_ref.at[pl.ds(b * TBLK, TBLK)], tbuf.at[slot], tsem.at[slot]
         )
 
-    def out_copy(i):
-        return pltpu.make_async_copy(obuf.at[i % 2], out_ref.at[pl.ds(i * per, per)], osem.at[i % 2])
-
     blocks = ROWS_DEV // TBLK
     for b in range(TSLOTS):
         table_copy(b).start()
-    for i in range(PIECES):
-        list_copy(i).start()
     tab[pl.ds(ROWS_DEV, 8), :] = jnp.zeros((8, E), jnp.float32)
     for b in range(blocks):
         table_copy(b).wait()
@@ -141,76 +127,130 @@
         if b + TSLOTS < blocks:
             table_copy(b + TSLOTS).start()
 
-    def level(base):
-        head = smem[base]
-        rows = [head & 0xFFFF] + [smem[base + i] for i in range(1, 8)]
-        return (head >> 16) & 15, jnp.concatenate([tab[pl.ds(r, 1), :] for r in rows], axis=0)
-
-    def chunk(c, piece):
-        base = (piece * per + c) * SLOTS
+
+def widen(table):
+    return pl.pallas_call(
+        widen_body,
+        out_shape=pltpu.VMEM((ROWS_DEV + 8, E), jnp.float32),
+        in_specs=[pl.BlockSpec(memory_space=pltpu.HBM)],
+        out_specs=pl.BlockSpec(memory_space=pltpu.VMEM),
+        scratch_shapes=[
+            pltpu.VMEM((TSLOTS, TBLK, E), jnp.bfloat16),
+            pltpu.SemaphoreType.DMA((TSLOTS,)),
+        ],
+        compiler_params=pltpu.CompilerParams(vmem_limit_bytes=6 * 2**20),
+        name="table_widen",
+    )(pltpu.with_memory_space_constraint(table, pltpu.HBM))
+
+
+def gather_body(quarter_ref, lists_ref, tab, out_ref, smem, acc, lsem, *, unroll):
+    quarter = quarter_ref[0]
+    planes = out_ref.shape[0] // 2
+    piece = 2 * SLOTS
+
+    def list_copy(m):
+        start = pl.multiple_of((4 * m + quarter) * piece, piece)
+        return pltpu.make_async_copy(
+            lists_ref.at[pl.ds(start, piece)], smem.at[pl.ds(m * piece, piece)], lsem.at[m]
+        )
+
+    for m in range(planes):
+        list_copy(m).start()
+
+    def level(at):
+        head = smem[at]
+        rows = [head & 0xFFFF] + [smem[at + i] for i in range(1, 8)]
+        rows = jnp.concatenate([tab[pl.ds(r, 1), :] for r in rows], axis=0)
+        return pl.multiple_of((head >> 13) & 0x78, 8), rows
+
+    def chunk(c, carry):
+        base = c * SLOTS
         acc[...] = jnp.zeros(acc.shape, jnp.float32)
         levels = smem[base] >> 20
 
         def step(k, carry):
             at = base + k * (8 * unroll)
             for g, rows in [level(at + 8 * u) for u in range(unroll)]:
-                acc[pl.ds(pl.multiple_of(g * 8, 8), 8), :] += rows
+                acc[pl.ds(g, 8), :] += rows
             return carry
 
-        lax.fori_loop(0, (levels + unroll - 1) // unroll, step, 0)
-        obuf[piece % 2, c] = acc[pl.ds(0, CHUNK), :].astype(jnp.bfloat16)
-
-    for i in range(PIECES):
-        list_copy(i).wait()
-        if i >= 2:
-            out_copy(i - 2).wait()
-        lax.fori_loop(0, per, lambda c, carry: (chunk(c, i), carry)[1], 0)
-        out_copy(i).start()
-    out_copy(PIECES - 2).wait()
-    out_copy(PIECES - 1).wait()
-
-
-def gather(lists, table, chunks, unroll=4):
+        lax.fori_loop(0, (levels + unroll - 1) >> (unroll.bit_length() - 1), step, 0)
+        out_ref[c] = acc[pl.ds(0, CHUNK), :].astype(jnp.bfloat16)
+        return carry
+
+    for m in range(planes):
+        list_copy(m).wait()
+    lax.fori_loop(0, 2 * planes, chunk, 0)
+
+
+def gather(quarter, lists, tab, planes, unroll=4):
     return pl.pallas_call(
         functools.partial(gather_body, unroll=unroll),
-        out_shape=pltpu.HBM((chunks, CHUNK, E), jnp.bfloat16),
-        in_specs=[pl.BlockSpec(memory_space=pl.ANY), pl.BlockSpec(memory_space=pltpu.HBM)],
-        out_specs=pl.BlockSpec(memory_space=pltpu.HBM),
+        out_shape=pltpu.VMEM((2 * planes, CHUNK, E), jnp.bfloat16),
+        in_specs=[
+            pl.BlockSpec(memory_space=pltpu.SMEM),
+            pl.BlockSpec(memory_space=pl.ANY),
+            pl.BlockSpec(memory_space=pltpu.VMEM),
+        ],
+        out_specs=pl.BlockSpec(memory_space=pltpu.VMEM),
         scratch_shapes=[
-            pltpu.VMEM((ROWS_DEV + 8, E), jnp.float32),
-            pltpu.VMEM((TSLOTS, TBLK, E), jnp.bfloat16),
-            pltpu.SMEM((chunks * SLOTS,), jnp.int32),
+            pltpu.SMEM((2 * planes * SLOTS,), jnp.int32),
             pltpu.VMEM((CHUNK + 8, E), jnp.float32),
-            pltpu.VMEM((2, chunks // PIECES, CHUNK, E), jnp.bfloat16),
-            pltpu.SemaphoreType.DMA((TSLOTS,)),
-            pltpu.SemaphoreType.DMA((PIECES,)),
-            pltpu.SemaphoreType.DMA((2,)),
+            pltpu.SemaphoreType.DMA((planes,)),
         ],
-        compiler_params=pltpu.CompilerParams(vmem_limit_bytes=32 * 2**20),
+        compiler_params=pltpu.CompilerParams(vmem_limit_bytes=4 * 2**20),
         name="bag_gather",
-    )(lists, pltpu.with_memory_space_constraint(table, pltpu.HBM))
-
-
-def unsort_body(part_ref, low_ref, high_ref, out_ref):
-    tables = out_ref.shape[1] // E
+    )(quarter, lists, tab)
+
+
+def combine_body(y_ref, lists_ref, part_0, part_1, part_2, part_3, out_ref):
+    y = y_ref[0]
+    parts = (part_0, part_1, part_2, part_3)
     bag = lax.broadcasted_iota(jnp.int32, (CHUNK, 4 * CHUNK), 0)
-    for t in range(tables):
-        for h in range(2):
-            where = (low_ref, high_ref)[h][t : t + 1, :]
-            pick = (bag == where).astype(jnp.float32).astype(jnp.bfloat16)
-            rows = part_ref[4 * t : 4 * t + 4, h].reshape(4 * CHUNK, E)
-            total = jnp.dot(pick, rows, preferred_element_type=jnp.float32)
-            out_ref[h * CHUNK : (h + 1) * CHUNK, t * E : (t + 1) * E] = total.astype(jnp.bfloat16)
-
-
-def unsort(parts, low, high):
-    return pl.pallas_call(
-        unsort_body,
-        out_shape=pltpu.VMEM((2 * CHUNK, parts.shape[0] // 4 * E), jnp.bfloat16),
-        in_specs=[pl.BlockSpec(memory_space=pltpu.VMEM)] * 3,
-        out_specs=pl.BlockSpec(memory_space=pltpu.VMEM),
-        name="bag_unsort",
-    )(pltpu.with_memory_space_constraint(parts, pltpu.VMEM), low, high)
+    for c in range(out_ref.shape[0]):
+        source = 8 * (c // 2) + 2 * y + c % 2
+        words = lax.shift_right_logical(lists_ref[source], 20) & (CHUNK - 1)
+        where = jnp.concatenate([words[2:3, :], words[3:4, :]], axis=1)
+        pick = (bag == where).astype(jnp.float32).astype(jnp.bfloat16)
+        rows = []
+        for j in range(4):
+            came = (y - j) & 3
+            row = parts[3][c]
+            for k in range(3):
+                row = jnp.where(came == k, parts[k][c], row)
+            rows.append(row)
+        total = jnp.dot(pick, jnp.concatenate(rows, axis=0), preferred_element_type=jnp.float32)
+        out_ref[c] = total.astype(jnp.bfloat16)
+
+
+def combine(y, lists, parts):
+    vmem = pl.BlockSpec(memory_space=pltpu.VMEM)
+    return pl.pallas_call(
+        combine_body,
+        out_shape=pltpu.VMEM(parts[0].shape, jnp.bfloat16),
+        in_specs=[pl.BlockSpec(memory_space=pltpu.SMEM)] + [vmem] * 5,
+        out_specs=vmem,
+        compiler_params=pltpu.CompilerParams(vmem_limit_bytes=4 * 2**20),
+        name="bag_combine",
+    )(y, lists, *[pltpu.with_memory_space_constraint(p, pltpu.VMEM) for p in parts])
+
+
+def rows_body(pooled_ref, out_ref):
+    for t in range(pooled_ref.shape[0]):
+        out_ref[:, t * E : (t + 1) * E] = pooled_ref[t]
+
+
+def feature_rows(pooled):
+    tables, samples, _ = pooled.shape
+    vmem = pl.BlockSpec(memory_space=pltpu.VMEM)
+    return pl.pallas_call(
+        rows_body,
+        out_shape=pltpu.VMEM((samples, tables * E), jnp.bfloat16),
+        in_specs=[vmem],
+        out_specs=vmem,
+        compiler_params=pltpu.CompilerParams(vmem_limit_bytes=2 * 2**20),
+        name="feature_rows",
+    )(pltpu.with_memory_space_constraint(pooled, pltpu.VMEM))
 
 
 def swap(x, axis):
@@ -224,7 +264,7 @@
     half = n_tables // n_sec
     section = lax.axis_index("section")
     dev = lax.axis_index("dev")
-    lists, order = prep(jnp.transpose(indices, (1, 2, 0)), pool_len)
+    lists = prep(jnp.transpose(indices, (1, 2, 0)), pool_len)
     ring = 4
     rows, cols = w_first.shape
     part = cols // HID_SPLIT
@@ -244,19 +284,19 @@
     pieces = [lax.dynamic_index_in_dim(pieces, (y - k) % ring, 0, False) for k in range(ring)]
     whole = lax.all_gather(jnp.concatenate(pieces), "dev", axis_index_groups=levels, tiled=True)
     both_axes = ("section", "dev")
-    blocks = range(n_sec * n_dev)
     arrived = lax.all_to_all(lists.reshape(n_sec * n_dev, 4, 128), both_axes, 0, 0, tiled=True)
-    order = order.reshape(n_sec, half, 4 * CHUNK)
-    odd = dev % 2
-    straight = [(b, (b % 2) * n_dev + b // 2) for b in blocks]
-    crossed = [(b, (1 - b % 2) * n_dev + b // 2) for b in blocks]
-    same = lax.ppermute(lax.dynamic_index_in_dim(order, odd, 0, False), both_axes, straight)
-    cross = lax.ppermute(lax.dynamic_index_in_dim(order, 1 - odd, 0, False), both_axes, crossed)
-    low = jnp.where(section == 0, same, cross)
-    high = jnp.where(section == 0, cross, same)
-    parts = gather(arrived.reshape(-1), tables, n_sec * n_dev)
-    parts = lax.all_to_all(parts.reshape(n_dev, 2 * CHUNK, E), "dev", 0, 0, tiled=True)
-    features = unsort(parts.reshape(n_dev, 2, CHUNK, E), low, high)
+    line = lax.broadcasted_iota(jnp.int32, arrived.shape, 1)
+    clean = jnp.where(line < 2, arrived, arrived & 0xFFFFF).reshape(-1)
+    tab = widen(tables)
+    parts = {}
+    for k in (2, 1, 3, 0):
+        quarter = ((y + k) % ring).reshape(1)
+        sums = gather(quarter, clean, tab, planes)
+        parts[k] = along(sums, k) if k else sums
+    pooled = combine(y.reshape(1), arrived, [parts[k] for k in range(ring)])
+    pooled = pooled.reshape(planes, 2 * CHUNK, E)
+    pooled = lax.all_to_all(pooled, "dev", 0, 0, axis_index_groups=levels, tiled=True)
+    features = feature_rows(pooled)
     bias = lax.dynamic_slice(b_first, (q * part,), (part,)).astype(jnp.float32)
     scale = lax.dynamic_slice(w_out, (q * part,), (part,)).astype(jnp.float32)
     far = lax.ppermute(features, "dev", [(d, d ^ 1) for d in range(n_dev)])

time: 154 us -> 144 us (0.935)
  blocking collectives: 39.3 us -> 17.8 us
  waiting for transfers between devices: 33.1 us -> 17.5 us
  starting transfers between devices: 28.8 us -> 40.5 us
  local copies, waits for them, and re-layouts: 1.82 us -> 13.5 us
  Pallas kernels: 27.4 us -> 30.9 us
    ppermute x2 -> x0, waiting for transfers between devices: 25.8 us -> none  [the longest x1 25.4 us: body(): lax.ppermute(lax.dynamic_index_in_dim(order, 1 - odd, 0, False), both_axe...]
    all_to_all x1 -> x0, blocking collectives: 21.5 us -> none  [body(): lax.all_to_all(lists.reshape(n_sec * n_dev, 4, 128), both_axes, 0, 0, til...]
    all_to_all x1 -> x2, starting transfers between devices: 15 us -> 27.5 us  [the longest x1 16.6 us: body(): lax.all_to_all(pooled, 'dev', 0, 0, axis_index_groups=levels, tiled=True)]
    unnamed x8 -> x12, local copies, waits for them, and re-layouts: 0.02 us -> 11.7 us
    ppermute x2 -> x0, starting transfers between devices: 6.69 us -> none  [the longest x1 4 us: body(): lax.ppermute(lax.dynamic_index_in_dim(order, odd, 0, False), both_axes, s...]
    pallas_call x2 -> x4, Pallas kernels: 3.67 us -> 10.4 us  [the longest x1 5.38 us: widen(): pl.pallas_call(widen_body, out_shape=pltpu.VMEM((ROWS_DEV + 8, E), jnp.fl...]
    ppermute x3 -> x6, waiting for transfers between devices: 2.14 us -> 8.31 us  [along(): lax.ppermute(x, 'dev', [(d, d // ring * ring + (d + k) % ring) for d in r...]
    ppermute x3 -> x6, starting transfers between devices: 5.87 us -> 10.9 us  [along(): lax.ppermute(x, 'dev', [(d, d // ring * ring + (d + k) % ring) for d in r...]
  transfers between devices with their start and end apart: 8 -> 10, of which waited for: 4 -> 4; matrix products, arithmetic and copies ran while one was open for 5% -> 5% of each run, Pallas kernels for 18% -> 22%
where the time goes in v5:
time: 144 us; the launch traced here: 143 us
  starting transfers between devices  40.5 us (28%)
  Pallas kernels  30.9 us (21%)
  blocking collectives  17.8 us (12%)
  waiting for transfers between devices  17.5 us (12%)
  between operations  13.6 us (9%)
  local copies, waits for them, and re-layouts  13.5 us (9%)
  matrix products  7.91 us (5%)
    pallas_call x4, Pallas kernels, gather(): pl.pallas_call(functools.partial(gather_body, unroll=unroll), out_shape=p...  20.6 us
    all_to_all x1, starting transfers between devices, body(): lax.all_to_all(pooled, 'dev', 0, 0, axis_index_groups=levels, tiled=True)  16.6 us
    all_to_all x2, blocking collectives, swap(): lax.all_to_all(jnp.broadcast_to(x[None], (2, *x.shape)), axis, 0, 0, tile...  12.3 us
    unnamed x12, local copies, waits for them, and re-layouts  11.7 us
    all_to_all x1, starting transfers between devices, body(): lax.all_to_all(lists.reshape(n_sec * n_dev, 4, 128), both_axes, 0, 0, til...  10.9 us
    ppermute x6, starting transfers between devices, along(): lax.ppermute(x, 'dev', [(d, d // ring * ring + (d + k) % ring) for d in r...  10.9 us
    all_to_all x1, waiting for transfers between devices, body(): lax.all_to_all(pooled, 'dev', 0, 0, axis_index_groups=levels, tiled=True)  9.15 us
    ppermute x6, waiting for transfers between devices, along(): lax.ppermute(x, 'dev', [(d, d // ring * ring + (d + k) % ring) for d in r...  8.31 us
  transfers between devices with their start and end apart: 10, of which 4 were waited for; matrix products, arithmetic and copies ran while one was open for 5% of the time, Pallas kernels for 22%

profile of v5, /device:TPU:1, one launch (start us, length us, event | category | flops | bytes accessed | tf_op | source)
XLA Modules:
  0.0 142.9 jit_solution(16809120922405967720)
XLA Ops:
  7.5 2.2 %collective-permute-start = (bf16[64,1024]{1,0:T(8,128)(2,1)S(1)}, bf16[64,1024]{1,0:T(8,128)(2,1)S(1)}, u32[]{:S(2)}, u32[]{:S(2)}) collective-permute-start(bf16[64,1024]{1,0:T(8,128)(2,1)S(1)} %get-tuple-element.23), channel_id=1, source_target_pairs={{0,1},{1,2},{2,3},{3,0},{4,5},{5,6},{6,7},{7,4},{8,9},{9,10},{10,1... | collective-permute-start | bytes 393224 | tf_op jit(solution)/shard_map/ppermute | solution.py:279
  9.7 2.6 %collective-permute-start.1 = (bf16[64,1024]{1,0:T(8,128)(2,1)S(1)}, bf16[64,1024]{1,0:T(8,128)(2,1)S(1)}, u32[]{:S(2)}, u32[]{:S(2)}) collective-permute-start(bf16[64,1024]{1,0:T(8,128)(2,1)S(1)} %get-tuple-element.13), channel_id=1, source_target_pairs={{0,2},{1,3},{2,0},{3,1},{4,6},{5,7},{6,4},{7,5},{8,10},{9,11},{10,... | collective-permute-start | bytes 393224 | tf_op jit(solution)/shard_map/ppermute | solution.py:279
  13.4 3.2 %bag_lists.1 = s32[512,128]{1,0:T(8,128)} custom-call(s32[32,8,64]{2,1,0:T(8,128)} %bitcast.46, s32[32]{0:T(128)} %pool_ref.1), custom_call_target="tpu_custom_call" | custom-call | tf_op jit(solution)/shard_map/bag_lists/pallas_call | solution.py:103
  19.1 10.9 %all-to-all-start = ((s32[128,4,128]{2,1,0:T(4,128)}), s32[128,4,128]{2,1,0:T(4,128)S(1)}, u32[]{:S(2)}, u32[]{:S(2)}) async-start(s32[128,4,128]{2,1,0:T(4,128)} %bitcast.2), calls=%async_computation | async-start | bytes 524288 | tf_op jit(solution)/shard_map/all_to_all | solution.py:287
  30.0 5.4 %table_widen.1.tab = f32[32776,128]{1,0:T(8,128)S(1)} custom-call(bf16[32768,128]{1,0:T(8,128)(2,1)} %table_ref.1), custom_call_target="tpu_custom_call" | custom-call | tf_op jit(solution)/shard_map/table_widen/pallas_call | solution.py:132
  35.4 5.7 %copy-done = f32[32776,128]{1,0:T(8,128)} copy-done((f32[32776,128]{1,0:T(8,128)}, f32[32776,128]{1,0:T(8,128)S(1)}, u32[]{:S(2)}) %copy-start) | copy-done | bytes 16781336
  41.3 6.0 %copy-done.1 = f32[32776,128]{1,0:T(8,128)S(1)} copy-done((f32[32776,128]{1,0:T(8,128)S(1)}, f32[32776,128]{1,0:T(8,128)}, u32[]{:S(2)}) %copy-start.1) | copy-done | bytes 16781336
  47.3 5.1 %bag_gather.5 = bf16[32,64,128]{2,1,0:T(8,128)(2,1)S(1)} custom-call(s32[1]{0:T(128)} %bitcast.5.quarter_ref, s32[65536]{0:T(1024)S(1)} %bitcast.41, f32[32776,128]{1,0:T(8,128)S(1)} %copy-done.1), custom_call_target="tpu_custom_call" | custom-call | tf_op jit(solution)/shard_map/bag_gather/pallas_call | solution.py:187
  52.4 1.6 %collective-permute-start.3 = (bf16[32,64,128]{2,1,0:T(8,128)(2,1)S(1)}, bf16[32,64,128]{2,1,0:T(8,128)(2,1)S(1)}, u32[]{:S(2)}, u32[]{:S(2)}) collective-permute-start(bf16[32,64,128]{2,1,0:T(8,128)(2,1)S(1)} %bag_gather.5), channel_id=1, source_target_pairs={{0,1},{1,2},{2,3},{3,0},{4,5},{5,6},{6,7},{7,4},{8,9},{9,10},{10,1... | collective-permute-start | bytes 1572872 | tf_op jit(solution)/shard_map/ppermute | solution.py:279
  54.0 5.3 %bag_gather.6 = bf16[32,64,128]{2,1,0:T(8,128)(2,1)S(1)} custom-call(s32[1]{0:T(128)} %bitcast.6.quarter_ref, s32[65536]{0:T(1024)S(1)} %bitcast.42, f32[32776,128]{1,0:T(8,128)S(1)} %copy-done.1), custom_call_target="tpu_custom_call" | custom-call | tf_op jit(solution)/shard_map/bag_gather/pallas_call | solution.py:187
  59.2 2.3 %collective-permute-start.4 = (bf16[32,64,128]{2,1,0:T(8,128)(2,1)S(1)}, bf16[32,64,128]{2,1,0:T(8,128)(2,1)S(1)}, u32[]{:S(2)}, u32[]{:S(2)}) collective-permute-start(bf16[32,64,128]{2,1,0:T(8,128)(2,1)S(1)} %bag_gather.6), channel_id=1, source_target_pairs={{0,2},{1,3},{2,0},{3,1},{4,6},{5,7},{6,4},{7,5},{8,10},{9,11},{10,... | collective-permute-start | bytes 1572872 | tf_op jit(solution)/shard_map/ppermute | solution.py:279
  61.5 5.1 %bag_gather.7 = bf16[32,64,128]{2,1,0:T(8,128)(2,1)S(1)} custom-call(s32[1]{0:T(128)} %bitcast.7.quarter_ref, s32[65536]{0:T(1024)S(1)} %bitcast.43, f32[32776,128]{1,0:T(8,128)S(1)} %copy-done.1), custom_call_target="tpu_custom_call" | custom-call | tf_op jit(solution)/shard_map/bag_gather/pallas_call | solution.py:187
  67.8 5.1 %bag_gather.4.part_0 = bf16[32,64,128]{2,1,0:T(8,128)(2,1)S(1)} custom-call(s32[1]{0:T(128)} %bitcast.3.quarter_ref, s32[65536]{0:T(1024)S(1)} %bitcast.44, f32[32776,128]{1,0:T(8,128)S(1)} %copy-done.1), custom_call_target="tpu_custom_call" | custom-call | tf_op jit(solution)/shard_map/bag_gather/pallas_call | solution.py:187
  72.9 2.9 %collective-permute-done.4.part_2 = bf16[32,64,128]{2,1,0:T(8,128)(2,1)S(1)} collective-permute-done((bf16[32,64,128]{2,1,0:T(8,128)(2,1)S(1)}, bf16[32,64,128]{2,1,0:T(8,128)(2,1)S(1)}, u32[]{:S(2)}, u32[]{:S(2)}) %collective-permute-start.4) | collective-permute-done | bytes 524320 | tf_op jit(solution)/shard_map/ppermute | solution.py:279
  75.8 3.9 %collective-permute-done.5.part_3 = bf16[32,64,128]{2,1,0:T(8,128)(2,1)S(1)} collective-permute-done((bf16[32,64,128]{2,1,0:T(8,128)(2,1)S(1)}, bf16[32,64,128]{2,1,0:T(8,128)(2,1)S(1)}, u32[]{:S(2)}, u32[]{:S(2)}) %collective-permute-start.5) | collective-permute-done | bytes 524320 | tf_op jit(solution)/shard_map/ppermute | solution.py:279
  79.8 1.6 %bag_combine.1 = bf16[32,64,128]{2,1,0:T(8,128)(2,1)} custom-call(s32[1]{0:T(128)} %bitcast.y_ref, s32[128,4,128]{2,1,0:T(4,128)S(1)} %all-to-all-done.lists_ref, bf16[32,64,128]{2,1,0:T(8,128)(2,1)S(1)} %bag_gather.4.part_0, bf16[32,64,128]{2,1,0:T(8,128)(2,1)S(1)} %collective-permute-done.3.part_1, bf16[32,64,128]{2,1,0:T(8,128)(2,1)S(1)} %collective-permute-done.4.part_2, ...), custom_call_target="tpu_custom_call" | custom-call | tf_op jit(solution)/shard_map/bag_combine/pallas_call | solution.py:228
  81.4 16.6 %all-to-all-start.1 = ((bf16[16,128,128]{2,1,0:T(8,128)(2,1)}), bf16[16,128,128]{2,1,0:T(8,128)(2,1)S(1)}, u32[]{:S(2)}, u32[]{:S(2)}) async-start(bf16[16,128,128]{2,1,0:T(8,128)(2,1)} %bitcast.8), calls=%async_computation.1 | async-start | bytes 1048576 | tf_op jit(solution)/shard_map/all_to_all | solution.py:298
  98.1 9.1 %all-to-all-done.1.pooled_ref = bf16[16,128,128]{2,1,0:T(8,128)(2,1)S(1)} async-done(((bf16[16,128,128]{2,1,0:T(8,128)(2,1)}), bf16[16,128,128]{2,1,0:T(8,128)(2,1)S(1)}, u32[]{:S(2)}, u32[]{:S(2)}) %all-to-all-start.1) | async-done | bytes 524320 | tf_op jit(solution)/shard_map/all_to_all | solution.py:298
  107.3 2.2 %collective-permute-start.6 = (bf16[128,2048]{1,0:T(8,128)(2,1)S(1)}, bf16[128,2048]{1,0:T(8,128)(2,1)S(1)}, u32[]{:S(2)}, u32[]{:S(2)}) collective-permute-start(bf16[128,2048]{1,0:T(8,128)(2,1)S(1)} %feature_rows.1), channel_id=1, source_target_pairs={{0,1},{1,0},{2,3},{3,2},{4,5},{5,4},{6,7},{7,6},{8,9},{9,8},{10,11... | collective-permute-start | bytes 1572872 | tf_op jit(solution)/shard_map/ppermute | solution.py:302
  109.6 7.7 %all_to_all.20 = bf16[2,128,2048]{2,1,0:T(8,128)(2,1)S(1)} all-to-all(bf16[2,128,2048]{2,1,0:T(8,128)(2,1)S(1)} %broadcast_in_dim.4), channel_id=1, replica_groups=mesh['section'=2,'dev'=64] {'section'}, dimensions={0} | all-to-all | bytes 2097152 | tf_op jit(solution)/shard_map/all_to_all | solution.py:257
  117.4 3.1 %fusion.2 = f32[128,1024]{1,0:T(8,128)S(1)} fusion(bf16[4096,1024]{1,0:T(8,128)(2,1)} %all-gather.4.cloned.1.call-done, bf16[2,128,2048]{2,1,0:T(8,128)(2,1)S(1)} %all_to_all.20), kind=kOutput, calls=%fused_computation.2 | convolution fusion | flops 536870912 | bytes 5242880 | tf_op jit(solution)/shard_map/dot_general | solution.py:308
  120.5 3.2 %fusion.32 = f32[128]{0:T(128)S(1)} fusion(f32[128,1024]{1,0:T(8,128)S(1)} %fusion.2, bf16[4096,1024]{1,0:T(8,128)(2,1)} %all-gather.4.cloned.1.call-done, bf16[2,128,2048]{2,1,0:T(8,128)(2,1)S(1)} %all_to_all.20, f32[1024]{0:T(1024)S(1)} %get-tuple-element.27, f32[1024]{0:T(1024)S(1)} %get-tuple-element.28), kind=kOutput, calls=%fused_computation.16 | convolution fusion | flops 537526144 | bytes 5251584 | tf_op jit(solution)/shard_map/dot_general | solution.py:307
  123.8 4.6 %all_to_all.21 = bf16[2,128,2048]{2,1,0:T(8,128)(2,1)S(1)} all-to-all(bf16[2,128,2048]{2,1,0:T(8,128)(2,1)S(1)} %broadcast_in_dim.5), channel_id=1, replica_groups=mesh['section'=2,'dev'=64] {'section'}, dimensions={0} | all-to-all | bytes 2097152 | tf_op jit(solution)/shard_map/all_to_all | solution.py:257
  130.1 5.5 %all-gather.1 = f32[4,2,128]{2,1,0:T(2,128)S(1)} all-gather(f32[1,2,128]{2,1,0:T(2,128)S(1)} %maximum_bitcast_fusion), channel_id=2, replica_groups={{0,1,64,65},{2,3,66,67},{4,5,68,69},{6,7,70,71},{8,9,72,73},{10,11,74,7..., dimensions={0}, use_global_device_ids=true | all-gather | bytes 5120 | tf_op jit(solution)/shard_map/all_gather | solution.py:317
  (38 shorter events, 8.3 us)
Async XLA Ops:
  6.5 110.8 %all-gather.4.cloned.1.call-start = ((), (), s32[]{:S(2)}) async-start(), calls=%async_computation.4 | async-start | bytes 8912896 | tf_op jit(solution)/shard_map/all_gather | solution.py:285
  7.5 9.1 %collective-permute-start = (bf16[64,1024]{1,0:T(8,128)(2,1)S(1)}, bf16[64,1024]{1,0:T(8,128)(2,1)S(1)}, u32[]{:S(2)}, u32[]{:S(2)}) collective-permute-start(bf16[64,1024]{1,0:T(8,128)(2,1)S(1)} %get-tuple-element.23), channel_id=1, source_target_pairs={{0,1},{1,2},{2,3},{3,0},{4,5},{5,6},{6,7},{7,4},{8,9},{9,10},{10,1... | collective-permute-start | bytes 393224 | tf_op jit(solution)/shard_map/ppermute | solution.py:279
  9.7 8.3 %collective-permute-start.1 = (bf16[64,1024]{1,0:T(8,128)(2,1)S(1)}, bf16[64,1024]{1,0:T(8,128)(2,1)S(1)}, u32[]{:S(2)}, u32[]{:S(2)}) collective-permute-start(bf16[64,1024]{1,0:T(8,128)(2,1)S(1)} %get-tuple-element.13), channel_id=1, source_target_pairs={{0,2},{1,3},{2,0},{3,1},{4,6},{5,7},{6,4},{7,5},{8,10},{9,11},{10,... | collective-permute-start | bytes 393224 | tf_op jit(solution)/shard_map/ppermute | solution.py:279
  12.3 5.7 %collective-permute-start.2 = (bf16[64,1024]{1,0:T(8,128)(2,1)S(1)}, bf16[64,1024]{1,0:T(8,128)(2,1)S(1)}, u32[]{:S(2)}, u32[]{:S(2)}) collective-permute-start(bf16[64,1024]{1,0:T(8,128)(2,1)S(1)} %get-tuple-element.23), channel_id=1, source_target_pairs={{0,3},{1,0},{2,1},{3,2},{4,7},{5,4},{6,5},{7,6},{8,11},{9,8},{10,9... | collective-permute-start | bytes 393224 | tf_op jit(solution)/shard_map/ppermute | solution.py:279
  19.1 22.1 %all-to-all-start = ((s32[128,4,128]{2,1,0:T(4,128)}), s32[128,4,128]{2,1,0:T(4,128)S(1)}, u32[]{:S(2)}, u32[]{:S(2)}) async-start(s32[128,4,128]{2,1,0:T(4,128)} %bitcast.2), calls=%async_computation | async-start | bytes 524288 | tf_op jit(solution)/shard_map/all_to_all | solution.py:287
  35.4 5.7 %copy-start = (f32[32776,128]{1,0:T(8,128)}, f32[32776,128]{1,0:T(8,128)S(1)}, u32[]{:S(2)}) copy-start(f32[32776,128]{1,0:T(8,128)S(1)} %table_widen.1.tab) | copy-start | bytes 50343940
  41.3 6.0 %copy-start.1 = (f32[32776,128]{1,0:T(8,128)S(1)}, f32[32776,128]{1,0:T(8,128)}, u32[]{:S(2)}) copy-start(f32[32776,128]{1,0:T(8,128)} %copy-done) | copy-start | bytes 50343940
  52.4 20.5 %collective-permute-start.3 = (bf16[32,64,128]{2,1,0:T(8,128)(2,1)S(1)}, bf16[32,64,128]{2,1,0:T(8,128)(2,1)S(1)}, u32[]{:S(2)}, u32[]{:S(2)}) collective-permute-start(bf16[32,64,128]{2,1,0:T(8,128)(2,1)S(1)} %bag_gather.5), channel_id=1, source_target_pairs={{0,1},{1,2},{2,3},{3,0},{4,5},{5,6},{6,7},{7,4},{8,9},{9,10},{10,1... | collective-permute-start | bytes 1572872 | tf_op jit(solution)/shard_map/ppermute | solution.py:279
  59.2 16.6 %collective-permute-start.4 = (bf16[32,64,128]{2,1,0:T(8,128)(2,1)S(1)}, bf16[32,64,128]{2,1,0:T(8,128)(2,1)S(1)}, u32[]{:S(2)}, u32[]{:S(2)}) collective-permute-start(bf16[32,64,128]{2,1,0:T(8,128)(2,1)S(1)} %bag_gather.6), channel_id=1, source_target_pairs={{0,2},{1,3},{2,0},{3,1},{4,6},{5,7},{6,4},{7,5},{8,10},{9,11},{10,... | collective-permute-start | bytes 1572872 | tf_op jit(solution)/shard_map/ppermute | solution.py:279
  66.6 13.1 %collective-permute-start.5 = (bf16[32,64,128]{2,1,0:T(8,128)(2,1)S(1)}, bf16[32,64,128]{2,1,0:T(8,128)(2,1)S(1)}, u32[]{:S(2)}, u32[]{:S(2)}) collective-permute-start(bf16[32,64,128]{2,1,0:T(8,128)(2,1)S(1)} %bag_gather.7), channel_id=1, source_target_pairs={{0,3},{1,0},{2,1},{3,2},{4,7},{5,4},{6,5},{7,6},{8,11},{9,8},{10,9... | collective-permute-start | bytes 1572872 | tf_op jit(solution)/shard_map/ppermute | solution.py:279
  67.8 30.3 %copy-start.2 = (bf16[2048]{0:T(1024)(128)(2,1)S(1)}, bf16[2048]{0:T(1024)(128)(2,1)}, u32[]{:S(2)}) copy-start(bf16[2048]{0:T(1024)(128)(2,1)} %param.11) | copy-start | bytes 12292
  67.8 30.3 %copy-start.3 = (bf16[2048]{0:T(1024)(128)(2,1)S(1)}, bf16[2048]{0:T(1024)(128)(2,1)}, u32[]{:S(2)}) copy-start(bf16[2048]{0:T(1024)(128)(2,1)} %param.10) | copy-start | bytes 12292
  81.4 25.8 %all-to-all-start.1 = ((bf16[16,128,128]{2,1,0:T(8,128)(2,1)}), bf16[16,128,128]{2,1,0:T(8,128)(2,1)S(1)}, u32[]{:S(2)}, u32[]{:S(2)}) async-start(bf16[16,128,128]{2,1,0:T(8,128)(2,1)} %bitcast.8), calls=%async_computation.1 | async-start | bytes 1048576 | tf_op jit(solution)/shard_map/all_to_all | solution.py:298
  107.3 16.4 %collective-permute-start.6 = (bf16[128,2048]{1,0:T(8,128)(2,1)S(1)}, bf16[128,2048]{1,0:T(8,128)(2,1)S(1)}, u32[]{:S(2)}, u32[]{:S(2)}) collective-permute-start(bf16[128,2048]{1,0:T(8,128)(2,1)S(1)} %feature_rows.1), channel_id=1, source_target_pairs={{0,1},{1,0},{2,3},{3,2},{4,5},{5,4},{6,7},{7,6},{8,9},{9,8},{10,11... | collective-permute-start | bytes 1572872 | tf_op jit(solution)/shard_map/ppermute | solution.py:302
  117.4 11.0 %slice-start = ((s8[8388608]{0:T(1024)(128)(4,1)}), s8[4194304]{0:T(1024)(128)(4,1)S(1)}, s32[]{:S(2)}) async-start(s8[8388608]{0:T(1024)(128)(4,1)} %bitcast.50), calls=%async_computation.5 | async-start | bytes 8388608
  120.5 8.0 %slice-start.1 = ((s8[8388608]{0:T(1024)(128)(4,1)}), s8[4194304]{0:T(1024)(128)(4,1)S(1)}, s32[]{:S(2)}) async-start(s8[8388608]{0:T(1024)(128)(4,1)} %bitcast.50), calls=%async_computation.6 | async-start | bytes 8388608
Sparse Core Ops, SparseCore 0:
  19.2 73.7 all-gather.3

commit v6 on v5

--- a/solution.py
+++ b/solution.py
@@ -110,40 +110,11 @@
     )(ids, pool_len)
 
 
-def widen_body(table_ref, tab, tbuf, tsem):
-    def table_copy(b):
-        slot = b % TSLOTS
-        return pltpu.make_async_copy(
-            table_ref.at[pl.ds(b * TBLK, TBLK)], tbuf.at[slot], tsem.at[slot]
-        )
-
-    blocks = ROWS_DEV // TBLK
-    for b in range(TSLOTS):
-        table_copy(b).start()
-    tab[pl.ds(ROWS_DEV, 8), :] = jnp.zeros((8, E), jnp.float32)
-    for b in range(blocks):
-        table_copy(b).wait()
-        tab[pl.ds(b * TBLK, TBLK), :] = tbuf[b % TSLOTS].astype(jnp.float32)
-        if b + TSLOTS < blocks:
-            table_copy(b + TSLOTS).start()
-
-
-def widen(table):
-    return pl.pallas_call(
-        widen_body,
-        out_shape=pltpu.VMEM((ROWS_DEV + 8, E), jnp.float32),
-        in_specs=[pl.BlockSpec(memory_space=pltpu.HBM)],
-        out_specs=pl.BlockSpec(memory_space=pltpu.VMEM),
-        scratch_shapes=[
-            pltpu.VMEM((TSLOTS, TBLK, E), jnp.bfloat16),
-            pltpu.SemaphoreType.DMA((TSLOTS,)),
-        ],
-        compiler_params=pltpu.CompilerParams(vmem_limit_bytes=6 * 2**20),
-        name="table_widen",
-    )(pltpu.with_memory_space_constraint(table, pltpu.HBM))
-
-
-def gather_body(quarter_ref, lists_ref, tab, out_ref, smem, acc, lsem, *, unroll):
+def gather_body(quarter_ref, lists_ref, *refs, unroll, widen):
+    if widen:
+        table_ref, out_ref, tab, tbuf, tsem, smem, acc, lsem = refs
+    else:
+        tab, out_ref, smem, acc, lsem = refs
     quarter = quarter_ref[0]
     planes = out_ref.shape[0] // 2
     piece = 2 * SLOTS
@@ -151,11 +122,31 @@
     def list_copy(m):
         start = pl.multiple_of((4 * m + quarter) * piece, piece)
         return pltpu.make_async_copy(
-            lists_ref.at[pl.ds(start, piece)], smem.at[pl.ds(m * piece, piece)], lsem.at[m]
+            lists_ref.at[pl.ds(start, piece)],
+            smem.at[pl.ds(pl.multiple_of(m * piece, piece), piece)],
+            lsem.at[m],
         )
 
+    if widen:
+
+        def table_copy(b):
+            slot = b % TSLOTS
+            return pltpu.make_async_copy(
+                table_ref.at[pl.ds(b * TBLK, TBLK)], tbuf.at[slot], tsem.at[slot]
+            )
+
+        blocks = ROWS_DEV // TBLK
+        for b in range(TSLOTS):
+            table_copy(b).start()
     for m in range(planes):
         list_copy(m).start()
+    if widen:
+        tab[pl.ds(ROWS_DEV, 8), :] = jnp.zeros((8, E), jnp.float32)
+        for b in range(blocks):
+            table_copy(b).wait()
+            tab[pl.ds(b * TBLK, TBLK), :] = tbuf[b % TSLOTS].astype(jnp.float32)
+            if b + TSLOTS < blocks:
+                table_copy(b + TSLOTS).start()
 
     def level(at):
         head = smem[at]
@@ -163,7 +154,7 @@
         rows = jnp.concatenate([tab[pl.ds(r, 1), :] for r in rows], axis=0)
         return pl.multiple_of((head >> 13) & 0x78, 8), rows
 
-    def chunk(c, carry):
+    def chunk(c):
         base = c * SLOTS
         acc[...] = jnp.zeros(acc.shape, jnp.float32)
         levels = smem[base] >> 20
@@ -176,31 +167,40 @@
 
         lax.fori_loop(0, (levels + unroll - 1) >> (unroll.bit_length() - 1), step, 0)
         out_ref[c] = acc[pl.ds(0, CHUNK), :].astype(jnp.bfloat16)
+
+    def plane(m, carry):
+        list_copy(m).wait()
+        chunk(2 * m)
+        chunk(2 * m + 1)
         return carry
 
-    for m in range(planes):
-        list_copy(m).wait()
-    lax.fori_loop(0, 2 * planes, chunk, 0)
-
-
-def gather(quarter, lists, tab, planes, unroll=4):
+    lax.fori_loop(0, planes, plane, 0)
+
+
+def gather(quarter, lists, table, planes, unroll=4, widen=False):
+    vmem = pl.BlockSpec(memory_space=pltpu.VMEM)
+    sums = pltpu.VMEM((2 * planes, CHUNK, E), jnp.bfloat16)
+    scratch = [
+        pltpu.SMEM((2 * planes * SLOTS,), jnp.int32),
+        pltpu.VMEM((CHUNK + 8, E), jnp.float32),
+        pltpu.SemaphoreType.DMA((planes,)),
+    ]
+    if widen:
+        table = pltpu.with_memory_space_constraint(table, pltpu.HBM)
+        scratch = [pltpu.VMEM((TSLOTS, TBLK, E), jnp.bfloat16), pltpu.SemaphoreType.DMA((TSLOTS,))] + scratch
     return pl.pallas_call(
-        functools.partial(gather_body, unroll=unroll),
-        out_shape=pltpu.VMEM((2 * planes, CHUNK, E), jnp.bfloat16),
+        functools.partial(gather_body, unroll=unroll, widen=widen),
+        out_shape=(sums, pltpu.VMEM((ROWS_DEV + 8, E), jnp.float32)) if widen else sums,
         in_specs=[
             pl.BlockSpec(memory_space=pltpu.SMEM),
             pl.BlockSpec(memory_space=pl.ANY),
-            pl.BlockSpec(memory_space=pltpu.VMEM),
+            pl.BlockSpec(memory_space=pltpu.HBM) if widen else vmem,
         ],
-        out_specs=pl.BlockSpec(memory_space=pltpu.VMEM),
-        scratch_shapes=[
-            pltpu.SMEM((2 * planes * SLOTS,), jnp.int32),
-            pltpu.VMEM((CHUNK + 8, E), jnp.float32),
-            pltpu.SemaphoreType.DMA((planes,)),
-        ],
-        compiler_params=pltpu.CompilerParams(vmem_limit_bytes=4 * 2**20),
+        out_specs=(vmem, vmem) if widen else vmem,
+        scratch_shapes=scratch,
+        compiler_params=pltpu.CompilerParams(vmem_limit_bytes=(6 if widen else 4) * 2**20),
         name="bag_gather",
-    )(quarter, lists, tab)
+    )(quarter, lists, table)
 
 
 def combine_body(y_ref, lists_ref, part_0, part_1, part_2, part_3, out_ref):
@@ -287,11 +287,14 @@
     arrived = lax.all_to_all(lists.reshape(n_sec * n_dev, 4, 128), both_axes, 0, 0, tiled=True)
     line = lax.broadcasted_iota(jnp.int32, arrived.shape, 1)
     clean = jnp.where(line < 2, arrived, arrived & 0xFFFFF).reshape(-1)
-    tab = widen(tables)
+    clean, tables = lax.optimization_barrier((clean, tables))
     parts = {}
     for k in (2, 1, 3, 0):
         quarter = ((y + k) % ring).reshape(1)
-        sums = gather(quarter, clean, tab, planes)
+        if k == 2:
+            sums, tab = gather(quarter, clean, tables, planes, widen=True)
+        else:
+            sums = gather(quarter, clean, tab, planes)
         parts[k] = along(sums, k) if k else sums
     pooled = combine(y.reshape(1), arrived, [parts[k] for k in range(ring)])
     pooled = pooled.reshape(planes, 2 * CHUNK, E)
@@ -309,13 +312,15 @@
         hidden = jnp.maximum(pre_act + bias[None, :], 0.0)
         return jnp.sum(hidden * scale[None, :], axis=1)
 
-    near_part = logits_of(features)
-    far, near_part = lax.optimization_barrier((far, near_part))
+    near = lax.all_gather(logits_of(features), "section").sum(0)
+    far, near = lax.optimization_barrier((far, near))
     far_part = logits_of(far)
-    by_chip = jnp.stack([jnp.where(q == 0, near_part, far_part), jnp.where(q == 0, far_part, near_part)])
-    quads = [[s * n_dev + 2 * p + i for s in range(n_sec) for i in range(2)] for p in range(n_dev // 2)]
-    quarters = lax.all_gather(by_chip, both_axes, axis_index_groups=quads)
-    return lax.dynamic_index_in_dim(quarters.sum(0), q, 0, False)
+
+    def to_partner(x, turn):
+        pairs = [(s * n_dev + d, (s ^ turn) * n_dev + (d ^ 1)) for s in range(n_sec) for d in range(n_dev)]
+        return lax.ppermute(x, both_axes, pairs)
+
+    return near + (to_partner(far_part, 0) + to_partner(far_part, 1))
 
 
 def solution(mesh):

time: 144 us -> 139 us (0.965)
  waiting for transfers between devices: 17.5 us -> 30.5 us
  local copies, waits for them, and re-layouts: 13.5 us -> 1.26 us
  starting transfers between devices: 40.5 us -> 34.9 us
  matrix products: 7.91 us -> 12 us
  blocking collectives: 17.8 us -> 14.1 us
    unnamed x12 -> x4, local copies, waits for them, and re-layouts: 11.7 us -> 0.01 us
    all_to_all x1, waiting for transfers between devices: 0.01 us -> 10.7 us  [body(): lax.all_to_all(lists.reshape(n_sec * n_dev, 4, 128), both_axes, 0, 0, til...]
    all_to_all x1, starting transfers between devices: 16.6 us -> 9.76 us  [body(): lax.all_to_all(pooled, 'dev', 0, 0, axis_index_groups=levels, tiled=True)]
    all_gather x1, blocking collectives: 5.51 us -> 1.83 us  [body(): near = lax.all_gather(logits_of(features), 'section').sum(0)]
    ppermute x0 -> x2, starting transfers between devices: none -> 2.08 us  [to_partner(): return lax.ppermute(x, both_axes, pairs)]
    dot_general x2, matrix products: 4.1 us -> 6.16 us  [logits_of(): jnp.dot(both[0], whole[:k_half], preferred_element_type=jnp.float32)]
    dot_general x2, matrix products: 3.81 us -> 5.86 us  [logits_of(): jnp.dot(both[1], whole[k_half:], preferred_element_type=jnp.float32)]
    pallas_call x5 -> x4, Pallas kernels: 26 us -> 25.3 us  [gather(): pl.pallas_call(functools.partial(gather_body, unroll=unroll, widen=widen)...]
  transfers between devices with their start and end apart: 10 -> 12, of which waited for: 4 -> 7; matrix products, arithmetic and copies ran while one was open for 5% -> 5% of each run, Pallas kernels for 22% -> 22%
where the time goes in v6:
time: 139 us; the launch traced here: 138 us
  starting transfers between devices  34.9 us (25%)
  waiting for transfers between devices  30.5 us (22%)
  Pallas kernels  30.4 us (22%)
  blocking collectives  14.1 us (10%)
  between operations  13.6 us (10%)
  matrix products  12 us (9%)
  other arithmetic  1.6 us (1%)
    pallas_call x4, Pallas kernels, gather(): pl.pallas_call(functools.partial(gather_body, unroll=unroll, widen=widen)...  25.3 us
    all_to_all x2, blocking collectives, swap(): lax.all_to_all(jnp.broadcast_to(x[None], (2, *x.shape)), axis, 0, 0, tile...  12.3 us
    all_to_all x1, starting transfers between devices, body(): lax.all_to_all(lists.reshape(n_sec * n_dev, 4, 128), both_axes, 0, 0, til...  10.9 us
    all_to_all x1, waiting for transfers between devices, body(): lax.all_to_all(lists.reshape(n_sec * n_dev, 4, 128), both_axes, 0, 0, til...  10.7 us
    all_to_all x1, starting transfers between devices, body(): lax.all_to_all(pooled, 'dev', 0, 0, axis_index_groups=levels, tiled=True)  9.76 us
    ppermute x6, starting transfers between devices, along(): lax.ppermute(x, 'dev', [(d, d // ring * ring + (d + k) % ring) for d in r...  9.64 us
    ppermute x6, waiting for transfers between devices, along(): lax.ppermute(x, 'dev', [(d, d // ring * ring + (d + k) % ring) for d in r...  9.5 us
    all_to_all x1, waiting for transfers between devices, body(): lax.all_to_all(pooled, 'dev', 0, 0, axis_index_groups=levels, tiled=True)  8.91 us
  transfers between devices with their start and end apart: 12, of which 7 were waited for; matrix products, arithmetic and copies ran while one was open for 5% of the time, Pallas kernels for 22%

profile of v6, /device:TPU:1, one launch (start us, length us, event | category | flops | bytes accessed | tf_op | source)
XLA Modules:
  0.0 138.3 jit_solution(7198729377199011015)
XLA Ops:
  7.5 2.2 %collective-permute-start = (bf16[64,1024]{1,0:T(8,128)(2,1)S(1)}, bf16[64,1024]{1,0:T(8,128)(2,1)S(1)}, u32[]{:S(2)}, u32[]{:S(2)}) collective-permute-start(bf16[64,1024]{1,0:T(8,128)(2,1)S(1)} %get-tuple-element.31), channel_id=1, source_target_pairs={{0,1},{1,2},{2,3},{3,0},{4,5},{5,6},{6,7},{7,4},{8,9},{9,10},{10,1... | collective-permute-start | bytes 393224 | tf_op jit(solution)/shard_map/ppermute | solution.py:279
  9.7 2.6 %collective-permute-start.1 = (bf16[64,1024]{1,0:T(8,128)(2,1)S(1)}, bf16[64,1024]{1,0:T(8,128)(2,1)S(1)}, u32[]{:S(2)}, u32[]{:S(2)}) collective-permute-start(bf16[64,1024]{1,0:T(8,128)(2,1)S(1)} %get-tuple-element.21), channel_id=1, source_target_pairs={{0,2},{1,3},{2,0},{3,1},{4,6},{5,7},{6,4},{7,5},{8,10},{9,11},{10,... | collective-permute-start | bytes 393224 | tf_op jit(solution)/shard_map/ppermute | solution.py:279
  13.4 3.2 %bag_lists.1 = s32[512,128]{1,0:T(8,128)} custom-call(s32[32,8,64]{2,1,0:T(8,128)} %bitcast.39, s32[32]{0:T(128)} %pool_ref.1), custom_call_target="tpu_custom_call" | custom-call | tf_op jit(solution)/shard_map/bag_lists/pallas_call | solution.py:103
  19.1 10.9 %all-to-all-start = ((s32[128,4,128]{2,1,0:T(4,128)}), s32[128,4,128]{2,1,0:T(4,128)S(1)}, u32[]{:S(2)}, u32[]{:S(2)}) async-start(s32[128,4,128]{2,1,0:T(4,128)} %bitcast.2), calls=%async_computation | async-start | bytes 524288 | tf_op jit(solution)/shard_map/all_to_all | solution.py:287
  30.1 10.7 %all-to-all-done.lists_ref = s32[128,4,128]{2,1,0:T(4,128)S(1)} async-done(((s32[128,4,128]{2,1,0:T(4,128)}), s32[128,4,128]{2,1,0:T(4,128)S(1)}, u32[]{:S(2)}, u32[]{:S(2)}) %all-to-all-start) | async-done | bytes 262176 | tf_op jit(solution)/shard_map/all_to_all | solution.py:287
  40.9 9.8 %bag_gather.4 = (bf16[32,64,128]{2,1,0:T(8,128)(2,1)S(1)}, f32[32776,128]{1,0:T(8,128)S(1)}) custom-call(s32[1]{0:T(128)} %bitcast.5.quarter_ref, s32[65536]{0:T(1024)S(1)} %bitcast.34, bf16[32768,128]{1,0:T(8,128)(2,1)} %refs_0_), custom_call_target="tpu_custom_call" | custom-call | tf_op jit(solution)/shard_map/bag_gather/pallas_call | solution.py:191
  50.7 5.3 %bag_gather.6 = bf16[32,64,128]{2,1,0:T(8,128)(2,1)S(1)} custom-call(s32[1]{0:T(128)} %bitcast.6.quarter_ref, s32[65536]{0:T(1024)S(1)} %bitcast.35, f32[32776,128]{1,0:T(8,128)S(1)} %get-tuple-element.19.refs_0_), custom_call_target="tpu_custom_call" | custom-call | tf_op jit(solution)/shard_map/bag_gather/pallas_call | solution.py:191
  56.4 1.7 %collective-permute-start.4 = (bf16[32,64,128]{2,1,0:T(8,128)(2,1)S(1)}, bf16[32,64,128]{2,1,0:T(8,128)(2,1)S(1)}, u32[]{:S(2)}, u32[]{:S(2)}) collective-permute-start(bf16[32,64,128]{2,1,0:T(8,128)(2,1)S(1)} %get-tuple-element.20), channel_id=1, source_target_pairs={{0,2},{1,3},{2,0},{3,1},{4,6},{5,7},{6,4},{7,5},{8,10},{9,11},{10,... | collective-permute-start | bytes 1572872 | tf_op jit(solution)/shard_map/ppermute | solution.py:279
  58.2 5.1 %bag_gather.7 = bf16[32,64,128]{2,1,0:T(8,128)(2,1)S(1)} custom-call(s32[1]{0:T(128)} %bitcast.7.quarter_ref, s32[65536]{0:T(1024)S(1)} %bitcast.36, f32[32776,128]{1,0:T(8,128)S(1)} %get-tuple-element.19.refs_0_), custom_call_target="tpu_custom_call" | custom-call | tf_op jit(solution)/shard_map/bag_gather/pallas_call | solution.py:191
  63.3 1.6 %collective-permute-start.5 = (bf16[32,64,128]{2,1,0:T(8,128)(2,1)S(1)}, bf16[32,64,128]{2,1,0:T(8,128)(2,1)S(1)}, u32[]{:S(2)}, u32[]{:S(2)}) collective-permute-start(bf16[32,64,128]{2,1,0:T(8,128)(2,1)S(1)} %bag_gather.7), channel_id=1, source_target_pairs={{0,3},{1,0},{2,1},{3,2},{4,7},{5,4},{6,5},{7,6},{8,11},{9,8},{10,9... | collective-permute-start | bytes 1572872 | tf_op jit(solution)/shard_map/ppermute | solution.py:279
  64.9 5.1 %bag_gather.5.part_0 = bf16[32,64,128]{2,1,0:T(8,128)(2,1)S(1)} custom-call(s32[1]{0:T(128)} %bitcast.3.quarter_ref, s32[65536]{0:T(1024)S(1)} %bitcast.37, f32[32776,128]{1,0:T(8,128)S(1)} %get-tuple-element.19.refs_0_), custom_call_target="tpu_custom_call" | custom-call | tf_op jit(solution)/shard_map/bag_gather/pallas_call | solution.py:191
  70.0 6.5 %collective-permute-done.4.part_2 = bf16[32,64,128]{2,1,0:T(8,128)(2,1)S(1)} collective-permute-done((bf16[32,64,128]{2,1,0:T(8,128)(2,1)S(1)}, bf16[32,64,128]{2,1,0:T(8,128)(2,1)S(1)}, u32[]{:S(2)}, u32[]{:S(2)}) %collective-permute-start.4) | collective-permute-done | bytes 524320 | tf_op jit(solution)/shard_map/ppermute | solution.py:279
  78.1 1.7 %bag_combine.1 = bf16[32,64,128]{2,1,0:T(8,128)(2,1)} custom-call(s32[1]{0:T(128)} %bitcast.y_ref, s32[128,4,128]{2,1,0:T(4,128)S(1)} %all-to-all-done.lists_ref, bf16[32,64,128]{2,1,0:T(8,128)(2,1)S(1)} %bag_gather.5.part_0, bf16[32,64,128]{2,1,0:T(8,128)(2,1)S(1)} %collective-permute-done.3.part_1, bf16[32,64,128]{2,1,0:T(8,128)(2,1)S(1)} %collective-permute-done.4.part_2, ...), custom_call_target="tpu_custom_call" | custom-call | tf_op jit(solution)/shard_map/bag_combine/pallas_call | solution.py:228
  79.8 9.8 %all-to-all-start.1 = ((bf16[16,128,128]{2,1,0:T(8,128)(2,1)}), bf16[16,128,128]{2,1,0:T(8,128)(2,1)S(1)}, u32[]{:S(2)}, u32[]{:S(2)}) async-start(bf16[16,128,128]{2,1,0:T(8,128)(2,1)} %bitcast.8), calls=%async_computation.1 | async-start | bytes 1048576 | tf_op jit(solution)/shard_map/all_to_all | solution.py:301
  89.6 8.9 %all-to-all-done.1.pooled_ref = bf16[16,128,128]{2,1,0:T(8,128)(2,1)S(1)} async-done(((bf16[16,128,128]{2,1,0:T(8,128)(2,1)}), bf16[16,128,128]{2,1,0:T(8,128)(2,1)S(1)}, u32[]{:S(2)}, u32[]{:S(2)}) %all-to-all-start.1) | async-done | bytes 524320 | tf_op jit(solution)/shard_map/all_to_all | solution.py:301
  98.6 2.5 %collective-permute-start.6 = (bf16[128,2048]{1,0:T(8,128)(2,1)S(1)}, bf16[128,2048]{1,0:T(8,128)(2,1)S(1)}, u32[]{:S(2)}, u32[]{:S(2)}) collective-permute-start(bf16[128,2048]{1,0:T(8,128)(2,1)S(1)} %feature_rows.1), channel_id=1, source_target_pairs={{0,1},{1,0},{2,3},{3,2},{4,5},{5,4},{6,7},{7,6},{8,9},{9,8},{10,11... | collective-permute-start | bytes 1572872 | tf_op jit(solution)/shard_map/ppermute | solution.py:305
  101.2 7.7 %all_to_all.20 = bf16[2,128,2048]{2,1,0:T(8,128)(2,1)S(1)} all-to-all(bf16[2,128,2048]{2,1,0:T(8,128)(2,1)S(1)} %broadcast_in_dim.4), channel_id=1, replica_groups=mesh['section'=2,'dev'=64] {'section'}, dimensions={0} | all-to-all | bytes 2097152 | tf_op jit(solution)/shard_map/all_to_all | solution.py:257
  108.9 2.9 %fusion.2 = f32[128,1024]{1,0:T(8,128)S(1)} fusion(bf16[4096,1024]{1,0:T(8,128)(2,1)} %all-gather.4.cloned.1.call-done, bf16[2,128,2048]{2,1,0:T(8,128)(2,1)S(1)} %all_to_all.20), kind=kOutput, calls=%fused_computation.2 | convolution fusion | flops 536870912 | bytes 5242880 | tf_op jit(solution)/shard_map/dot_general | solution.py:311
  111.9 3.1 %fusion.32 = f32[128]{0:T(128)S(1)} fusion(f32[128,1024]{1,0:T(8,128)S(1)} %fusion.2, bf16[4096,1024]{1,0:T(8,128)(2,1)} %all-gather.4.cloned.1.call-done, bf16[2,128,2048]{2,1,0:T(8,128)(2,1)S(1)} %all_to_all.20, f32[1024]{0:T(1024)S(1)} %get-tuple-element.33, f32[1024]{0:T(1024)S(1)} %get-tuple-element.34), kind=kOutput, calls=%fused_computation.16 | convolution fusion | flops 537526144 | bytes 5251584 | tf_op jit(solution)/shard_map/dot_general | solution.py:310
  115.0 1.8 %all-gather.1 = f32[2,1,128]{2,1,0:T(1,128)S(1)} all-gather(f32[1,1,128]{2,1,0:T(1,128)S(1)} %bitcast.43), channel_id=2, replica_groups=mesh['section'=2,'dev'=64] {'section'}, dimensions={0}, use_global_device_ids=true | all-gather | bytes 1536 | tf_op jit(solution)/shard_map/all_gather | solution.py:315
  116.9 4.5 %all_to_all.21 = bf16[2,128,2048]{2,1,0:T(8,128)(2,1)S(1)} all-to-all(bf16[2,128,2048]{2,1,0:T(8,128)(2,1)S(1)} %broadcast_in_dim.5), channel_id=1, replica_groups=mesh['section'=2,'dev'=64] {'section'}, dimensions={0} | all-to-all | bytes 2097152 | tf_op jit(solution)/shard_map/all_to_all | solution.py:257
  121.5 2.9 %fusion = f32[128,1024]{1,0:T(8,128)S(1)} fusion(bf16[4096,1024]{1,0:T(8,128)(2,1)} %all-gather.4.cloned.1.call-done, bf16[2,128,2048]{2,1,0:T(8,128)(2,1)S(1)} %all_to_all.21), kind=kOutput, calls=%fused_computation | convolution fusion | flops 536870912 | bytes 5242880 | tf_op jit(solution)/shard_map/dot_general | solution.py:311
  124.4 3.1 %fusion.35 = f32[128]{0:T(128)S(1)} fusion(f32[128,1024]{1,0:T(8,128)S(1)} %fusion, bf16[4096,1024]{1,0:T(8,128)(2,1)} %all-gather.4.cloned.1.call-done, bf16[2,128,2048]{2,1,0:T(8,128)(2,1)S(1)} %all_to_all.21, f32[1024]{0:T(1024)S(1)} %get-tuple-element.33, f32[1024]{0:T(1024)S(1)} %get-tuple-element.34), kind=kOutput, calls=%fused_computation.17 | convolution fusion | flops 537526144 | bytes 5251584 | tf_op jit(solution)/shard_map/dot_general | solution.py:310
  127.9 1.7 %collective-permute-start.8 = (f32[128]{0:T(128)S(1)}, f32[128]{0:T(128)S(1)}, u32[]{:S(2)}, u32[]{:S(2)}) collective-permute-start(f32[128]{0:T(128)S(1)} %fusion.35), channel_id=1, source_target_pairs={{0,65},{1,64},{2,67},{3,66},{4,69},{5,68},{6,71},{7,70},{8,73},{9,... | collective-permute-start | bytes 1544 | tf_op jit(solution)/shard_map/ppermute | solution.py:321
  (30 shorter events, 9.3 us)
Async XLA Ops:
  6.5 102.4 %all-gather.4.cloned.1.call-start = ((), (), s32[]{:S(2)}) async-start(), calls=%async_computation.4 | async-start | bytes 8912896 | tf_op jit(solution)/shard_map/all_gather | solution.py:285
  7.5 9.1 %collective-permute-start = (bf16[64,1024]{1,0:T(8,128)(2,1)S(1)}, bf16[64,1024]{1,0:T(8,128)(2,1)S(1)}, u32[]{:S(2)}, u32[]{:S(2)}) collective-permute-start(bf16[64,1024]{1,0:T(8,128)(2,1)S(1)} %get-tuple-element.31), channel_id=1, source_target_pairs={{0,1},{1,2},{2,3},{3,0},{4,5},{5,6},{6,7},{7,4},{8,9},{9,10},{10,1... | collective-permute-start | bytes 393224 | tf_op jit(solution)/shard_map/ppermute | solution.py:279
  9.7 8.3 %collective-permute-start.1 = (bf16[64,1024]{1,0:T(8,128)(2,1)S(1)}, bf16[64,1024]{1,0:T(8,128)(2,1)S(1)}, u32[]{:S(2)}, u32[]{:S(2)}) collective-permute-start(bf16[64,1024]{1,0:T(8,128)(2,1)S(1)} %get-tuple-element.21), channel_id=1, source_target_pairs={{0,2},{1,3},{2,0},{3,1},{4,6},{5,7},{6,4},{7,5},{8,10},{9,11},{10,... | collective-permute-start | bytes 393224 | tf_op jit(solution)/shard_map/ppermute | solution.py:279
  12.3 5.7 %collective-permute-start.2 = (bf16[64,1024]{1,0:T(8,128)(2,1)S(1)}, bf16[64,1024]{1,0:T(8,128)(2,1)S(1)}, u32[]{:S(2)}, u32[]{:S(2)}) collective-permute-start(bf16[64,1024]{1,0:T(8,128)(2,1)S(1)} %get-tuple-element.31), channel_id=1, source_target_pairs={{0,3},{1,0},{2,1},{3,2},{4,7},{5,4},{6,5},{7,6},{8,11},{9,8},{10,9... | collective-permute-start | bytes 393224 | tf_op jit(solution)/shard_map/ppermute | solution.py:279
  19.1 21.7 %all-to-all-start = ((s32[128,4,128]{2,1,0:T(4,128)}), s32[128,4,128]{2,1,0:T(4,128)S(1)}, u32[]{:S(2)}, u32[]{:S(2)}) async-start(s32[128,4,128]{2,1,0:T(4,128)} %bitcast.2), calls=%async_computation | async-start | bytes 524288 | tf_op jit(solution)/shard_map/all_to_all | solution.py:287
  56.0 14.1 %collective-permute-start.3 = (bf16[32,64,128]{2,1,0:T(8,128)(2,1)S(1)}, bf16[32,64,128]{2,1,0:T(8,128)(2,1)S(1)}, u32[]{:S(2)}, u32[]{:S(2)}) collective-permute-start(bf16[32,64,128]{2,1,0:T(8,128)(2,1)S(1)} %bag_gather.6), channel_id=1, source_target_pairs={{0,1},{1,2},{2,3},{3,0},{4,5},{5,6},{6,7},{7,4},{8,9},{9,10},{10,1... | collective-permute-start | bytes 1572872 | tf_op jit(solution)/shard_map/ppermute | solution.py:279
  56.4 20.1 %collective-permute-start.4 = (bf16[32,64,128]{2,1,0:T(8,128)(2,1)S(1)}, bf16[32,64,128]{2,1,0:T(8,128)(2,1)S(1)}, u32[]{:S(2)}, u32[]{:S(2)}) collective-permute-start(bf16[32,64,128]{2,1,0:T(8,128)(2,1)S(1)} %get-tuple-element.20), channel_id=1, source_target_pairs={{0,2},{1,3},{2,0},{3,1},{4,6},{5,7},{6,4},{7,5},{8,10},{9,11},{10,... | collective-permute-start | bytes 1572872 | tf_op jit(solution)/shard_map/ppermute | solution.py:279
  63.3 14.8 %collective-permute-start.5 = (bf16[32,64,128]{2,1,0:T(8,128)(2,1)S(1)}, bf16[32,64,128]{2,1,0:T(8,128)(2,1)S(1)}, u32[]{:S(2)}, u32[]{:S(2)}) collective-permute-start(bf16[32,64,128]{2,1,0:T(8,128)(2,1)S(1)} %bag_gather.7), channel_id=1, source_target_pairs={{0,3},{1,0},{2,1},{3,2},{4,7},{5,4},{6,5},{7,6},{8,11},{9,8},{10,9... | collective-permute-start | bytes 1572872 | tf_op jit(solution)/shard_map/ppermute | solution.py:279
  64.9 24.7 %copy-start = (bf16[2048]{0:T(1024)(128)(2,1)S(1)}, bf16[2048]{0:T(1024)(128)(2,1)}, u32[]{:S(2)}) copy-start(bf16[2048]{0:T(1024)(128)(2,1)} %param.11) | copy-start | bytes 12292
  64.9 24.7 %copy-start.1 = (bf16[2048]{0:T(1024)(128)(2,1)S(1)}, bf16[2048]{0:T(1024)(128)(2,1)}, u32[]{:S(2)}) copy-start(bf16[2048]{0:T(1024)(128)(2,1)} %param.10) | copy-start | bytes 12292
  79.8 18.7 %all-to-all-start.1 = ((bf16[16,128,128]{2,1,0:T(8,128)(2,1)}), bf16[16,128,128]{2,1,0:T(8,128)(2,1)S(1)}, u32[]{:S(2)}, u32[]{:S(2)}) async-start(bf16[16,128,128]{2,1,0:T(8,128)(2,1)} %bitcast.8), calls=%async_computation.1 | async-start | bytes 1048576 | tf_op jit(solution)/shard_map/all_to_all | solution.py:301
  98.6 18.2 %collective-permute-start.6 = (bf16[128,2048]{1,0:T(8,128)(2,1)S(1)}, bf16[128,2048]{1,0:T(8,128)(2,1)S(1)}, u32[]{:S(2)}, u32[]{:S(2)}) collective-permute-start(bf16[128,2048]{1,0:T(8,128)(2,1)S(1)} %feature_rows.1), channel_id=1, source_target_pairs={{0,1},{1,0},{2,3},{3,2},{4,5},{5,4},{6,7},{7,6},{8,9},{9,8},{10,11... | collective-permute-start | bytes 1572872 | tf_op jit(solution)/shard_map/ppermute | solution.py:305
  127.5 2.5 %collective-permute-start.7 = (f32[128]{0:T(128)S(1)}, f32[128]{0:T(128)S(1)}, u32[]{:S(2)}, u32[]{:S(2)}) collective-permute-start(f32[128]{0:T(128)S(1)} %fusion.35), channel_id=1, source_target_pairs={{0,1},{1,0},{2,3},{3,2},{4,5},{5,4},{6,7},{7,6},{8,9},{9,8},{10,11... | collective-permute-start | bytes 1544 | tf_op jit(solution)/shard_map/ppermute | solution.py:321
  127.9 3.0 %collective-permute-start.8 = (f32[128]{0:T(128)S(1)}, f32[128]{0:T(128)S(1)}, u32[]{:S(2)}, u32[]{:S(2)}) collective-permute-start(f32[128]{0:T(128)S(1)} %fusion.35), channel_id=1, source_target_pairs={{0,65},{1,64},{2,67},{3,66},{4,69},{5,68},{6,71},{7,70},{8,73},{9,... | collective-permute-start | bytes 1544 | tf_op jit(solution)/shard_map/ppermute | solution.py:321
Sparse Core Ops, SparseCore 0:
  19.2 73.7 all-gather.3

commit v7 on v6

--- a/solution.py
+++ b/solution.py
@@ -6,6 +6,7 @@
 from jax.experimental import pallas as pl
 from jax.experimental.pallas import tpu as pltpu
 from jax.sharding import PartitionSpec as P
+
 
 E = 128
 ROWS_DEV = 32768
@@ -16,6 +17,7 @@
 TBLK = 2048
 TSLOTS = 4
 HID_SPLIT = 2
+WBLK = 512
 SORT8 = (
     (0, 2), (1, 3), (4, 6), (5, 7), (0, 4), (1, 5), (2, 6), (3, 7), (0, 1), (2, 3),
     (4, 5), (6, 7), (2, 4), (3, 5), (1, 4), (3, 6), (1, 2), (3, 4), (5, 6),
@@ -253,6 +255,50 @@
     )(pltpu.with_memory_space_constraint(pooled, pltpu.VMEM))
 
 
+def dense_body(both_ref, w_ref, bias_ref, scale_ref, *refs, stream):
+    if stream:
+        out_ref, kept, acc, sem = refs
+        blocks = [pl.ds(b * WBLK, WBLK) for b in range(kept.shape[0] // WBLK)]
+        copies = [pltpu.make_async_copy(w_ref.at[b], kept.at[b], sem.at[i]) for i, b in enumerate(blocks)]
+        for copy in copies:
+            copy.start()
+    else:
+        out_ref, acc = refs
+        kept = w_ref
+        blocks = [pl.ds(b * WBLK, WBLK) for b in range(kept.shape[0] // WBLK)]
+    wide = both_ref.shape[2]
+    for i, block in enumerate(blocks):
+        if stream:
+            copies[i].wait()
+        at = i * WBLK
+        x = both_ref[at // wide, :, at % wide : at % wide + WBLK]
+        prod = jnp.dot(x, kept[block, :], preferred_element_type=jnp.float32)
+        acc[...] = prod if i == 0 else acc[...] + prod
+    part = jnp.maximum(acc[...] + bias_ref[...], 0.0) * scale_ref[...]
+    lanes = sum(part[:, 128 * i : 128 * i + 128] for i in range(part.shape[1] // 128))
+    out_ref[...] = jnp.sum(lanes.T, axis=0, keepdims=True)
+
+
+def dense(both, weights, bias, scale, stream):
+    vmem = pl.BlockSpec(memory_space=pltpu.VMEM)
+    samples = both.shape[1]
+    rows, units = weights.shape
+    out = pltpu.VMEM((1, samples), jnp.float32)
+    scratch = [pltpu.VMEM((samples, units), jnp.float32)]
+    if stream:
+        weights = pltpu.with_memory_space_constraint(weights, pltpu.HBM)
+        scratch.append(pltpu.SemaphoreType.DMA((rows // WBLK,)))
+    return pl.pallas_call(
+        functools.partial(dense_body, stream=stream),
+        out_shape=(out, pltpu.VMEM(weights.shape, weights.dtype)) if stream else out,
+        in_specs=[vmem, pl.BlockSpec(memory_space=pltpu.HBM) if stream else vmem, vmem, vmem],
+        out_specs=(vmem, vmem) if stream else vmem,
+        scratch_shapes=scratch,
+        compiler_params=pltpu.CompilerParams(vmem_limit_bytes=8 * 2**20),
+        name="dense_near" if stream else "dense_far",
+    )(pltpu.with_memory_space_constraint(both, pltpu.VMEM), weights, bias, scale)
+
+
 def swap(x, axis):
     return lax.all_to_all(jnp.broadcast_to(x[None], (2, *x.shape)), axis, 0, 0, tiled=True)
 
@@ -260,9 +306,6 @@
 def body(indices, pool_len, tables, w_first, b_first, w_out):
     n_dev = lax.axis_size("dev")
     n_sec = lax.axis_size("section")
-    n_tables = indices.shape[1]
-    half = n_tables // n_sec
-    section = lax.axis_index("section")
     dev = lax.axis_index("dev")
     lists = prep(jnp.transpose(indices, (1, 2, 0)), pool_len)
     ring = 4
@@ -279,7 +322,6 @@
         return lax.ppermute(x, "dev", [(d, d // ring * ring + (d + k) % ring) for d in range(n_dev)])
 
     pieces = [keep, along(give, 1), along(keep, 2), along(give, 3)]
-    pieces, lists = lax.optimization_barrier((pieces, lists))
     pieces = jnp.stack(pieces)
     pieces = [lax.dynamic_index_in_dim(pieces, (y - k) % ring, 0, False) for k in range(ring)]
     whole = lax.all_gather(jnp.concatenate(pieces), "dev", axis_index_groups=levels, tiled=True)
@@ -303,24 +345,18 @@
     bias = lax.dynamic_slice(b_first, (q * part,), (part,)).astype(jnp.float32)
     scale = lax.dynamic_slice(w_out, (q * part,), (part,)).astype(jnp.float32)
     far = lax.ppermute(features, "dev", [(d, d ^ 1) for d in range(n_dev)])
-    k_half = half * E
-
-    def logits_of(mine):
-        both = swap(mine, "section")
-        pre_act = jnp.dot(both[0], whole[:k_half], preferred_element_type=jnp.float32)
-        pre_act += jnp.dot(both[1], whole[k_half:], preferred_element_type=jnp.float32)
-        hidden = jnp.maximum(pre_act + bias[None, :], 0.0)
-        return jnp.sum(hidden * scale[None, :], axis=1)
-
-    near = lax.all_gather(logits_of(features), "section").sum(0)
+    bias, scale = bias.reshape(1, part), scale.reshape(1, part)
+    near, kept = dense(swap(features, "section"), whole, bias, scale, True)
+    near = lax.all_gather(near.reshape(-1), "section")
     far, near = lax.optimization_barrier((far, near))
-    far_part = logits_of(far)
+    far_part = dense(swap(far, "section"), kept, bias, scale, False).reshape(-1)
+    far_part, near = lax.optimization_barrier((far_part, near))
 
     def to_partner(x, turn):
         pairs = [(s * n_dev + d, (s ^ turn) * n_dev + (d ^ 1)) for s in range(n_sec) for d in range(n_dev)]
         return lax.ppermute(x, both_axes, pairs)
 
-    return near + (to_partner(far_part, 0) + to_partner(far_part, 1))
+    return (near[0] + near[1]) + (to_partner(far_part, 0) + to_partner(far_part, 1))
 
 
 def solution(mesh):

time: 139 us -> 140 us (level)
  starting transfers between devices: 34.9 us -> 18.1 us
  blocking collectives: 14.1 us -> 30.7 us
  Pallas kernels: 30.4 us -> 43.5 us
  matrix products: 12 us -> 0 us
    all_to_all x0 -> x1, blocking collectives: none -> 18.4 us  [body(): lax.all_to_all(pooled, 'dev', 0, 0, axis_index_groups=levels, tiled=True)]
    dot_general x4 -> x0, matrix products: 12 us -> none  [the longest x2 6.16 us: logits_of(): jnp.dot(both[0], whole[:k_half], preferred_element_type=jnp.float32)]
    all_to_all x1 -> x0, starting transfers between devices: 9.76 us -> none  [body(): lax.all_to_all(pooled, 'dev', 0, 0, axis_index_groups=levels, tiled=True)]
    all_to_all x1 -> x0, waiting for transfers between devices: 8.91 us -> none  [body(): lax.all_to_all(pooled, 'dev', 0, 0, axis_index_groups=levels, tiled=True)]
    pallas_call x4, Pallas kernels: 25.3 us -> 34.1 us  [gather(): pl.pallas_call(functools.partial(gather_body, unroll=unroll, widen=widen)...]
    ppermute x6, waiting for transfers between devices: 9.5 us -> 15.3 us  [along(): lax.ppermute(x, 'dev', [(d, d // ring * ring + (d + k) % ring) for d in r...]
    pallas_call x0 -> x2, Pallas kernels: none -> 5.23 us  [dense(): pl.pallas_call(functools.partial(dense_body, stream=stream), out_shape=(o...]
    all_to_all x1, starting transfers between devices: 10.9 us -> 8 us  [body(): lax.all_to_all(lists.reshape(n_sec * n_dev, 4, 128), both_axes, 0, 0, til...]
  transfers between devices with their start and end apart: 12 -> 11, of which waited for: 7 -> 9; matrix products, arithmetic and copies ran while one was open for 5% -> 0% of each run, Pallas kernels for 22% -> 30%
where the time goes in v7:
time: 140 us; the launch traced here: 139 us
  Pallas kernels  43.5 us (31%)
  blocking collectives  30.7 us (22%)
  waiting for transfers between devices  30.6 us (22%)
  starting transfers between devices  18.1 us (13%)
  between operations  13.6 us (10%)
  other arithmetic  1.61 us (1%)
    pallas_call x4, Pallas kernels, gather(): pl.pallas_call(functools.partial(gather_body, unroll=unroll, widen=widen)...  34.1 us
    all_to_all x1, blocking collectives, body(): lax.all_to_all(pooled, 'dev', 0, 0, axis_index_groups=levels, tiled=True)  18.4 us
    ppermute x6, waiting for transfers between devices, along(): lax.ppermute(x, 'dev', [(d, d // ring * ring + (d + k) % ring) for d in r...  15.3 us
    all_to_all x1, waiting for transfers between devices, body(): lax.all_to_all(lists.reshape(n_sec * n_dev, 4, 128), both_axes, 0, 0, til...  11.9 us
    all_to_all x2, blocking collectives, swap(): lax.all_to_all(jnp.broadcast_to(x[None], (2, *x.shape)), axis, 0, 0, tile...  10.4 us
    all_to_all x1, starting transfers between devices, body(): lax.all_to_all(lists.reshape(n_sec * n_dev, 4, 128), both_axes, 0, 0, til...  8 us
    ppermute x6, starting transfers between devices, along(): lax.ppermute(x, 'dev', [(d, d // ring * ring + (d + k) % ring) for d in r...  7.91 us
    pallas_call x2, Pallas kernels, dense(): pl.pallas_call(functools.partial(dense_body, stream=stream), out_shape=(o...  5.23 us
  transfers between devices with their start and end apart: 11, of which 9 were waited for; matrix products, arithmetic and copies ran while one was open for 0% of the time, Pallas kernels for 30%

profile of v7, /device:TPU:1, one launch (start us, length us, event | category | flops | bytes accessed | tf_op | source)
XLA Modules:
  0.0 139.5 jit_solution(1186984485733932409)
XLA Ops:
  6.5 1.0 constant_dynamic-slice_fusion.1
  7.5 3.6 %collective-permute-start.6 = (bf16[64,1024]{1,0:T(8,128)(2,1)S(1)}, bf16[64,1024]{1,0:T(8,128)(2,1)S(1)}, u32[]{:S(2)}, u32[]{:S(2)}) collective-permute-start(bf16[64,1024]{1,0:T(8,128)(2,1)S(1)} %get-tuple-element.30), channel_id=1, source_target_pairs={{0,3},{1,0},{2,1},{3,2},{4,7},{5,4},{6,5},{7,6},{8,11},{9,8},{10,9... | collective-permute-start | bytes 393224 | tf_op jit(solution)/shard_map/ppermute | solution.py:322
  12.2 4.0 %collective-permute-done.6 = bf16[64,1024]{1,0:T(8,128)(2,1)S(1)} collective-permute-done((bf16[64,1024]{1,0:T(8,128)(2,1)S(1)}, bf16[64,1024]{1,0:T(8,128)(2,1)S(1)}, u32[]{:S(2)}, u32[]{:S(2)}) %collective-permute-start.6) | collective-permute-done | bytes 131104 | tf_op jit(solution)/shard_map/ppermute | solution.py:322
  16.6 4.2 %collective-permute-done.4 = bf16[64,1024]{1,0:T(8,128)(2,1)S(1)} collective-permute-done((bf16[64,1024]{1,0:T(8,128)(2,1)S(1)}, bf16[64,1024]{1,0:T(8,128)(2,1)S(1)}, u32[]{:S(2)}, u32[]{:S(2)}) %collective-permute-start.4) | collective-permute-done | bytes 131104 | tf_op jit(solution)/shard_map/ppermute | solution.py:322
  20.9 0.9 pad_maximum_fusion.1
  21.8 3.2 %bag_lists.1 = s32[512,128]{1,0:T(8,128)} custom-call(s32[32,8,64]{2,1,0:T(8,128)} %bitcast.41, s32[32]{0:T(128)} %pool_ref.1), custom_call_target="tpu_custom_call" | custom-call | tf_op jit(solution)/shard_map/bag_lists/pallas_call | solution.py:105
  25.0 8.0 %all-to-all-start = ((s32[128,4,128]{2,1,0:T(4,128)}), s32[128,4,128]{2,1,0:T(4,128)S(1)}, u32[]{:S(2)}, u32[]{:S(2)}) async-start(s32[128,4,128]{2,1,0:T(4,128)} %bitcast.2), calls=%async_computation | async-start | bytes 524288 | tf_op jit(solution)/shard_map/all_to_all | solution.py:329
  33.1 11.9 %all-to-all-done.lists_ref = s32[128,4,128]{2,1,0:T(4,128)S(1)} async-done(((s32[128,4,128]{2,1,0:T(4,128)}), s32[128,4,128]{2,1,0:T(4,128)S(1)}, u32[]{:S(2)}, u32[]{:S(2)}) %all-to-all-start) | async-done | bytes 262176 | tf_op jit(solution)/shard_map/all_to_all | solution.py:329
  45.1 11.9 %bag_gather.4 = (bf16[32,64,128]{2,1,0:T(8,128)(2,1)S(1)}, f32[32776,128]{1,0:T(8,128)S(1)}) custom-call(s32[1]{0:T(128)} %bitcast.5.quarter_ref, s32[65536]{0:T(1024)S(1)} %bitcast.28, bf16[32768,128]{1,0:T(8,128)(2,1)} %refs_0_), custom_call_target="tpu_custom_call" | custom-call | tf_op jit(solution)/shard_map/bag_gather/pallas_call | solution.py:193
  57.0 7.5 %bag_gather.6 = bf16[32,64,128]{2,1,0:T(8,128)(2,1)S(1)} custom-call(s32[1]{0:T(128)} %bitcast.6.quarter_ref, s32[65536]{0:T(1024)S(1)} %bitcast.29, f32[32776,128]{1,0:T(8,128)S(1)} %get-tuple-element.17.refs_0_), custom_call_target="tpu_custom_call" | custom-call | tf_op jit(solution)/shard_map/bag_gather/pallas_call | solution.py:193
  64.6 3.1 %collective-permute-start.1 = (bf16[32,64,128]{2,1,0:T(8,128)(2,1)S(1)}, bf16[32,64,128]{2,1,0:T(8,128)(2,1)S(1)}, u32[]{:S(2)}, u32[]{:S(2)}) collective-permute-start(bf16[32,64,128]{2,1,0:T(8,128)(2,1)S(1)} %get-tuple-element.18), channel_id=1, source_target_pairs={{0,2},{1,3},{2,0},{3,1},{4,6},{5,7},{6,4},{7,5},{8,10},{9,11},{10,... | collective-permute-start | bytes 1572872 | tf_op jit(solution)/shard_map/ppermute | solution.py:322
  67.7 7.4 %bag_gather.7 = bf16[32,64,128]{2,1,0:T(8,128)(2,1)S(1)} custom-call(s32[1]{0:T(128)} %bitcast.7.quarter_ref, s32[65536]{0:T(1024)S(1)} %bitcast.30, f32[32776,128]{1,0:T(8,128)S(1)} %get-tuple-element.17.refs_0_), custom_call_target="tpu_custom_call" | custom-call | tf_op jit(solution)/shard_map/bag_gather/pallas_call | solution.py:193
  75.2 7.3 %bag_gather.5.part_0 = bf16[32,64,128]{2,1,0:T(8,128)(2,1)S(1)} custom-call(s32[1]{0:T(128)} %bitcast.3.quarter_ref, s32[65536]{0:T(1024)S(1)} %bitcast.31, f32[32776,128]{1,0:T(8,128)S(1)} %get-tuple-element.17.refs_0_), custom_call_target="tpu_custom_call" | custom-call | tf_op jit(solution)/shard_map/bag_gather/pallas_call | solution.py:193
  82.5 5.5 %collective-permute-done.1.part_2 = bf16[32,64,128]{2,1,0:T(8,128)(2,1)S(1)} collective-permute-done((bf16[32,64,128]{2,1,0:T(8,128)(2,1)S(1)}, bf16[32,64,128]{2,1,0:T(8,128)(2,1)S(1)}, u32[]{:S(2)}, u32[]{:S(2)}) %collective-permute-start.1) | collective-permute-done | bytes 524320 | tf_op jit(solution)/shard_map/ppermute | solution.py:322
  88.1 1.2 collective-permute-done.2.part_3
  89.2 0.9 bag_combine.1
  90.1 18.4 %all_to_all.20.pooled_ref = bf16[16,128,128]{2,1,0:T(8,128)(2,1)S(1)} all-to-all(bf16[16,128,128]{2,1,0:T(8,128)(2,1)S(1)} %bitcast.32), channel_id=1, replica_groups={{0,4,8,12,16,20,24,28,32,36,40,44,48,52,56,60},{1,5,9,13,17,21,25,29,33..., dimensions={0} | all-to-all | bytes 1048576 | tf_op jit(solution)/shard_map/all_to_all | solution.py:343
  108.9 5.0 %all_to_all.21.both_ref = bf16[2,128,2048]{2,1,0:T(8,128)(2,1)S(1)} all-to-all(bf16[2,128,2048]{2,1,0:T(8,128)(2,1)S(1)} %broadcast_in_dim.4), channel_id=1, replica_groups=mesh['section'=2,'dev'=64] {'section'}, dimensions={0} | all-to-all | bytes 2097152 | tf_op jit(solution)/shard_map/all_to_all | solution.py:303
  113.9 3.9 %dense_near.1 = (f32[1,128]{1,0:T(1,128)S(1)}, bf16[4096,1024]{1,0:T(8,128)(2,1)S(1)}) custom-call(bf16[2,128,2048]{2,1,0:T(8,128)(2,1)S(1)} %all_to_all.21.both_ref, bf16[4096,1024]{1,0:T(8,128)(2,1)} %all-gather.3.cloned.1.call-done.w_ref, f32[1,1024]{1,0:T(1,128)S(1)} %bitcast.35, f32[1,1024]{1,0:T(1,128)S(1)} %bitcast.33), custom_call_target="tpu_custom_call" | custom-call | tf_op jit(solution)/shard_map/dense_near/pallas_call | solution.py:291
  117.8 1.8 %all-gather = f32[2,1,128]{2,1,0:T(1,128)S(1)} all-gather(f32[1,1,128]{2,1,0:T(1,128)S(1)} %bitcast.39), channel_id=1, replica_groups=mesh['section'=2,'dev'=64] {'section'}, dimensions={0}, use_global_device_ids=true | all-gather | bytes 1536 | tf_op jit(solution)/shard_map/all_gather | solution.py:350
  119.7 2.2 %collective-permute-done.3 = bf16[128,2048]{1,0:T(8,128)(2,1)S(1)} collective-permute-done((bf16[128,2048]{1,0:T(8,128)(2,1)S(1)}, bf16[128,2048]{1,0:T(8,128)(2,1)S(1)}, u32[]{:S(2)}, u32[]{:S(2)}) %collective-permute-start.3) | collective-permute-done | bytes 524320 | tf_op jit(solution)/shard_map/ppermute | solution.py:347
  122.0 5.5 %all_to_all.22.both_ref = bf16[2,128,2048]{2,1,0:T(8,128)(2,1)S(1)} all-to-all(bf16[2,128,2048]{2,1,0:T(8,128)(2,1)S(1)} %broadcast_in_dim.5), channel_id=1, replica_groups=mesh['section'=2,'dev'=64] {'section'}, dimensions={0} | all-to-all | bytes 2097152 | tf_op jit(solution)/shard_map/all_to_all | solution.py:303
  127.4 1.4 dense_far.1
  128.9 2.0 %collective-permute-start.8 = (f32[128]{0:T(128)S(1)}, f32[128]{0:T(128)S(1)}, u32[]{:S(2)}, u32[]{:S(2)}) collective-permute-start(f32[128]{0:T(128)S(1)} %bitcast.38), channel_id=1, source_target_pairs={{0,65},{1,64},{2,67},{3,66},{4,69},{5,68},{6,71},{7,70},{8,73},{9,... | collective-permute-start | bytes 1544 | tf_op jit(solution)/shard_map/ppermute | solution.py:357
  (26 shorter events, 4.2 us)
Async XLA Ops:
  6.5 107.4 %all-gather.3.cloned.1.call-start = ((), (), s32[]{:S(2)}) async-start(), calls=%async_computation.4 | async-start | bytes 8912896 | tf_op jit(solution)/shard_map/all_gather | solution.py:327
  7.5 8.7 %collective-permute-start.6 = (bf16[64,1024]{1,0:T(8,128)(2,1)S(1)}, bf16[64,1024]{1,0:T(8,128)(2,1)S(1)}, u32[]{:S(2)}, u32[]{:S(2)}) collective-permute-start(bf16[64,1024]{1,0:T(8,128)(2,1)S(1)} %get-tuple-element.30), channel_id=1, source_target_pairs={{0,3},{1,0},{2,1},{3,2},{4,7},{5,4},{6,5},{7,6},{8,11},{9,8},{10,9... | collective-permute-start | bytes 393224 | tf_op jit(solution)/shard_map/ppermute | solution.py:322
  11.1 5.4 %collective-permute-start.5 = (bf16[64,1024]{1,0:T(8,128)(2,1)S(1)}, bf16[64,1024]{1,0:T(8,128)(2,1)S(1)}, u32[]{:S(2)}, u32[]{:S(2)}) collective-permute-start(bf16[64,1024]{1,0:T(8,128)(2,1)S(1)} %get-tuple-element.29), channel_id=1, source_target_pairs={{0,2},{1,3},{2,0},{3,1},{4,6},{5,7},{6,4},{7,5},{8,10},{9,11},{10,... | collective-permute-start | bytes 393224 | tf_op jit(solution)/shard_map/ppermute | solution.py:322
  11.5 9.3 %collective-permute-start.4 = (bf16[64,1024]{1,0:T(8,128)(2,1)S(1)}, bf16[64,1024]{1,0:T(8,128)(2,1)S(1)}, u32[]{:S(2)}, u32[]{:S(2)}) collective-permute-start(bf16[64,1024]{1,0:T(8,128)(2,1)S(1)} %get-tuple-element.30), channel_id=1, source_target_pairs={{0,1},{1,2},{2,3},{3,0},{4,5},{5,6},{6,7},{7,4},{8,9},{9,10},{10,1... | collective-permute-start | bytes 393224 | tf_op jit(solution)/shard_map/ppermute | solution.py:322
  25.0 19.9 %all-to-all-start = ((s32[128,4,128]{2,1,0:T(4,128)}), s32[128,4,128]{2,1,0:T(4,128)S(1)}, u32[]{:S(2)}, u32[]{:S(2)}) async-start(s32[128,4,128]{2,1,0:T(4,128)} %bitcast.2), calls=%async_computation | async-start | bytes 524288 | tf_op jit(solution)/shard_map/all_to_all | solution.py:329
  64.6 18.0 %collective-permute-start = (bf16[32,64,128]{2,1,0:T(8,128)(2,1)S(1)}, bf16[32,64,128]{2,1,0:T(8,128)(2,1)S(1)}, u32[]{:S(2)}, u32[]{:S(2)}) collective-permute-start(bf16[32,64,128]{2,1,0:T(8,128)(2,1)S(1)} %bag_gather.6), channel_id=1, source_target_pairs={{0,1},{1,2},{2,3},{3,0},{4,5},{5,6},{6,7},{7,4},{8,9},{9,10},{10,1... | collective-permute-start | bytes 1572872 | tf_op jit(solution)/shard_map/ppermute | solution.py:322
  64.6 23.4 %collective-permute-start.1 = (bf16[32,64,128]{2,1,0:T(8,128)(2,1)S(1)}, bf16[32,64,128]{2,1,0:T(8,128)(2,1)S(1)}, u32[]{:S(2)}, u32[]{:S(2)}) collective-permute-start(bf16[32,64,128]{2,1,0:T(8,128)(2,1)S(1)} %get-tuple-element.18), channel_id=1, source_target_pairs={{0,2},{1,3},{2,0},{3,1},{4,6},{5,7},{6,4},{7,5},{8,10},{9,11},{10,... | collective-permute-start | bytes 1572872 | tf_op jit(solution)/shard_map/ppermute | solution.py:322
  75.1 14.1 %collective-permute-start.2 = (bf16[32,64,128]{2,1,0:T(8,128)(2,1)S(1)}, bf16[32,64,128]{2,1,0:T(8,128)(2,1)S(1)}, u32[]{:S(2)}, u32[]{:S(2)}) collective-permute-start(bf16[32,64,128]{2,1,0:T(8,128)(2,1)S(1)} %bag_gather.7), channel_id=1, source_target_pairs={{0,3},{1,0},{2,1},{3,2},{4,7},{5,4},{6,5},{7,6},{8,11},{9,8},{10,9... | collective-permute-start | bytes 1572872 | tf_op jit(solution)/shard_map/ppermute | solution.py:322
  75.2 33.6 %copy-start = (bf16[2048]{0:T(1024)(128)(2,1)S(1)}, bf16[2048]{0:T(1024)(128)(2,1)}, u32[]{:S(2)}) copy-start(bf16[2048]{0:T(1024)(128)(2,1)} %param.11) | copy-start | bytes 12292
  75.2 33.6 %copy-start.1 = (bf16[2048]{0:T(1024)(128)(2,1)S(1)}, bf16[2048]{0:T(1024)(128)(2,1)}, u32[]{:S(2)}) copy-start(bf16[2048]{0:T(1024)(128)(2,1)} %param.10) | copy-start | bytes 12292
  108.7 13.2 %collective-permute-start.3 = (bf16[128,2048]{1,0:T(8,128)(2,1)S(1)}, bf16[128,2048]{1,0:T(8,128)(2,1)S(1)}, u32[]{:S(2)}, u32[]{:S(2)}) collective-permute-start(bf16[128,2048]{1,0:T(8,128)(2,1)S(1)} %feature_rows.1), channel_id=1, source_target_pairs={{0,1},{1,0},{2,3},{3,2},{4,5},{5,4},{6,7},{7,6},{8,9},{9,8},{10,11... | collective-permute-start | bytes 1572872 | tf_op jit(solution)/shard_map/ppermute | solution.py:347
  128.8 2.5 %collective-permute-start.7 = (f32[128]{0:T(128)S(1)}, f32[128]{0:T(128)S(1)}, u32[]{:S(2)}, u32[]{:S(2)}) collective-permute-start(f32[128]{0:T(128)S(1)} %bitcast.37), channel_id=1, source_target_pairs={{0,1},{1,0},{2,3},{3,2},{4,5},{5,4},{6,7},{7,6},{8,9},{9,8},{10,11... | collective-permute-start | bytes 1544 | tf_op jit(solution)/shard_map/ppermute | solution.py:357
  128.9 3.2 %collective-permute-start.8 = (f32[128]{0:T(128)S(1)}, f32[128]{0:T(128)S(1)}, u32[]{:S(2)}, u32[]{:S(2)}) collective-permute-start(f32[128]{0:T(128)S(1)} %bitcast.38), channel_id=1, source_target_pairs={{0,65},{1,64},{2,67},{3,66},{4,69},{5,68},{6,71},{7,70},{8,73},{9,... | collective-permute-start | bytes 1544 | tf_op jit(solution)/shard_map/ppermute | solution.py:357
Sparse Core Ops, SparseCore 0:
  22.0 72.8 all-gather.2

commit v8 on v7

--- a/solution.py
+++ b/solution.py
@@ -18,6 +18,7 @@
 TSLOTS = 4
 HID_SPLIT = 2
 WBLK = 512
+CALLS = (("c", 2, 0, 2), ("b", 1, 0, 2), ("d", 3, 0, 1), ("e", 3, 1, 1), ("a", 0, 0, 2))
 SORT8 = (
     (0, 2), (1, 3), (4, 6), (5, 7), (0, 4), (1, 5), (2, 6), (3, 7), (0, 1), (2, 3),
     (4, 5), (6, 7), (2, 4), (3, 5), (1, 4), (3, 6), (1, 2), (3, 4), (5, 6),
@@ -112,17 +113,17 @@
     )(ids, pool_len)
 
 
-def gather_body(quarter_ref, lists_ref, *refs, unroll, widen):
+def gather_body(y_ref, lists_ref, *refs, unroll, widen, first, ahead):
     if widen:
         table_ref, out_ref, tab, tbuf, tsem, smem, acc, lsem = refs
     else:
         tab, out_ref, smem, acc, lsem = refs
-    quarter = quarter_ref[0]
+    quarter = (y_ref[0] + ahead) & 3
     planes = out_ref.shape[0] // 2
     piece = 2 * SLOTS
 
     def list_copy(m):
-        start = pl.multiple_of((4 * m + quarter) * piece, piece)
+        start = pl.multiple_of((4 * (first + m) + quarter) * piece, piece)
         return pltpu.make_async_copy(
             lists_ref.at[pl.ds(start, piece)],
             smem.at[pl.ds(pl.multiple_of(m * piece, piece), piece)],
@@ -179,7 +180,7 @@
     lax.fori_loop(0, planes, plane, 0)
 
 
-def gather(quarter, lists, table, planes, unroll=4, widen=False):
+def gather(y, ahead, lists, table, planes, first=0, unroll=4, widen=False):
     vmem = pl.BlockSpec(memory_space=pltpu.VMEM)
     sums = pltpu.VMEM((2 * planes, CHUNK, E), jnp.bfloat16)
     scratch = [
@@ -191,7 +192,7 @@
         table = pltpu.with_memory_space_constraint(table, pltpu.HBM)
         scratch = [pltpu.VMEM((TSLOTS, TBLK, E), jnp.bfloat16), pltpu.SemaphoreType.DMA((TSLOTS,))] + scratch
     return pl.pallas_call(
-        functools.partial(gather_body, unroll=unroll, widen=widen),
+        functools.partial(gather_body, unroll=unroll, widen=widen, first=first, ahead=ahead),
         out_shape=(sums, pltpu.VMEM((ROWS_DEV + 8, E), jnp.float32)) if widen else sums,
         in_specs=[
             pl.BlockSpec(memory_space=pltpu.SMEM),
@@ -202,12 +203,13 @@
         scratch_shapes=scratch,
         compiler_params=pltpu.CompilerParams(vmem_limit_bytes=(6 if widen else 4) * 2**20),
         name="bag_gather",
-    )(quarter, lists, table)
-
-
-def combine_body(y_ref, lists_ref, part_0, part_1, part_2, part_3, out_ref):
+    )(y, lists, table)
+
+
+def combine_body(y_ref, lists_ref, part_0, part_1, part_2, part_3, part_3b, out_ref):
     y = y_ref[0]
-    parts = (part_0, part_1, part_2, part_3)
+    parts = (part_0, part_1, part_2)
+    half = part_3.shape[0]
     bag = lax.broadcasted_iota(jnp.int32, (CHUNK, 4 * CHUNK), 0)
     for c in range(out_ref.shape[0]):
         source = 8 * (c // 2) + 2 * y + c % 2
@@ -217,7 +219,7 @@
         rows = []
         for j in range(4):
             came = (y - j) & 3
-            row = parts[3][c]
+            row = part_3[c] if c < half else part_3b[c - half]
             for k in range(3):
                 row = jnp.where(came == k, parts[k][c], row)
             rows.append(row)
@@ -230,7 +232,7 @@
     return pl.pallas_call(
         combine_body,
         out_shape=pltpu.VMEM(parts[0].shape, jnp.bfloat16),
-        in_specs=[pl.BlockSpec(memory_space=pltpu.SMEM)] + [vmem] * 5,
+        in_specs=[pl.BlockSpec(memory_space=pltpu.SMEM)] + [vmem] * (1 + len(parts)),
         out_specs=vmem,
         compiler_params=pltpu.CompilerParams(vmem_limit_bytes=4 * 2**20),
         name="bag_combine",
@@ -330,15 +332,17 @@
     line = lax.broadcasted_iota(jnp.int32, arrived.shape, 1)
     clean = jnp.where(line < 2, arrived, arrived & 0xFFFFF).reshape(-1)
     clean, tables = lax.optimization_barrier((clean, tables))
-    parts = {}
-    for k in (2, 1, 3, 0):
-        quarter = ((y + k) % ring).reshape(1)
-        if k == 2:
-            sums, tab = gather(quarter, clean, tables, planes, widen=True)
+    here = y.reshape(1)
+    split = planes // 2
+    parts, tab = {}, None
+    for name, k, first, count in CALLS:
+        first, count = first * split, count * split
+        if tab is None:
+            sums, tab = gather(here, k, clean, tables, count, first, widen=True)
         else:
-            sums = gather(quarter, clean, tab, planes)
-        parts[k] = along(sums, k) if k else sums
-    pooled = combine(y.reshape(1), arrived, [parts[k] for k in range(ring)])
+            sums = gather(here, k, clean, tab, count, first)
+        parts[name] = along(sums, k) if k else sums
+    pooled = combine(here, arrived, [parts[name] for name in "abcde"])
     pooled = pooled.reshape(planes, 2 * CHUNK, E)
     pooled = lax.all_to_all(pooled, "dev", 0, 0, axis_index_groups=levels, tiled=True)
     features = feature_rows(pooled)

time: 140 us -> 140 us (level)
    ppermute x6 -> x7, waiting for transfers between devices: 15.3 us -> 14.2 us  [along(): lax.ppermute(x, 'dev', [(d, d // ring * ring + (d + k) % ring) for d in r...]
    pallas_call x4 -> x5, Pallas kernels: 34.1 us -> 34.7 us  [gather(): pl.pallas_call(functools.partial(gather_body, unroll=unroll, widen=widen,...]
    ppermute x6 -> x7, starting transfers between devices: 7.91 us -> 8.21 us  [along(): lax.ppermute(x, 'dev', [(d, d // ring * ring + (d + k) % ring) for d in r...]
  transfers between devices with their start and end apart: 11 -> 12, of which waited for: 9 -> 8; matrix products, arithmetic and copies ran while one was open for 0% -> 0% of each run, Pallas kernels for 30% -> 31%
where the time goes in v8:
time: 140 us; the launch traced here: 139 us
  Pallas kernels  44.1 us (32%)
  blocking collectives  31.1 us (22%)
  waiting for transfers between devices  29.3 us (21%)
  starting transfers between devices  18.5 us (13%)
  between operations  13.6 us (10%)
  other arithmetic  1.59 us (1%)
    pallas_call x5, Pallas kernels, gather(): pl.pallas_call(functools.partial(gather_body, unroll=unroll, widen=widen,...  34.7 us
    all_to_all x1, blocking collectives, body(): lax.all_to_all(pooled, 'dev', 0, 0, axis_index_groups=levels, tiled=True)  18.8 us
    ppermute x7, waiting for transfers between devices, along(): lax.ppermute(x, 'dev', [(d, d // ring * ring + (d + k) % ring) for d in r...  14.2 us
    all_to_all x1, waiting for transfers between devices, body(): lax.all_to_all(lists.reshape(n_sec * n_dev, 4, 128), both_axes, 0, 0, til...  11.7 us
    all_to_all x2, blocking collectives, swap(): lax.all_to_all(jnp.broadcast_to(x[None], (2, *x.shape)), axis, 0, 0, tile...  10.5 us
    ppermute x7, starting transfers between devices, along(): lax.ppermute(x, 'dev', [(d, d // ring * ring + (d + k) % ring) for d in r...  8.21 us
    all_to_all x1, starting transfers between devices, body(): lax.all_to_all(lists.reshape(n_sec * n_dev, 4, 128), both_axes, 0, 0, til...  8 us
    pallas_call x2, Pallas kernels, dense(): pl.pallas_call(functools.partial(dense_body, stream=stream), out_shape=(o...  5.23 us
  transfers between devices with their start and end apart: 12, of which 8 were waited for; matrix products, arithmetic and copies ran while one was open for 0% of the time, Pallas kernels for 31%

profile of v8, /device:TPU:1, one launch (start us, length us, event | category | flops | bytes accessed | tf_op | source)
XLA Modules:
  0.0 139.4 jit_solution(13029615769991165848)
XLA Ops:
  6.5 1.0 constant_dynamic-slice_fusion.1
  7.5 3.6 %collective-permute-start.7 = (bf16[64,1024]{1,0:T(8,128)(2,1)S(1)}, bf16[64,1024]{1,0:T(8,128)(2,1)S(1)}, u32[]{:S(2)}, u32[]{:S(2)}) collective-permute-start(bf16[64,1024]{1,0:T(8,128)(2,1)S(1)} %get-tuple-element.30), channel_id=1, source_target_pairs={{0,3},{1,0},{2,1},{3,2},{4,7},{5,4},{6,5},{7,6},{8,11},{9,8},{10,9... | collective-permute-start | bytes 393224 | tf_op jit(solution)/shard_map/ppermute | solution.py:324
  12.2 4.0 %collective-permute-done.7 = bf16[64,1024]{1,0:T(8,128)(2,1)S(1)} collective-permute-done((bf16[64,1024]{1,0:T(8,128)(2,1)S(1)}, bf16[64,1024]{1,0:T(8,128)(2,1)S(1)}, u32[]{:S(2)}, u32[]{:S(2)}) %collective-permute-start.7) | collective-permute-done | bytes 131104 | tf_op jit(solution)/shard_map/ppermute | solution.py:324
  16.6 4.2 %collective-permute-done.5 = bf16[64,1024]{1,0:T(8,128)(2,1)S(1)} collective-permute-done((bf16[64,1024]{1,0:T(8,128)(2,1)S(1)}, bf16[64,1024]{1,0:T(8,128)(2,1)S(1)}, u32[]{:S(2)}, u32[]{:S(2)}) %collective-permute-start.5) | collective-permute-done | bytes 131104 | tf_op jit(solution)/shard_map/ppermute | solution.py:324
  20.9 0.9 pad_maximum_fusion.1
  21.8 3.2 %bag_lists.1 = s32[512,128]{1,0:T(8,128)} custom-call(s32[32,8,64]{2,1,0:T(8,128)} %bitcast.38, s32[32]{0:T(128)} %pool_ref.1), custom_call_target="tpu_custom_call" | custom-call | tf_op jit(solution)/shard_map/bag_lists/pallas_call | solution.py:106
  25.1 8.0 %all-to-all-start = ((s32[128,4,128]{2,1,0:T(4,128)}), s32[128,4,128]{2,1,0:T(4,128)S(1)}, u32[]{:S(2)}, u32[]{:S(2)}) async-start(s32[128,4,128]{2,1,0:T(4,128)} %bitcast.2), calls=%async_computation | async-start | bytes 524288 | tf_op jit(solution)/shard_map/all_to_all | solution.py:331
  33.1 11.7 %all-to-all-done.lists_ref = s32[128,4,128]{2,1,0:T(4,128)S(1)} async-done(((s32[128,4,128]{2,1,0:T(4,128)}), s32[128,4,128]{2,1,0:T(4,128)S(1)}, u32[]{:S(2)}, u32[]{:S(2)}) %all-to-all-start) | async-done | bytes 262176 | tf_op jit(solution)/shard_map/all_to_all | solution.py:331
  44.9 11.9 %bag_gather.5 = (bf16[32,64,128]{2,1,0:T(8,128)(2,1)S(1)}, f32[32776,128]{1,0:T(8,128)S(1)}) custom-call(s32[1]{0:T(128)} %bitcast.y_ref, s32[65536]{0:T(1024)S(1)} %bitcast.24, bf16[32768,128]{1,0:T(8,128)(2,1)} %refs_0_), custom_call_target="tpu_custom_call" | custom-call | tf_op jit(solution)/shard_map/bag_gather/pallas_call | solution.py:194
  56.9 7.5 %bag_gather.7 = bf16[32,64,128]{2,1,0:T(8,128)(2,1)S(1)} custom-call(s32[1]{0:T(128)} %bitcast.y_ref, s32[65536]{0:T(1024)S(1)} %bitcast.25, f32[32776,128]{1,0:T(8,128)S(1)} %get-tuple-element.17.refs_0_), custom_call_target="tpu_custom_call" | custom-call | tf_op jit(solution)/shard_map/bag_gather/pallas_call | solution.py:194
  64.8 3.0 %collective-permute-start.1 = (bf16[32,64,128]{2,1,0:T(8,128)(2,1)S(1)}, bf16[32,64,128]{2,1,0:T(8,128)(2,1)S(1)}, u32[]{:S(2)}, u32[]{:S(2)}) collective-permute-start(bf16[32,64,128]{2,1,0:T(8,128)(2,1)S(1)} %get-tuple-element.18), channel_id=1, source_target_pairs={{0,2},{1,3},{2,0},{3,1},{4,6},{5,7},{6,4},{7,5},{8,10},{9,11},{10,... | collective-permute-start | bytes 1572872 | tf_op jit(solution)/shard_map/ppermute | solution.py:324
  67.8 4.0 %bag_gather.8 = bf16[16,64,128]{2,1,0:T(8,128)(2,1)S(1)} custom-call(s32[1]{0:T(128)} %bitcast.y_ref, s32[65536]{0:T(1024)S(1)} %bitcast.26, f32[32776,128]{1,0:T(8,128)S(1)} %get-tuple-element.17.refs_0_), custom_call_target="tpu_custom_call" | custom-call | tf_op jit(solution)/shard_map/bag_gather/pallas_call | solution.py:194
  71.8 3.9 %bag_gather.9 = bf16[16,64,128]{2,1,0:T(8,128)(2,1)S(1)} custom-call(s32[1]{0:T(128)} %bitcast.y_ref, s32[65536]{0:T(1024)S(1)} %bitcast.27, f32[32776,128]{1,0:T(8,128)S(1)} %get-tuple-element.17.refs_0_), custom_call_target="tpu_custom_call" | custom-call | tf_op jit(solution)/shard_map/bag_gather/pallas_call | solution.py:194
  75.9 7.3 %bag_gather.6.part_0 = bf16[32,64,128]{2,1,0:T(8,128)(2,1)S(1)} custom-call(s32[1]{0:T(128)} %bitcast.y_ref, s32[65536]{0:T(1024)S(1)} %bitcast.28, f32[32776,128]{1,0:T(8,128)S(1)} %get-tuple-element.17.refs_0_), custom_call_target="tpu_custom_call" | custom-call | tf_op jit(solution)/shard_map/bag_gather/pallas_call | solution.py:194
  83.3 5.6 %collective-permute-done.3.part_3b = bf16[16,64,128]{2,1,0:T(8,128)(2,1)S(1)} collective-permute-done((bf16[16,64,128]{2,1,0:T(8,128)(2,1)S(1)}, bf16[16,64,128]{2,1,0:T(8,128)(2,1)S(1)}, u32[]{:S(2)}, u32[]{:S(2)}) %collective-permute-start.3) | collective-permute-done | bytes 262176 | tf_op jit(solution)/shard_map/ppermute | solution.py:324
  88.8 0.9 bag_combine.1
  89.7 18.8 %all_to_all.20.pooled_ref = bf16[16,128,128]{2,1,0:T(8,128)(2,1)S(1)} all-to-all(bf16[16,128,128]{2,1,0:T(8,128)(2,1)S(1)} %bitcast.29), channel_id=1, replica_groups={{0,4,8,12,16,20,24,28,32,36,40,44,48,52,56,60},{1,5,9,13,17,21,25,29,33..., dimensions={0} | all-to-all | bytes 1048576 | tf_op jit(solution)/shard_map/all_to_all | solution.py:347
  109.0 5.0 %all_to_all.21.both_ref = bf16[2,128,2048]{2,1,0:T(8,128)(2,1)S(1)} all-to-all(bf16[2,128,2048]{2,1,0:T(8,128)(2,1)S(1)} %broadcast_in_dim.4), channel_id=1, replica_groups=mesh['section'=2,'dev'=64] {'section'}, dimensions={0} | all-to-all | bytes 2097152 | tf_op jit(solution)/shard_map/all_to_all | solution.py:305
  114.0 3.9 %dense_near.1 = (f32[1,128]{1,0:T(1,128)S(1)}, bf16[4096,1024]{1,0:T(8,128)(2,1)S(1)}) custom-call(bf16[2,128,2048]{2,1,0:T(8,128)(2,1)S(1)} %all_to_all.21.both_ref, bf16[4096,1024]{1,0:T(8,128)(2,1)} %all-gather.3.cloned.1.call-done.w_ref, f32[1,1024]{1,0:T(1,128)S(1)} %bitcast.32, f32[1,1024]{1,0:T(1,128)S(1)} %bitcast.30), custom_call_target="tpu_custom_call" | custom-call | tf_op jit(solution)/shard_map/dense_near/pallas_call | solution.py:293
  117.8 1.8 %all-gather = f32[2,1,128]{2,1,0:T(1,128)S(1)} all-gather(f32[1,1,128]{2,1,0:T(1,128)S(1)} %bitcast.36), channel_id=1, replica_groups=mesh['section'=2,'dev'=64] {'section'}, dimensions={0}, use_global_device_ids=true | all-gather | bytes 1536 | tf_op jit(solution)/shard_map/all_gather | solution.py:354
  119.7 2.1 %collective-permute-done.4 = bf16[128,2048]{1,0:T(8,128)(2,1)S(1)} collective-permute-done((bf16[128,2048]{1,0:T(8,128)(2,1)S(1)}, bf16[128,2048]{1,0:T(8,128)(2,1)S(1)}, u32[]{:S(2)}, u32[]{:S(2)}) %collective-permute-start.4) | collective-permute-done | bytes 524320 | tf_op jit(solution)/shard_map/ppermute | solution.py:351
  121.9 5.5 %all_to_all.22.both_ref = bf16[2,128,2048]{2,1,0:T(8,128)(2,1)S(1)} all-to-all(bf16[2,128,2048]{2,1,0:T(8,128)(2,1)S(1)} %broadcast_in_dim.5), channel_id=1, replica_groups=mesh['section'=2,'dev'=64] {'section'}, dimensions={0} | all-to-all | bytes 2097152 | tf_op jit(solution)/shard_map/all_to_all | solution.py:305
  127.3 1.4 dense_far.1
  128.9 1.9 %collective-permute-start.9 = (f32[128]{0:T(128)S(1)}, f32[128]{0:T(128)S(1)}, u32[]{:S(2)}, u32[]{:S(2)}) collective-permute-start(f32[128]{0:T(128)S(1)} %bitcast.35), channel_id=1, source_target_pairs={{0,65},{1,64},{2,67},{3,66},{4,69},{5,68},{6,71},{7,70},{8,73},{9,... | collective-permute-start | bytes 1544 | tf_op jit(solution)/shard_map/ppermute | solution.py:361
  (29 shorter events, 4.8 us)
Async XLA Ops:
  6.5 107.4 %all-gather.3.cloned.1.call-start = ((), (), s32[]{:S(2)}) async-start(), calls=%async_computation.4 | async-start | bytes 8912896 | tf_op jit(solution)/shard_map/all_gather | solution.py:329
  7.5 8.7 %collective-permute-start.7 = (bf16[64,1024]{1,0:T(8,128)(2,1)S(1)}, bf16[64,1024]{1,0:T(8,128)(2,1)S(1)}, u32[]{:S(2)}, u32[]{:S(2)}) collective-permute-start(bf16[64,1024]{1,0:T(8,128)(2,1)S(1)} %get-tuple-element.30), channel_id=1, source_target_pairs={{0,3},{1,0},{2,1},{3,2},{4,7},{5,4},{6,5},{7,6},{8,11},{9,8},{10,9... | collective-permute-start | bytes 393224 | tf_op jit(solution)/shard_map/ppermute | solution.py:324
  11.1 5.4 %collective-permute-start.6 = (bf16[64,1024]{1,0:T(8,128)(2,1)S(1)}, bf16[64,1024]{1,0:T(8,128)(2,1)S(1)}, u32[]{:S(2)}, u32[]{:S(2)}) collective-permute-start(bf16[64,1024]{1,0:T(8,128)(2,1)S(1)} %get-tuple-element.29), channel_id=1, source_target_pairs={{0,2},{1,3},{2,0},{3,1},{4,6},{5,7},{6,4},{7,5},{8,10},{9,11},{10,... | collective-permute-start | bytes 393224 | tf_op jit(solution)/shard_map/ppermute | solution.py:324
  11.5 9.3 %collective-permute-start.5 = (bf16[64,1024]{1,0:T(8,128)(2,1)S(1)}, bf16[64,1024]{1,0:T(8,128)(2,1)S(1)}, u32[]{:S(2)}, u32[]{:S(2)}) collective-permute-start(bf16[64,1024]{1,0:T(8,128)(2,1)S(1)} %get-tuple-element.30), channel_id=1, source_target_pairs={{0,1},{1,2},{2,3},{3,0},{4,5},{5,6},{6,7},{7,4},{8,9},{9,10},{10,1... | collective-permute-start | bytes 393224 | tf_op jit(solution)/shard_map/ppermute | solution.py:324
  25.1 19.8 %all-to-all-start = ((s32[128,4,128]{2,1,0:T(4,128)}), s32[128,4,128]{2,1,0:T(4,128)S(1)}, u32[]{:S(2)}, u32[]{:S(2)}) async-start(s32[128,4,128]{2,1,0:T(4,128)} %bitcast.2), calls=%async_computation | async-start | bytes 524288 | tf_op jit(solution)/shard_map/all_to_all | solution.py:331
  64.4 24.5 %collective-permute-start = (bf16[32,64,128]{2,1,0:T(8,128)(2,1)S(1)}, bf16[32,64,128]{2,1,0:T(8,128)(2,1)S(1)}, u32[]{:S(2)}, u32[]{:S(2)}) collective-permute-start(bf16[32,64,128]{2,1,0:T(8,128)(2,1)S(1)} %bag_gather.7), channel_id=1, source_target_pairs={{0,1},{1,2},{2,3},{3,0},{4,5},{5,6},{6,7},{7,4},{8,9},{9,10},{10,1... | collective-permute-start | bytes 1572872 | tf_op jit(solution)/shard_map/ppermute | solution.py:324
  64.8 24.1 %collective-permute-start.1 = (bf16[32,64,128]{2,1,0:T(8,128)(2,1)S(1)}, bf16[32,64,128]{2,1,0:T(8,128)(2,1)S(1)}, u32[]{:S(2)}, u32[]{:S(2)}) collective-permute-start(bf16[32,64,128]{2,1,0:T(8,128)(2,1)S(1)} %get-tuple-element.18), channel_id=1, source_target_pairs={{0,2},{1,3},{2,0},{3,1},{4,6},{5,7},{6,4},{7,5},{8,10},{9,11},{10,... | collective-permute-start | bytes 1572872 | tf_op jit(solution)/shard_map/ppermute | solution.py:324
  75.8 33.1 %copy-start = (bf16[2048]{0:T(1024)(128)(2,1)S(1)}, bf16[2048]{0:T(1024)(128)(2,1)}, u32[]{:S(2)}) copy-start(bf16[2048]{0:T(1024)(128)(2,1)} %param.11) | copy-start | bytes 12292
  75.8 33.1 %copy-start.1 = (bf16[2048]{0:T(1024)(128)(2,1)S(1)}, bf16[2048]{0:T(1024)(128)(2,1)}, u32[]{:S(2)}) copy-start(bf16[2048]{0:T(1024)(128)(2,1)} %param.10) | copy-start | bytes 12292
  75.8 7.5 %collective-permute-start.2 = (bf16[16,64,128]{2,1,0:T(8,128)(2,1)S(1)}, bf16[16,64,128]{2,1,0:T(8,128)(2,1)S(1)}, u32[]{:S(2)}, u32[]{:S(2)}) collective-permute-start(bf16[16,64,128]{2,1,0:T(8,128)(2,1)S(1)} %bag_gather.8), channel_id=1, source_target_pairs={{0,3},{1,0},{2,1},{3,2},{4,7},{5,4},{6,5},{7,6},{8,11},{9,8},{10,9... | collective-permute-start | bytes 786440 | tf_op jit(solution)/shard_map/ppermute | solution.py:324
  75.9 13.0 %collective-permute-start.3 = (bf16[16,64,128]{2,1,0:T(8,128)(2,1)S(1)}, bf16[16,64,128]{2,1,0:T(8,128)(2,1)S(1)}, u32[]{:S(2)}, u32[]{:S(2)}) collective-permute-start(bf16[16,64,128]{2,1,0:T(8,128)(2,1)S(1)} %bag_gather.9), channel_id=1, source_target_pairs={{0,3},{1,0},{2,1},{3,2},{4,7},{5,4},{6,5},{7,6},{8,11},{9,8},{10,9... | collective-permute-start | bytes 786440 | tf_op jit(solution)/shard_map/ppermute | solution.py:324
  108.6 13.2 %collective-permute-start.4 = (bf16[128,2048]{1,0:T(8,128)(2,1)S(1)}, bf16[128,2048]{1,0:T(8,128)(2,1)S(1)}, u32[]{:S(2)}, u32[]{:S(2)}) collective-permute-start(bf16[128,2048]{1,0:T(8,128)(2,1)S(1)} %feature_rows.1), channel_id=1, source_target_pairs={{0,1},{1,0},{2,3},{3,2},{4,5},{5,4},{6,7},{7,6},{8,9},{9,8},{10,11... | collective-permute-start | bytes 1572872 | tf_op jit(solution)/shard_map/ppermute | solution.py:351
  128.7 2.5 %collective-permute-start.8 = (f32[128]{0:T(128)S(1)}, f32[128]{0:T(128)S(1)}, u32[]{:S(2)}, u32[]{:S(2)}) collective-permute-start(f32[128]{0:T(128)S(1)} %bitcast.34), channel_id=1, source_target_pairs={{0,1},{1,0},{2,3},{3,2},{4,5},{5,4},{6,7},{7,6},{8,9},{9,8},{10,11... | collective-permute-start | bytes 1544 | tf_op jit(solution)/shard_map/ppermute | solution.py:361
  128.9 3.1 %collective-permute-start.9 = (f32[128]{0:T(128)S(1)}, f32[128]{0:T(128)S(1)}, u32[]{:S(2)}, u32[]{:S(2)}) collective-permute-start(f32[128]{0:T(128)S(1)} %bitcast.35), channel_id=1, source_target_pairs={{0,65},{1,64},{2,67},{3,66},{4,69},{5,68},{6,71},{7,70},{8,73},{9,... | collective-permute-start | bytes 1544 | tf_op jit(solution)/shard_map/ppermute | solution.py:361
Sparse Core Ops, SparseCore 0:
  22.0 72.8 all-gather.2

commit v9 on v8

--- a/solution.py
+++ b/solution.py
@@ -16,6 +16,7 @@
 DEAD = ROWS_DEV | (8 << 16)
 TBLK = 2048
 TSLOTS = 4
+LSLOTS = 4
 HID_SPLIT = 2
 WBLK = 512
 CALLS = (("c", 2, 0, 2), ("b", 1, 0, 2), ("d", 3, 0, 1), ("e", 3, 1, 1), ("a", 0, 0, 2))
@@ -25,7 +26,7 @@
 )
 
 
-def prep_body(x_ref, pool_ref, list_ref, order_ref):
+def prep_body(x_ref, pool_ref, list_ref, order_ref, group_ref):
     shape = (CHUNK, 128)
     tables = x_ref.shape[0]
     lane = lax.broadcasted_iota(jnp.int32, shape, 1)
@@ -92,9 +93,11 @@
     mask = jnp.where(head, 0xFFFFF, 0xFFFF)
     groups = [w & mask for w in groups]
     groups[0] = groups[0] | jnp.where(head, jnp.broadcast_to(total << 20, tile), 0)
+    for k in range(64):
+        group_ref[8 * k : 8 * k + 8, :] = groups[k]
     for i in range(4):
-        block = jnp.concatenate(groups[16 * i : 16 * i + 16], axis=0)
-        block = block.T
+        block = [group_ref[pl.ds(2 * i + n, 64, stride=8), :] for n in range(2)]
+        block = jnp.concatenate(block, axis=0).T
         for j in range(4):
             rows = block[j * tables : (j + 1) * tables, :]
             if i >= 2:
@@ -108,7 +111,7 @@
         out_shape=pltpu.VMEM((128 * 4, 128), jnp.int32),
         out_specs=pl.BlockSpec(memory_space=pltpu.VMEM),
         in_specs=[pl.BlockSpec(memory_space=pltpu.VMEM), pl.BlockSpec(memory_space=pltpu.SMEM)],
-        scratch_shapes=[pltpu.VMEM((ids.shape[0], 4 * CHUNK), jnp.int32)],
+        scratch_shapes=[pltpu.VMEM((ids.shape[0], 4 * CHUNK), jnp.int32), pltpu.VMEM((SLOTS, 128), jnp.int32)],
         name="bag_lists",
     )(ids, pool_len)
 
@@ -122,12 +125,10 @@
     planes = out_ref.shape[0] // 2
     piece = 2 * SLOTS
 
-    def list_copy(m):
+    def list_copy(m, slot):
         start = pl.multiple_of((4 * (first + m) + quarter) * piece, piece)
         return pltpu.make_async_copy(
-            lists_ref.at[pl.ds(start, piece)],
-            smem.at[pl.ds(pl.multiple_of(m * piece, piece), piece)],
-            lsem.at[m],
+            lists_ref.at[pl.ds(start, piece)], smem.at[pl.ds(slot * piece, piece)], lsem.at[slot]
         )
 
     if widen:
@@ -141,8 +142,8 @@
         blocks = ROWS_DEV // TBLK
         for b in range(TSLOTS):
             table_copy(b).start()
-    for m in range(planes):
-        list_copy(m).start()
+    for slot in range(LSLOTS):
+        list_copy(slot, slot).start()
     if widen:
         tab[pl.ds(ROWS_DEV, 8), :] = jnp.zeros((8, E), jnp.float32)
         for b in range(blocks):
@@ -151,42 +152,49 @@
             if b + TSLOTS < blocks:
                 table_copy(b + TSLOTS).start()
 
-    def level(at):
-        head = smem[at]
-        rows = [head & 0xFFFF] + [smem[at + i] for i in range(1, 8)]
-        rows = jnp.concatenate([tab[pl.ds(r, 1), :] for r in rows], axis=0)
-        return pl.multiple_of((head >> 13) & 0x78, 8), rows
-
-    def chunk(c):
-        base = c * SLOTS
+    def chunk(slot, h, c):
+        at = slot * piece + h * SLOTS
+        words = [smem.at[pl.ds(at + 64 * i, 64)] for i in range(8)]
         acc[...] = jnp.zeros(acc.shape, jnp.float32)
-        levels = smem[base] >> 20
+        levels = words[0][0] >> 20
+
+        def level(n):
+            head = words[0][n]
+            rows = [head & 0xFFFF] + [w[n] for w in words[1:]]
+            rows = jnp.concatenate([tab[pl.ds(r, 1), :] for r in rows], axis=0)
+            return pl.multiple_of((head >> 13) & 0x78, 8), rows
 
         def step(k, carry):
-            at = base + k * (8 * unroll)
-            for g, rows in [level(at + 8 * u) for u in range(unroll)]:
+            for g, rows in [level(k * unroll + u) for u in range(unroll)]:
                 acc[pl.ds(g, 8), :] += rows
             return carry
 
         lax.fori_loop(0, (levels + unroll - 1) >> (unroll.bit_length() - 1), step, 0)
         out_ref[c] = acc[pl.ds(0, CHUNK), :].astype(jnp.bfloat16)
 
-    def plane(m, carry):
-        list_copy(m).wait()
-        chunk(2 * m)
-        chunk(2 * m + 1)
+    def round_of(n, carry):
+        for slot in range(LSLOTS):
+            m = n * LSLOTS + slot
+            list_copy(m, slot).wait()
+            for h in range(2):
+                chunk(slot, h, 2 * m + h)
+
+            @pl.when(m + LSLOTS < planes)
+            def _():
+                list_copy(m + LSLOTS, slot).start()
+
         return carry
 
-    lax.fori_loop(0, planes, plane, 0)
+    lax.fori_loop(0, planes // LSLOTS, round_of, 0)
 
 
 def gather(y, ahead, lists, table, planes, first=0, unroll=4, widen=False):
     vmem = pl.BlockSpec(memory_space=pltpu.VMEM)
     sums = pltpu.VMEM((2 * planes, CHUNK, E), jnp.bfloat16)
     scratch = [
-        pltpu.SMEM((2 * planes * SLOTS,), jnp.int32),
+        pltpu.SMEM((LSLOTS * 2 * SLOTS,), jnp.int32),
         pltpu.VMEM((CHUNK + 8, E), jnp.float32),
-        pltpu.SemaphoreType.DMA((planes,)),
+        pltpu.SemaphoreType.DMA((LSLOTS,)),
     ]
     if widen:
         table = pltpu.with_memory_space_constraint(table, pltpu.HBM)

time: 140 us -> 138 us (0.986)
  Pallas kernels: 44.1 us -> 39.3 us
  waiting for transfers between devices: 29.3 us -> 32 us
    pallas_call x5, Pallas kernels: 34.7 us -> 29.8 us  [gather(): pl.pallas_call(functools.partial(gather_body, unroll=unroll, widen=widen,...]
    ppermute x7, waiting for transfers between devices: 14.2 us -> 16.9 us  [along(): lax.ppermute(x, 'dev', [(d, d // ring * ring + (d + k) % ring) for d in r...]
  transfers between devices with their start and end apart: 12 -> 12, of which waited for: 8 -> 9; matrix products, arithmetic and copies ran while one was open for 0% -> 0% of each run, Pallas kernels for 31% -> 28%
where the time goes in v9:
time: 138 us; the launch traced here: 137 us
  Pallas kernels  39.3 us (28%)
  waiting for transfers between devices  32 us (23%)
  blocking collectives  31.2 us (23%)
  starting transfers between devices  18.4 us (13%)
  between operations  13.6 us (10%)
  other arithmetic  1.6 us (1%)
    pallas_call x5, Pallas kernels, gather(): pl.pallas_call(functools.partial(gather_body, unroll=unroll, widen=widen,...  29.8 us
    all_to_all x1, blocking collectives, body(): lax.all_to_all(pooled, 'dev', 0, 0, axis_index_groups=levels, tiled=True)  18.7 us
    ppermute x7, waiting for transfers between devices, along(): lax.ppermute(x, 'dev', [(d, d // ring * ring + (d + k) % ring) for d in r...  16.9 us
    all_to_all x1, waiting for transfers between devices, body(): lax.all_to_all(lists.reshape(n_sec * n_dev, 4, 128), both_axes, 0, 0, til...  11.8 us
    all_to_all x2, blocking collectives, swap(): lax.all_to_all(jnp.broadcast_to(x[None], (2, *x.shape)), axis, 0, 0, tile...  10.6 us
    ppermute x7, starting transfers between devices, along(): lax.ppermute(x, 'dev', [(d, d // ring * ring + (d + k) % ring) for d in r...  8.21 us
    all_to_all x1, starting transfers between devices, body(): lax.all_to_all(lists.reshape(n_sec * n_dev, 4, 128), both_axes, 0, 0, til...  8 us
    pallas_call x2, Pallas kernels, dense(): pl.pallas_call(functools.partial(dense_body, stream=stream), out_shape=(o...  5.23 us
  transfers between devices with their start and end apart: 12, of which 9 were waited for; matrix products, arithmetic and copies ran while one was open for 0% of the time, Pallas kernels for 28%

profile of v9, /device:TPU:1, one launch (start us, length us, event | category | flops | bytes accessed | tf_op | source)
XLA Modules:
  0.0 137.3 jit_solution(9877421262552752587)
XLA Ops:
  6.5 1.0 constant_dynamic-slice_fusion.1
  7.5 3.6 %collective-permute-start.7 = (bf16[64,1024]{1,0:T(8,128)(2,1)S(1)}, bf16[64,1024]{1,0:T(8,128)(2,1)S(1)}, u32[]{:S(2)}, u32[]{:S(2)}) collective-permute-start(bf16[64,1024]{1,0:T(8,128)(2,1)S(1)} %get-tuple-element.30), channel_id=1, source_target_pairs={{0,3},{1,0},{2,1},{3,2},{4,7},{5,4},{6,5},{7,6},{8,11},{9,8},{10,9... | collective-permute-start | bytes 393224 | tf_op jit(solution)/shard_map/ppermute | solution.py:332
  12.2 4.0 %collective-permute-done.7 = bf16[64,1024]{1,0:T(8,128)(2,1)S(1)} collective-permute-done((bf16[64,1024]{1,0:T(8,128)(2,1)S(1)}, bf16[64,1024]{1,0:T(8,128)(2,1)S(1)}, u32[]{:S(2)}, u32[]{:S(2)}) %collective-permute-start.7) | collective-permute-done | bytes 131104 | tf_op jit(solution)/shard_map/ppermute | solution.py:332
  16.6 4.2 %collective-permute-done.5 = bf16[64,1024]{1,0:T(8,128)(2,1)S(1)} collective-permute-done((bf16[64,1024]{1,0:T(8,128)(2,1)S(1)}, bf16[64,1024]{1,0:T(8,128)(2,1)S(1)}, u32[]{:S(2)}, u32[]{:S(2)}) %collective-permute-start.5) | collective-permute-done | bytes 131104 | tf_op jit(solution)/shard_map/ppermute | solution.py:332
  20.9 0.9 pad_maximum_fusion.1
  21.8 3.3 %bag_lists.1 = s32[512,128]{1,0:T(8,128)} custom-call(s32[32,8,64]{2,1,0:T(8,128)} %bitcast.38, s32[32]{0:T(128)} %pool_ref.1), custom_call_target="tpu_custom_call" | custom-call | tf_op jit(solution)/shard_map/bag_lists/pallas_call | solution.py:109
  25.1 8.0 %all-to-all-start = ((s32[128,4,128]{2,1,0:T(4,128)}), s32[128,4,128]{2,1,0:T(4,128)S(1)}, u32[]{:S(2)}, u32[]{:S(2)}) async-start(s32[128,4,128]{2,1,0:T(4,128)} %bitcast.2), calls=%async_computation | async-start | bytes 524288 | tf_op jit(solution)/shard_map/all_to_all | solution.py:339
  33.1 11.8 %all-to-all-done.lists_ref = s32[128,4,128]{2,1,0:T(4,128)S(1)} async-done(((s32[128,4,128]{2,1,0:T(4,128)}), s32[128,4,128]{2,1,0:T(4,128)S(1)}, u32[]{:S(2)}, u32[]{:S(2)}) %all-to-all-start) | async-done | bytes 262176 | tf_op jit(solution)/shard_map/all_to_all | solution.py:339
  45.0 10.7 %bag_gather.5 = (bf16[32,64,128]{2,1,0:T(8,128)(2,1)S(1)}, f32[32776,128]{1,0:T(8,128)S(1)}) custom-call(s32[1]{0:T(128)} %bitcast.y_ref, s32[65536]{0:T(1024)S(1)} %bitcast.24, bf16[32768,128]{1,0:T(8,128)(2,1)} %refs_0_), custom_call_target="tpu_custom_call" | custom-call | tf_op jit(solution)/shard_map/bag_gather/pallas_call | solution.py:202
  55.7 6.3 %bag_gather.7 = bf16[32,64,128]{2,1,0:T(8,128)(2,1)S(1)} custom-call(s32[1]{0:T(128)} %bitcast.y_ref, s32[65536]{0:T(1024)S(1)} %bitcast.25, f32[32776,128]{1,0:T(8,128)S(1)} %get-tuple-element.17.refs_0_), custom_call_target="tpu_custom_call" | custom-call | tf_op jit(solution)/shard_map/bag_gather/pallas_call | solution.py:202
  62.3 3.1 %collective-permute-start.1 = (bf16[32,64,128]{2,1,0:T(8,128)(2,1)S(1)}, bf16[32,64,128]{2,1,0:T(8,128)(2,1)S(1)}, u32[]{:S(2)}, u32[]{:S(2)}) collective-permute-start(bf16[32,64,128]{2,1,0:T(8,128)(2,1)S(1)} %get-tuple-element.18), channel_id=1, source_target_pairs={{0,2},{1,3},{2,0},{3,1},{4,6},{5,7},{6,4},{7,5},{8,10},{9,11},{10,... | collective-permute-start | bytes 1572872 | tf_op jit(solution)/shard_map/ppermute | solution.py:332
  65.4 3.4 %bag_gather.8 = bf16[16,64,128]{2,1,0:T(8,128)(2,1)S(1)} custom-call(s32[1]{0:T(128)} %bitcast.y_ref, s32[65536]{0:T(1024)S(1)} %bitcast.26, f32[32776,128]{1,0:T(8,128)S(1)} %get-tuple-element.17.refs_0_), custom_call_target="tpu_custom_call" | custom-call | tf_op jit(solution)/shard_map/bag_gather/pallas_call | solution.py:202
  68.8 3.4 %bag_gather.9 = bf16[16,64,128]{2,1,0:T(8,128)(2,1)S(1)} custom-call(s32[1]{0:T(128)} %bitcast.y_ref, s32[65536]{0:T(1024)S(1)} %bitcast.27, f32[32776,128]{1,0:T(8,128)S(1)} %get-tuple-element.17.refs_0_), custom_call_target="tpu_custom_call" | custom-call | tf_op jit(solution)/shard_map/bag_gather/pallas_call | solution.py:202
  72.4 6.1 %bag_gather.6.part_0 = bf16[32,64,128]{2,1,0:T(8,128)(2,1)S(1)} custom-call(s32[1]{0:T(128)} %bitcast.y_ref, s32[65536]{0:T(1024)S(1)} %bitcast.28, f32[32776,128]{1,0:T(8,128)S(1)} %get-tuple-element.17.refs_0_), custom_call_target="tpu_custom_call" | custom-call | tf_op jit(solution)/shard_map/bag_gather/pallas_call | solution.py:202
  78.5 2.7 %collective-permute-done.2.part_3 = bf16[16,64,128]{2,1,0:T(8,128)(2,1)S(1)} collective-permute-done((bf16[16,64,128]{2,1,0:T(8,128)(2,1)S(1)}, bf16[16,64,128]{2,1,0:T(8,128)(2,1)S(1)}, u32[]{:S(2)}, u32[]{:S(2)}) %collective-permute-start.2) | collective-permute-done | bytes 262176 | tf_op jit(solution)/shard_map/ppermute | solution.py:332
  81.1 5.6 %collective-permute-done.3.part_3b = bf16[16,64,128]{2,1,0:T(8,128)(2,1)S(1)} collective-permute-done((bf16[16,64,128]{2,1,0:T(8,128)(2,1)S(1)}, bf16[16,64,128]{2,1,0:T(8,128)(2,1)S(1)}, u32[]{:S(2)}, u32[]{:S(2)}) %collective-permute-start.3) | collective-permute-done | bytes 262176 | tf_op jit(solution)/shard_map/ppermute | solution.py:332
  87.6 18.7 %all_to_all.20.pooled_ref = bf16[16,128,128]{2,1,0:T(8,128)(2,1)S(1)} all-to-all(bf16[16,128,128]{2,1,0:T(8,128)(2,1)S(1)} %bitcast.29), channel_id=1, replica_groups={{0,4,8,12,16,20,24,28,32,36,40,44,48,52,56,60},{1,5,9,13,17,21,25,29,33..., dimensions={0} | all-to-all | bytes 1048576 | tf_op jit(solution)/shard_map/all_to_all | solution.py:355
  106.7 5.0 %all_to_all.21.both_ref = bf16[2,128,2048]{2,1,0:T(8,128)(2,1)S(1)} all-to-all(bf16[2,128,2048]{2,1,0:T(8,128)(2,1)S(1)} %broadcast_in_dim.4), channel_id=1, replica_groups=mesh['section'=2,'dev'=64] {'section'}, dimensions={0} | all-to-all | bytes 2097152 | tf_op jit(solution)/shard_map/all_to_all | solution.py:313
  111.7 3.9 %dense_near.1 = (f32[1,128]{1,0:T(1,128)S(1)}, bf16[4096,1024]{1,0:T(8,128)(2,1)S(1)}) custom-call(bf16[2,128,2048]{2,1,0:T(8,128)(2,1)S(1)} %all_to_all.21.both_ref, bf16[4096,1024]{1,0:T(8,128)(2,1)} %all-gather.3.cloned.1.call-done.w_ref, f32[1,1024]{1,0:T(1,128)S(1)} %bitcast.32, f32[1,1024]{1,0:T(1,128)S(1)} %bitcast.30), custom_call_target="tpu_custom_call" | custom-call | tf_op jit(solution)/shard_map/dense_near/pallas_call | solution.py:301
  115.5 1.8 %all-gather = f32[2,1,128]{2,1,0:T(1,128)S(1)} all-gather(f32[1,1,128]{2,1,0:T(1,128)S(1)} %bitcast.36), channel_id=1, replica_groups=mesh['section'=2,'dev'=64] {'section'}, dimensions={0}, use_global_device_ids=true | all-gather | bytes 1536 | tf_op jit(solution)/shard_map/all_gather | solution.py:362
  117.4 2.0 %collective-permute-done.4 = bf16[128,2048]{1,0:T(8,128)(2,1)S(1)} collective-permute-done((bf16[128,2048]{1,0:T(8,128)(2,1)S(1)}, bf16[128,2048]{1,0:T(8,128)(2,1)S(1)}, u32[]{:S(2)}, u32[]{:S(2)}) %collective-permute-start.4) | collective-permute-done | bytes 524320 | tf_op jit(solution)/shard_map/ppermute | solution.py:359
  119.5 5.7 %all_to_all.22.both_ref = bf16[2,128,2048]{2,1,0:T(8,128)(2,1)S(1)} all-to-all(bf16[2,128,2048]{2,1,0:T(8,128)(2,1)S(1)} %broadcast_in_dim.5), channel_id=1, replica_groups=mesh['section'=2,'dev'=64] {'section'}, dimensions={0} | all-to-all | bytes 2097152 | tf_op jit(solution)/shard_map/all_to_all | solution.py:313
  125.2 1.4 dense_far.1
  126.6 2.0 %collective-permute-start.9 = (f32[128]{0:T(128)S(1)}, f32[128]{0:T(128)S(1)}, u32[]{:S(2)}, u32[]{:S(2)}) collective-permute-start(f32[128]{0:T(128)S(1)} %bitcast.35), channel_id=1, source_target_pairs={{0,65},{1,64},{2,67},{3,66},{4,69},{5,68},{6,71},{7,70},{8,73},{9,... | collective-permute-start | bytes 1544 | tf_op jit(solution)/shard_map/ppermute | solution.py:369
  (29 shorter events, 5.4 us)
Async XLA Ops:
  6.5 105.1 %all-gather.3.cloned.1.call-start = ((), (), s32[]{:S(2)}) async-start(), calls=%async_computation.4 | async-start | bytes 8912896 | tf_op jit(solution)/shard_map/all_gather | solution.py:337
  7.5 8.7 %collective-permute-start.7 = (bf16[64,1024]{1,0:T(8,128)(2,1)S(1)}, bf16[64,1024]{1,0:T(8,128)(2,1)S(1)}, u32[]{:S(2)}, u32[]{:S(2)}) collective-permute-start(bf16[64,1024]{1,0:T(8,128)(2,1)S(1)} %get-tuple-element.30), channel_id=1, source_target_pairs={{0,3},{1,0},{2,1},{3,2},{4,7},{5,4},{6,5},{7,6},{8,11},{9,8},{10,9... | collective-permute-start | bytes 393224 | tf_op jit(solution)/shard_map/ppermute | solution.py:332
  11.1 5.4 %collective-permute-start.6 = (bf16[64,1024]{1,0:T(8,128)(2,1)S(1)}, bf16[64,1024]{1,0:T(8,128)(2,1)S(1)}, u32[]{:S(2)}, u32[]{:S(2)}) collective-permute-start(bf16[64,1024]{1,0:T(8,128)(2,1)S(1)} %get-tuple-element.29), channel_id=1, source_target_pairs={{0,2},{1,3},{2,0},{3,1},{4,6},{5,7},{6,4},{7,5},{8,10},{9,11},{10,... | collective-permute-start | bytes 393224 | tf_op jit(solution)/shard_map/ppermute | solution.py:332
  11.5 9.3 %collective-permute-start.5 = (bf16[64,1024]{1,0:T(8,128)(2,1)S(1)}, bf16[64,1024]{1,0:T(8,128)(2,1)S(1)}, u32[]{:S(2)}, u32[]{:S(2)}) collective-permute-start(bf16[64,1024]{1,0:T(8,128)(2,1)S(1)} %get-tuple-element.30), channel_id=1, source_target_pairs={{0,1},{1,2},{2,3},{3,0},{4,5},{5,6},{6,7},{7,4},{8,9},{9,10},{10,1... | collective-permute-start | bytes 393224 | tf_op jit(solution)/shard_map/ppermute | solution.py:332
  25.1 19.8 %all-to-all-start = ((s32[128,4,128]{2,1,0:T(4,128)}), s32[128,4,128]{2,1,0:T(4,128)S(1)}, u32[]{:S(2)}, u32[]{:S(2)}) async-start(s32[128,4,128]{2,1,0:T(4,128)} %bitcast.2), calls=%async_computation | async-start | bytes 524288 | tf_op jit(solution)/shard_map/all_to_all | solution.py:339
  62.0 24.7 %collective-permute-start = (bf16[32,64,128]{2,1,0:T(8,128)(2,1)S(1)}, bf16[32,64,128]{2,1,0:T(8,128)(2,1)S(1)}, u32[]{:S(2)}, u32[]{:S(2)}) collective-permute-start(bf16[32,64,128]{2,1,0:T(8,128)(2,1)S(1)} %bag_gather.7), channel_id=1, source_target_pairs={{0,1},{1,2},{2,3},{3,0},{4,5},{5,6},{6,7},{7,4},{8,9},{9,10},{10,1... | collective-permute-start | bytes 1572872 | tf_op jit(solution)/shard_map/ppermute | solution.py:332
  62.3 24.4 %collective-permute-start.1 = (bf16[32,64,128]{2,1,0:T(8,128)(2,1)S(1)}, bf16[32,64,128]{2,1,0:T(8,128)(2,1)S(1)}, u32[]{:S(2)}, u32[]{:S(2)}) collective-permute-start(bf16[32,64,128]{2,1,0:T(8,128)(2,1)S(1)} %get-tuple-element.18), channel_id=1, source_target_pairs={{0,2},{1,3},{2,0},{3,1},{4,6},{5,7},{6,4},{7,5},{8,10},{9,11},{10,... | collective-permute-start | bytes 1572872 | tf_op jit(solution)/shard_map/ppermute | solution.py:332
  72.2 34.4 %copy-start = (bf16[2048]{0:T(1024)(128)(2,1)S(1)}, bf16[2048]{0:T(1024)(128)(2,1)}, u32[]{:S(2)}) copy-start(bf16[2048]{0:T(1024)(128)(2,1)} %param.11) | copy-start | bytes 12292
  72.2 34.4 %copy-start.1 = (bf16[2048]{0:T(1024)(128)(2,1)S(1)}, bf16[2048]{0:T(1024)(128)(2,1)}, u32[]{:S(2)}) copy-start(bf16[2048]{0:T(1024)(128)(2,1)} %param.10) | copy-start | bytes 12292
  72.2 8.9 %collective-permute-start.2 = (bf16[16,64,128]{2,1,0:T(8,128)(2,1)S(1)}, bf16[16,64,128]{2,1,0:T(8,128)(2,1)S(1)}, u32[]{:S(2)}, u32[]{:S(2)}) collective-permute-start(bf16[16,64,128]{2,1,0:T(8,128)(2,1)S(1)} %bag_gather.8), channel_id=1, source_target_pairs={{0,3},{1,0},{2,1},{3,2},{4,7},{5,4},{6,5},{7,6},{8,11},{9,8},{10,9... | collective-permute-start | bytes 786440 | tf_op jit(solution)/shard_map/ppermute | solution.py:332
  72.3 14.5 %collective-permute-start.3 = (bf16[16,64,128]{2,1,0:T(8,128)(2,1)S(1)}, bf16[16,64,128]{2,1,0:T(8,128)(2,1)S(1)}, u32[]{:S(2)}, u32[]{:S(2)}) collective-permute-start(bf16[16,64,128]{2,1,0:T(8,128)(2,1)S(1)} %bag_gather.9), channel_id=1, source_target_pairs={{0,3},{1,0},{2,1},{3,2},{4,7},{5,4},{6,5},{7,6},{8,11},{9,8},{10,9... | collective-permute-start | bytes 786440 | tf_op jit(solution)/shard_map/ppermute | solution.py:332
  106.5 12.9 %collective-permute-start.4 = (bf16[128,2048]{1,0:T(8,128)(2,1)S(1)}, bf16[128,2048]{1,0:T(8,128)(2,1)S(1)}, u32[]{:S(2)}, u32[]{:S(2)}) collective-permute-start(bf16[128,2048]{1,0:T(8,128)(2,1)S(1)} %feature_rows.1), channel_id=1, source_target_pairs={{0,1},{1,0},{2,3},{3,2},{4,5},{5,4},{6,7},{7,6},{8,9},{9,8},{10,11... | collective-permute-start | bytes 1572872 | tf_op jit(solution)/shard_map/ppermute | solution.py:359
  126.6 2.5 %collective-permute-start.8 = (f32[128]{0:T(128)S(1)}, f32[128]{0:T(128)S(1)}, u32[]{:S(2)}, u32[]{:S(2)}) collective-permute-start(f32[128]{0:T(128)S(1)} %bitcast.34), channel_id=1, source_target_pairs={{0,1},{1,0},{2,3},{3,2},{4,5},{5,4},{6,7},{7,6},{8,9},{9,8},{10,11... | collective-permute-start | bytes 1544 | tf_op jit(solution)/shard_map/ppermute | solution.py:369
  126.6 3.2 %collective-permute-start.9 = (f32[128]{0:T(128)S(1)}, f32[128]{0:T(128)S(1)}, u32[]{:S(2)}, u32[]{:S(2)}) collective-permute-start(f32[128]{0:T(128)S(1)} %bitcast.35), channel_id=1, source_target_pairs={{0,65},{1,64},{2,67},{3,66},{4,69},{5,68},{6,71},{7,70},{8,73},{9,... | collective-permute-start | bytes 1544 | tf_op jit(solution)/shard_map/ppermute | solution.py:369
Sparse Core Ops, SparseCore 0:
  22.0 72.8 all-gather.2

commit v10 on v9

--- a/solution.py
+++ b/solution.py
@@ -332,6 +332,7 @@
         return lax.ppermute(x, "dev", [(d, d // ring * ring + (d + k) % ring) for d in range(n_dev)])
 
     pieces = [keep, along(give, 1), along(keep, 2), along(give, 3)]
+    pieces, lists = lax.optimization_barrier((pieces, lists))
     pieces = jnp.stack(pieces)
     pieces = [lax.dynamic_index_in_dim(pieces, (y - k) % ring, 0, False) for k in range(ring)]
     whole = lax.all_gather(jnp.concatenate(pieces), "dev", axis_index_groups=levels, tiled=True)
@@ -359,16 +360,15 @@
     far = lax.ppermute(features, "dev", [(d, d ^ 1) for d in range(n_dev)])
     bias, scale = bias.reshape(1, part), scale.reshape(1, part)
     near, kept = dense(swap(features, "section"), whole, bias, scale, True)
-    near = lax.all_gather(near.reshape(-1), "section")
+    near = near.reshape(-1)
     far, near = lax.optimization_barrier((far, near))
     far_part = dense(swap(far, "section"), kept, bias, scale, False).reshape(-1)
-    far_part, near = lax.optimization_barrier((far_part, near))
-
-    def to_partner(x, turn):
-        pairs = [(s * n_dev + d, (s ^ turn) * n_dev + (d ^ 1)) for s in range(n_sec) for d in range(n_dev)]
+
+    def moved(x, core, chip):
+        pairs = [(s * n_dev + d, (s ^ core) * n_dev + (d ^ chip)) for s in range(n_sec) for d in range(n_dev)]
         return lax.ppermute(x, both_axes, pairs)
 
-    return (near[0] + near[1]) + (to_partner(far_part, 0) + to_partner(far_part, 1))
+    return (near + moved(near, 1, 0)) + (moved(far_part, 0, 1) + moved(far_part, 1, 1))
 
 
 def solution(mesh):

time: 138 us -> 133 us (0.964)
  waiting for transfers between devices: 32 us -> 24.9 us
  starting transfers between devices: 18.4 us -> 24.9 us
  blocking collectives: 31.2 us -> 26.8 us
    ppermute x7, waiting for transfers between devices: 16.9 us -> 10.2 us  [along(): lax.ppermute(x, 'dev', [(d, d // ring * ring + (d + k) % ring) for d in r...]
    all_to_all x1, blocking collectives: 18.7 us -> 15.3 us  [body(): lax.all_to_all(pooled, 'dev', 0, 0, axis_index_groups=levels, tiled=True)]
    all_to_all x1, starting transfers between devices: 8 us -> 10.9 us  [body(): lax.all_to_all(lists.reshape(n_sec * n_dev, 4, 128), both_axes, 0, 0, til...]
    ppermute x1, starting transfers between devices: 0.09 us -> 2.6 us  [body(): far = lax.ppermute(features, 'dev', [(d, d ^ 1) for d in range(n_dev)])]
    all_gather x1 -> x0, blocking collectives: 1.84 us -> none  [body(): near = lax.all_gather(near.reshape(-1), 'section')]
  transfers between devices with their start and end apart: 12 -> 13, of which waited for: 9 -> 7; matrix products, arithmetic and copies ran while one was open for 0% -> 0% of each run, Pallas kernels for 28% -> 29%
where the time goes in v10:
time: 133 us; the launch traced here: 132 us
  Pallas kernels  39.4 us (30%)
  blocking collectives  26.8 us (20%)
  starting transfers between devices  24.9 us (19%)
  waiting for transfers between devices  24.9 us (19%)
  between operations  13.5 us (10%)
  other arithmetic  1.6 us (1%)
    pallas_call x5, Pallas kernels, gather(): pl.pallas_call(functools.partial(gather_body, unroll=unroll, widen=widen,...  29.9 us
    all_to_all x1, blocking collectives, body(): lax.all_to_all(pooled, 'dev', 0, 0, axis_index_groups=levels, tiled=True)  15.3 us
    all_to_all x2, blocking collectives, swap(): lax.all_to_all(jnp.broadcast_to(x[None], (2, *x.shape)), axis, 0, 0, tile...  11.5 us
    all_to_all x1, starting transfers between devices, body(): lax.all_to_all(lists.reshape(n_sec * n_dev, 4, 128), both_axes, 0, 0, til...  10.9 us
    all_to_all x1, waiting for transfers between devices, body(): lax.all_to_all(lists.reshape(n_sec * n_dev, 4, 128), both_axes, 0, 0, til...  10.8 us
    ppermute x7, waiting for transfers between devices, along(): lax.ppermute(x, 'dev', [(d, d // ring * ring + (d + k) % ring) for d in r...  10.2 us
    ppermute x7, starting transfers between devices, along(): lax.ppermute(x, 'dev', [(d, d // ring * ring + (d + k) % ring) for d in r...  9.19 us
    pallas_call x2, Pallas kernels, dense(): pl.pallas_call(functools.partial(dense_body, stream=stream), out_shape=(o...  5.23 us
  transfers between devices with their start and end apart: 13, of which 7 were waited for; matrix products, arithmetic and copies ran while one was open for 0% of the time, Pallas kernels for 29%

profile of v10, /device:TPU:1, one launch (start us, length us, event | category | flops | bytes accessed | tf_op | source)
XLA Modules:
  0.0 132.4 jit_solution(17630932410387140631)
XLA Ops:
  7.5 2.2 %collective-permute-start = (bf16[64,1024]{1,0:T(8,128)(2,1)S(1)}, bf16[64,1024]{1,0:T(8,128)(2,1)S(1)}, u32[]{:S(2)}, u32[]{:S(2)}) collective-permute-start(bf16[64,1024]{1,0:T(8,128)(2,1)S(1)} %get-tuple-element.35), channel_id=1, source_target_pairs={{0,1},{1,2},{2,3},{3,0},{4,5},{5,6},{6,7},{7,4},{8,9},{9,10},{10,1... | collective-permute-start | bytes 393224 | tf_op jit(solution)/shard_map/ppermute | solution.py:332
  9.7 2.6 %collective-permute-start.1 = (bf16[64,1024]{1,0:T(8,128)(2,1)S(1)}, bf16[64,1024]{1,0:T(8,128)(2,1)S(1)}, u32[]{:S(2)}, u32[]{:S(2)}) collective-permute-start(bf16[64,1024]{1,0:T(8,128)(2,1)S(1)} %get-tuple-element.23), channel_id=1, source_target_pairs={{0,2},{1,3},{2,0},{3,1},{4,6},{5,7},{6,4},{7,5},{8,10},{9,11},{10,... | collective-permute-start | bytes 393224 | tf_op jit(solution)/shard_map/ppermute | solution.py:332
  13.4 3.3 %bag_lists.1 = s32[512,128]{1,0:T(8,128)} custom-call(s32[32,8,64]{2,1,0:T(8,128)} %bitcast.36, s32[32]{0:T(128)} %pool_ref.1), custom_call_target="tpu_custom_call" | custom-call | tf_op jit(solution)/shard_map/bag_lists/pallas_call | solution.py:109
  16.7 1.4 %collective-permute-done.1 = bf16[64,1024]{1,0:T(8,128)(2,1)S(1)} collective-permute-done((bf16[64,1024]{1,0:T(8,128)(2,1)S(1)}, bf16[64,1024]{1,0:T(8,128)(2,1)S(1)}, u32[]{:S(2)}, u32[]{:S(2)}) %collective-permute-start.1) | collective-permute-done | bytes 131104 | tf_op jit(solution)/shard_map/ppermute | solution.py:332
  19.1 10.9 %all-to-all-start = ((s32[128,4,128]{2,1,0:T(4,128)}), s32[128,4,128]{2,1,0:T(4,128)S(1)}, u32[]{:S(2)}, u32[]{:S(2)}) async-start(s32[128,4,128]{2,1,0:T(4,128)} %bitcast.2), calls=%async_computation | async-start | bytes 524288 | tf_op jit(solution)/shard_map/all_to_all | solution.py:340
  30.0 10.8 %all-to-all-done.lists_ref = s32[128,4,128]{2,1,0:T(4,128)S(1)} async-done(((s32[128,4,128]{2,1,0:T(4,128)}), s32[128,4,128]{2,1,0:T(4,128)S(1)}, u32[]{:S(2)}, u32[]{:S(2)}) %all-to-all-start) | async-done | bytes 262176 | tf_op jit(solution)/shard_map/all_to_all | solution.py:340
  40.9 10.8 %bag_gather.5 = (bf16[32,64,128]{2,1,0:T(8,128)(2,1)S(1)}, f32[32776,128]{1,0:T(8,128)S(1)}) custom-call(s32[1]{0:T(128)} %bitcast.y_ref, s32[65536]{0:T(1024)S(1)} %bitcast.21, bf16[32768,128]{1,0:T(8,128)(2,1)} %refs_0_), custom_call_target="tpu_custom_call" | custom-call | tf_op jit(solution)/shard_map/bag_gather/pallas_call | solution.py:202
  51.7 6.3 %bag_gather.7 = bf16[32,64,128]{2,1,0:T(8,128)(2,1)S(1)} custom-call(s32[1]{0:T(128)} %bitcast.y_ref, s32[65536]{0:T(1024)S(1)} %bitcast.22, f32[32776,128]{1,0:T(8,128)S(1)} %get-tuple-element.21.refs_0_), custom_call_target="tpu_custom_call" | custom-call | tf_op jit(solution)/shard_map/bag_gather/pallas_call | solution.py:202
  58.2 1.9 %collective-permute-start.4 = (bf16[32,64,128]{2,1,0:T(8,128)(2,1)S(1)}, bf16[32,64,128]{2,1,0:T(8,128)(2,1)S(1)}, u32[]{:S(2)}, u32[]{:S(2)}) collective-permute-start(bf16[32,64,128]{2,1,0:T(8,128)(2,1)S(1)} %get-tuple-element.22), channel_id=1, source_target_pairs={{0,2},{1,3},{2,0},{3,1},{4,6},{5,7},{6,4},{7,5},{8,10},{9,11},{10,... | collective-permute-start | bytes 1572872 | tf_op jit(solution)/shard_map/ppermute | solution.py:332
  60.0 3.4 %bag_gather.8 = bf16[16,64,128]{2,1,0:T(8,128)(2,1)S(1)} custom-call(s32[1]{0:T(128)} %bitcast.y_ref, s32[65536]{0:T(1024)S(1)} %bitcast.23, f32[32776,128]{1,0:T(8,128)S(1)} %get-tuple-element.21.refs_0_), custom_call_target="tpu_custom_call" | custom-call | tf_op jit(solution)/shard_map/bag_gather/pallas_call | solution.py:202
  63.5 3.4 %bag_gather.9 = bf16[16,64,128]{2,1,0:T(8,128)(2,1)S(1)} custom-call(s32[1]{0:T(128)} %bitcast.y_ref, s32[65536]{0:T(1024)S(1)} %bitcast.24, f32[32776,128]{1,0:T(8,128)S(1)} %get-tuple-element.21.refs_0_), custom_call_target="tpu_custom_call" | custom-call | tf_op jit(solution)/shard_map/bag_gather/pallas_call | solution.py:202
  66.8 1.1 collective-permute-start.5
  68.1 6.1 %bag_gather.6.part_0 = bf16[32,64,128]{2,1,0:T(8,128)(2,1)S(1)} custom-call(s32[1]{0:T(128)} %bitcast.y_ref, s32[65536]{0:T(1024)S(1)} %bitcast.25, f32[32776,128]{1,0:T(8,128)S(1)} %get-tuple-element.21.refs_0_), custom_call_target="tpu_custom_call" | custom-call | tf_op jit(solution)/shard_map/bag_gather/pallas_call | solution.py:202
  74.2 3.2 %collective-permute-done.5.part_3 = bf16[16,64,128]{2,1,0:T(8,128)(2,1)S(1)} collective-permute-done((bf16[16,64,128]{2,1,0:T(8,128)(2,1)S(1)}, bf16[16,64,128]{2,1,0:T(8,128)(2,1)S(1)}, u32[]{:S(2)}, u32[]{:S(2)}) %collective-permute-start.5) | collective-permute-done | bytes 262176 | tf_op jit(solution)/shard_map/ppermute | solution.py:332
  77.4 5.6 %collective-permute-done.6.part_3b = bf16[16,64,128]{2,1,0:T(8,128)(2,1)S(1)} collective-permute-done((bf16[16,64,128]{2,1,0:T(8,128)(2,1)S(1)}, bf16[16,64,128]{2,1,0:T(8,128)(2,1)S(1)}, u32[]{:S(2)}, u32[]{:S(2)}) %collective-permute-start.6) | collective-permute-done | bytes 262176 | tf_op jit(solution)/shard_map/ppermute | solution.py:332
  83.9 15.3 %all_to_all.20.pooled_ref = bf16[16,128,128]{2,1,0:T(8,128)(2,1)S(1)} all-to-all(bf16[16,128,128]{2,1,0:T(8,128)(2,1)S(1)} %bitcast.26), channel_id=1, replica_groups={{0,4,8,12,16,20,24,28,32,36,40,44,48,52,56,60},{1,5,9,13,17,21,25,29,33..., dimensions={0} | all-to-all | bytes 1048576 | tf_op jit(solution)/shard_map/all_to_all | solution.py:356
  99.3 2.6 %collective-permute-start.7 = (bf16[128,2048]{1,0:T(8,128)(2,1)S(1)}, bf16[128,2048]{1,0:T(8,128)(2,1)S(1)}, u32[]{:S(2)}, u32[]{:S(2)}) collective-permute-start(bf16[128,2048]{1,0:T(8,128)(2,1)S(1)} %feature_rows.1), channel_id=1, source_target_pairs={{0,1},{1,0},{2,3},{3,2},{4,5},{5,4},{6,7},{7,6},{8,9},{9,8},{10,11... | collective-permute-start | bytes 1572872 | tf_op jit(solution)/shard_map/ppermute | solution.py:360
  102.0 5.3 %all_to_all.21.both_ref = bf16[2,128,2048]{2,1,0:T(8,128)(2,1)S(1)} all-to-all(bf16[2,128,2048]{2,1,0:T(8,128)(2,1)S(1)} %broadcast_in_dim.4), channel_id=1, replica_groups=mesh['section'=2,'dev'=64] {'section'}, dimensions={0} | all-to-all | bytes 2097152 | tf_op jit(solution)/shard_map/all_to_all | solution.py:313
  107.4 3.9 %dense_near.1 = (f32[1,128]{1,0:T(1,128)S(1)}, bf16[4096,1024]{1,0:T(8,128)(2,1)S(1)}) custom-call(bf16[2,128,2048]{2,1,0:T(8,128)(2,1)S(1)} %all_to_all.21.both_ref, bf16[4096,1024]{1,0:T(8,128)(2,1)} %all-gather.2.cloned.1.call-done.w_ref, f32[1,1024]{1,0:T(1,128)S(1)} %bitcast.29, f32[1,1024]{1,0:T(1,128)S(1)} %bitcast.27), custom_call_target="tpu_custom_call" | custom-call | tf_op jit(solution)/shard_map/dense_near/pallas_call | solution.py:301
  111.3 1.6 %collective-permute-done.7 = bf16[128,2048]{1,0:T(8,128)(2,1)S(1)} collective-permute-done((bf16[128,2048]{1,0:T(8,128)(2,1)S(1)}, bf16[128,2048]{1,0:T(8,128)(2,1)S(1)}, u32[]{:S(2)}, u32[]{:S(2)}) %collective-permute-start.7) | collective-permute-done | bytes 524320 | tf_op jit(solution)/shard_map/ppermute | solution.py:360
  112.9 6.2 %all_to_all.22.both_ref = bf16[2,128,2048]{2,1,0:T(8,128)(2,1)S(1)} all-to-all(bf16[2,128,2048]{2,1,0:T(8,128)(2,1)S(1)} %broadcast_in_dim.5), channel_id=1, replica_groups=mesh['section'=2,'dev'=64] {'section'}, dimensions={0} | all-to-all | bytes 2097152 | tf_op jit(solution)/shard_map/all_to_all | solution.py:313
  119.1 1.4 %dense_far.1 = f32[1,128]{1,0:T(1,128)S(1)} custom-call(bf16[2,128,2048]{2,1,0:T(8,128)(2,1)S(1)} %all_to_all.22.both_ref, bf16[4096,1024]{1,0:T(8,128)(2,1)S(1)} %get-tuple-element.30.w_ref, f32[1,1024]{1,0:T(1,128)S(1)} %bitcast.30, f32[1,1024]{1,0:T(1,128)S(1)} %bitcast.28), custom_call_target="tpu_custom_call" | custom-call | tf_op jit(solution)/shard_map/dense_far/pallas_call | solution.py:301
  120.5 1.5 %collective-permute-start.9 = (f32[128]{0:T(128)S(1)}, f32[128]{0:T(128)S(1)}, u32[]{:S(2)}, u32[]{:S(2)}) collective-permute-start(f32[128]{0:T(128)S(1)} %bitcast.31), channel_id=1, source_target_pairs={{0,1},{1,0},{2,3},{3,2},{4,5},{5,4},{6,7},{7,6},{8,9},{9,8},{10,11... | collective-permute-start | bytes 1544 | tf_op jit(solution)/shard_map/ppermute | solution.py:369
  123.0 2.0 %collective-permute-done.10 = f32[128]{0:T(128)S(1)} collective-permute-done((f32[128]{0:T(128)S(1)}, f32[128]{0:T(128)S(1)}, u32[]{:S(2)}, u32[]{:S(2)}) %collective-permute-start.10) | collective-permute-done | bytes 544 | tf_op jit(solution)/shard_map/ppermute | solution.py:369
  (30 shorter events, 6.3 us)
Async XLA Ops:
  6.5 100.8 %all-gather.2.cloned.1.call-start = ((), (), s32[]{:S(2)}) async-start(), calls=%async_computation.4 | async-start | bytes 8912896 | tf_op jit(solution)/shard_map/all_gather | solution.py:338
  7.5 9.1 %collective-permute-start = (bf16[64,1024]{1,0:T(8,128)(2,1)S(1)}, bf16[64,1024]{1,0:T(8,128)(2,1)S(1)}, u32[]{:S(2)}, u32[]{:S(2)}) collective-permute-start(bf16[64,1024]{1,0:T(8,128)(2,1)S(1)} %get-tuple-element.35), channel_id=1, source_target_pairs={{0,1},{1,2},{2,3},{3,0},{4,5},{5,6},{6,7},{7,4},{8,9},{9,10},{10,1... | collective-permute-start | bytes 393224 | tf_op jit(solution)/shard_map/ppermute | solution.py:332
  9.7 8.3 %collective-permute-start.1 = (bf16[64,1024]{1,0:T(8,128)(2,1)S(1)}, bf16[64,1024]{1,0:T(8,128)(2,1)S(1)}, u32[]{:S(2)}, u32[]{:S(2)}) collective-permute-start(bf16[64,1024]{1,0:T(8,128)(2,1)S(1)} %get-tuple-element.23), channel_id=1, source_target_pairs={{0,2},{1,3},{2,0},{3,1},{4,6},{5,7},{6,4},{7,5},{8,10},{9,11},{10,... | collective-permute-start | bytes 393224 | tf_op jit(solution)/shard_map/ppermute | solution.py:332
  12.3 5.7 %collective-permute-start.2 = (bf16[64,1024]{1,0:T(8,128)(2,1)S(1)}, bf16[64,1024]{1,0:T(8,128)(2,1)S(1)}, u32[]{:S(2)}, u32[]{:S(2)}) collective-permute-start(bf16[64,1024]{1,0:T(8,128)(2,1)S(1)} %get-tuple-element.35), channel_id=1, source_target_pairs={{0,3},{1,0},{2,1},{3,2},{4,7},{5,4},{6,5},{7,6},{8,11},{9,8},{10,9... | collective-permute-start | bytes 393224 | tf_op jit(solution)/shard_map/ppermute | solution.py:332
  19.1 21.7 %all-to-all-start = ((s32[128,4,128]{2,1,0:T(4,128)}), s32[128,4,128]{2,1,0:T(4,128)S(1)}, u32[]{:S(2)}, u32[]{:S(2)}) async-start(s32[128,4,128]{2,1,0:T(4,128)} %bitcast.2), calls=%async_computation | async-start | bytes 524288 | tf_op jit(solution)/shard_map/all_to_all | solution.py:340
  58.0 25.0 %collective-permute-start.3 = (bf16[32,64,128]{2,1,0:T(8,128)(2,1)S(1)}, bf16[32,64,128]{2,1,0:T(8,128)(2,1)S(1)}, u32[]{:S(2)}, u32[]{:S(2)}) collective-permute-start(bf16[32,64,128]{2,1,0:T(8,128)(2,1)S(1)} %bag_gather.7), channel_id=1, source_target_pairs={{0,1},{1,2},{2,3},{3,0},{4,5},{5,6},{6,7},{7,4},{8,9},{9,10},{10,1... | collective-permute-start | bytes 1572872 | tf_op jit(solution)/shard_map/ppermute | solution.py:332
  58.2 24.8 %collective-permute-start.4 = (bf16[32,64,128]{2,1,0:T(8,128)(2,1)S(1)}, bf16[32,64,128]{2,1,0:T(8,128)(2,1)S(1)}, u32[]{:S(2)}, u32[]{:S(2)}) collective-permute-start(bf16[32,64,128]{2,1,0:T(8,128)(2,1)S(1)} %get-tuple-element.22), channel_id=1, source_target_pairs={{0,2},{1,3},{2,0},{3,1},{4,6},{5,7},{6,4},{7,5},{8,10},{9,11},{10,... | collective-permute-start | bytes 1572872 | tf_op jit(solution)/shard_map/ppermute | solution.py:332
  66.8 35.1 %copy-start = (bf16[2048]{0:T(1024)(128)(2,1)S(1)}, bf16[2048]{0:T(1024)(128)(2,1)}, u32[]{:S(2)}) copy-start(bf16[2048]{0:T(1024)(128)(2,1)} %param.11) | copy-start | bytes 12292
  66.8 35.1 %copy-start.1 = (bf16[2048]{0:T(1024)(128)(2,1)S(1)}, bf16[2048]{0:T(1024)(128)(2,1)}, u32[]{:S(2)}) copy-start(bf16[2048]{0:T(1024)(128)(2,1)} %param.10) | copy-start | bytes 12292
  66.8 10.5 %collective-permute-start.5 = (bf16[16,64,128]{2,1,0:T(8,128)(2,1)S(1)}, bf16[16,64,128]{2,1,0:T(8,128)(2,1)S(1)}, u32[]{:S(2)}, u32[]{:S(2)}) collective-permute-start(bf16[16,64,128]{2,1,0:T(8,128)(2,1)S(1)} %bag_gather.8), channel_id=1, source_target_pairs={{0,3},{1,0},{2,1},{3,2},{4,7},{5,4},{6,5},{7,6},{8,11},{9,8},{10,9... | collective-permute-start | bytes 786440 | tf_op jit(solution)/shard_map/ppermute | solution.py:332
  67.9 15.1 %collective-permute-start.6 = (bf16[16,64,128]{2,1,0:T(8,128)(2,1)S(1)}, bf16[16,64,128]{2,1,0:T(8,128)(2,1)S(1)}, u32[]{:S(2)}, u32[]{:S(2)}) collective-permute-start(bf16[16,64,128]{2,1,0:T(8,128)(2,1)S(1)} %bag_gather.9), channel_id=1, source_target_pairs={{0,3},{1,0},{2,1},{3,2},{4,7},{5,4},{6,5},{7,6},{8,11},{9,8},{10,9... | collective-permute-start | bytes 786440 | tf_op jit(solution)/shard_map/ppermute | solution.py:332
  99.3 13.5 %collective-permute-start.7 = (bf16[128,2048]{1,0:T(8,128)(2,1)S(1)}, bf16[128,2048]{1,0:T(8,128)(2,1)S(1)}, u32[]{:S(2)}, u32[]{:S(2)}) collective-permute-start(bf16[128,2048]{1,0:T(8,128)(2,1)S(1)} %feature_rows.1), channel_id=1, source_target_pairs={{0,1},{1,0},{2,3},{3,2},{4,5},{5,4},{6,7},{7,6},{8,9},{9,8},{10,11... | collective-permute-start | bytes 1572872 | tf_op jit(solution)/shard_map/ppermute | solution.py:360
  120.5 2.5 %collective-permute-start.9 = (f32[128]{0:T(128)S(1)}, f32[128]{0:T(128)S(1)}, u32[]{:S(2)}, u32[]{:S(2)}) collective-permute-start(f32[128]{0:T(128)S(1)} %bitcast.31), channel_id=1, source_target_pairs={{0,1},{1,0},{2,3},{3,2},{4,5},{5,4},{6,7},{7,6},{8,9},{9,8},{10,11... | collective-permute-start | bytes 1544 | tf_op jit(solution)/shard_map/ppermute | solution.py:369
  122.0 3.0 %collective-permute-start.10 = (f32[128]{0:T(128)S(1)}, f32[128]{0:T(128)S(1)}, u32[]{:S(2)}, u32[]{:S(2)}) collective-permute-start(f32[128]{0:T(128)S(1)} %bitcast.32), channel_id=1, source_target_pairs={{0,65},{1,64},{2,67},{3,66},{4,69},{5,68},{6,71},{7,70},{8,73},{9,... | collective-permute-start | bytes 1544 | tf_op jit(solution)/shard_map/ppermute | solution.py:369
  122.5 2.5 %collective-permute-start.8 = (f32[128]{0:T(128)S(1)}, f32[128]{0:T(128)S(1)}, u32[]{:S(2)}, u32[]{:S(2)}) collective-permute-start(f32[128]{0:T(128)S(1)} %bitcast.33), channel_id=1, source_target_pairs={{0,64},{1,65},{2,66},{3,67},{4,68},{5,69},{6,70},{7,71},{8,72},{9,... | collective-permute-start | bytes 1544 | tf_op jit(solution)/shard_map/ppermute | solution.py:369
Sparse Core Ops, SparseCore 0:
  19.2 73.7 all-gather.1

commit v11 on v10

--- a/solution.py
+++ b/solution.py
@@ -14,7 +14,7 @@
 CHUNK = 64
 SLOTS = POOL * CHUNK
 DEAD = ROWS_DEV | (8 << 16)
-TBLK = 2048
+TBLK = 4096
 TSLOTS = 4
 LSLOTS = 4
 HID_SPLIT = 2
@@ -209,7 +209,7 @@
         ],
         out_specs=(vmem, vmem) if widen else vmem,
         scratch_shapes=scratch,
-        compiler_params=pltpu.CompilerParams(vmem_limit_bytes=(6 if widen else 4) * 2**20),
+        compiler_params=pltpu.CompilerParams(vmem_limit_bytes=(8 if widen else 4) * 2**20),
         name="bag_gather",
     )(y, lists, table)
 
@@ -357,18 +357,23 @@
     features = feature_rows(pooled)
     bias = lax.dynamic_slice(b_first, (q * part,), (part,)).astype(jnp.float32)
     scale = lax.dynamic_slice(w_out, (q * part,), (part,)).astype(jnp.float32)
-    far = lax.ppermute(features, "dev", [(d, d ^ 1) for d in range(n_dev)])
+    ways = [[d // ring * ring + (d + (1 if d % 2 == h else ring - 1)) % ring for d in range(n_dev)] for h in range(2)]
+    far = [
+        lax.ppermute(features[h * CHUNK : (h + 1) * CHUNK], "dev", list(enumerate(ways[h]))) for h in range(2)
+    ]
     bias, scale = bias.reshape(1, part), scale.reshape(1, part)
     near, kept = dense(swap(features, "section"), whole, bias, scale, True)
     near = near.reshape(-1)
-    far, near = lax.optimization_barrier((far, near))
-    far_part = dense(swap(far, "section"), kept, bias, scale, False).reshape(-1)
-
-    def moved(x, core, chip):
-        pairs = [(s * n_dev + d, (s ^ core) * n_dev + (d ^ chip)) for s in range(n_sec) for d in range(n_dev)]
+
+    def moved(x, core, way):
+        pairs = [(s * n_dev + d, (s ^ core) * n_dev + way[d]) for s in range(n_sec) for d in range(n_dev)]
         return lax.ppermute(x, both_axes, pairs)
 
-    return (near + moved(near, 1, 0)) + (moved(far_part, 0, 1) + moved(far_part, 1, 1))
+    near_2 = moved(near, 1, range(n_dev))
+    far, near, near_2 = lax.optimization_barrier((far, near, near_2))
+    far_part = dense(swap(jnp.concatenate(far), "section"), kept, bias, scale, False).reshape(2, CHUNK)
+    back = [moved(far_part[h], core, ways[h]) for h in range(2) for core in range(2)]
+    return (near + near_2) + jnp.concatenate([back[0] + back[1], back[2] + back[3]])
 
 
 def solution(mesh):

time: 133 us -> 135 us (1.015)
  starting transfers between devices: 24.9 us -> 27.9 us
  blocking collectives: 26.8 us -> 28.5 us
  waiting for transfers between devices: 24.9 us -> 23.4 us
    ppermute x3 -> x5, starting transfers between devices: 2.19 us -> 5.36 us  [moved(): return lax.ppermute(x, both_axes, pairs)]
    all_to_all x1, blocking collectives: 15.3 us -> 18.1 us  [body(): lax.all_to_all(pooled, 'dev', 0, 0, axis_index_groups=levels, tiled=True)]
    ppermute x1 -> x2, waiting for transfers between devices: 1.56 us -> 0.01 us  [body(): lax.ppermute(features[h * CHUNK:(h + 1) * CHUNK], 'dev', list(enumerate(w...]
  transfers between devices with their start and end apart: 13 -> 16, of which waited for: 7 -> 8; matrix products, arithmetic and copies ran while one was open for 0% -> 0% of each run, Pallas kernels for 29% -> 27%
where the time goes in v11:
time: 135 us; the launch traced here: 134 us
  Pallas kernels  38.1 us (28%)
  blocking collectives  28.5 us (21%)
  starting transfers between devices  27.9 us (21%)
  waiting for transfers between devices  23.4 us (17%)
  between operations  13.6 us (10%)
  other arithmetic  1.72 us (1%)
  local copies, waits for them, and re-layouts  1.38 us (1%)
    pallas_call x5, Pallas kernels, gather(): pl.pallas_call(functools.partial(gather_body, unroll=unroll, widen=widen,...  28.6 us
    all_to_all x1, blocking collectives, body(): lax.all_to_all(pooled, 'dev', 0, 0, axis_index_groups=levels, tiled=True)  18.1 us
    all_to_all x1, starting transfers between devices, body(): lax.all_to_all(lists.reshape(n_sec * n_dev, 4, 128), both_axes, 0, 0, til...  10.9 us
    all_to_all x1, waiting for transfers between devices, body(): lax.all_to_all(lists.reshape(n_sec * n_dev, 4, 128), both_axes, 0, 0, til...  10.8 us
    all_to_all x2, blocking collectives, swap(): lax.all_to_all(jnp.broadcast_to(x[None], (2, *x.shape)), axis, 0, 0, tile...  10.4 us
    ppermute x7, waiting for transfers between devices, along(): lax.ppermute(x, 'dev', [(d, d // ring * ring + (d + k) % ring) for d in r...  10.3 us
    ppermute x7, starting transfers between devices, along(): lax.ppermute(x, 'dev', [(d, d // ring * ring + (d + k) % ring) for d in r...  9.18 us
    ppermute x5, starting transfers between devices, moved(): return lax.ppermute(x, both_axes, pairs)  5.36 us
  transfers between devices with their start and end apart: 16, of which 8 were waited for; matrix products, arithmetic and copies ran while one was open for 0% of the time, Pallas kernels for 27%

profile of v11, /device:TPU:1, one launch (start us, length us, event | category | flops | bytes accessed | tf_op | source)
XLA Modules:
  0.0 134.5 jit_solution(7383636497948253774)
XLA Ops:
  7.5 2.2 %collective-permute-start = (bf16[64,1024]{1,0:T(8,128)(2,1)S(1)}, bf16[64,1024]{1,0:T(8,128)(2,1)S(1)}, u32[]{:S(2)}, u32[]{:S(2)}) collective-permute-start(bf16[64,1024]{1,0:T(8,128)(2,1)S(1)} %get-tuple-element.41), channel_id=1, source_target_pairs={{0,1},{1,2},{2,3},{3,0},{4,5},{5,6},{6,7},{7,4},{8,9},{9,10},{10,1... | collective-permute-start | bytes 393224 | tf_op jit(solution)/shard_map/ppermute | solution.py:332
  9.7 2.6 %collective-permute-start.1 = (bf16[64,1024]{1,0:T(8,128)(2,1)S(1)}, bf16[64,1024]{1,0:T(8,128)(2,1)S(1)}, u32[]{:S(2)}, u32[]{:S(2)}) collective-permute-start(bf16[64,1024]{1,0:T(8,128)(2,1)S(1)} %get-tuple-element.25), channel_id=1, source_target_pairs={{0,2},{1,3},{2,0},{3,1},{4,6},{5,7},{6,4},{7,5},{8,10},{9,11},{10,... | collective-permute-start | bytes 393224 | tf_op jit(solution)/shard_map/ppermute | solution.py:332
  13.4 3.2 %bag_lists.1 = s32[512,128]{1,0:T(8,128)} custom-call(s32[32,8,64]{2,1,0:T(8,128)} %bitcast.37, s32[32]{0:T(128)} %pool_ref.1), custom_call_target="tpu_custom_call" | custom-call | tf_op jit(solution)/shard_map/bag_lists/pallas_call | solution.py:109
  16.6 1.4 %collective-permute-done.1 = bf16[64,1024]{1,0:T(8,128)(2,1)S(1)} collective-permute-done((bf16[64,1024]{1,0:T(8,128)(2,1)S(1)}, bf16[64,1024]{1,0:T(8,128)(2,1)S(1)}, u32[]{:S(2)}, u32[]{:S(2)}) %collective-permute-start.1) | collective-permute-done | bytes 131104 | tf_op jit(solution)/shard_map/ppermute | solution.py:332
  19.1 10.9 %all-to-all-start = ((s32[128,4,128]{2,1,0:T(4,128)}), s32[128,4,128]{2,1,0:T(4,128)S(1)}, u32[]{:S(2)}, u32[]{:S(2)}) async-start(s32[128,4,128]{2,1,0:T(4,128)} %bitcast.2), calls=%async_computation | async-start | bytes 524288 | tf_op jit(solution)/shard_map/all_to_all | solution.py:340
  30.0 10.8 %all-to-all-done.lists_ref = s32[128,4,128]{2,1,0:T(4,128)S(1)} async-done(((s32[128,4,128]{2,1,0:T(4,128)}), s32[128,4,128]{2,1,0:T(4,128)S(1)}, u32[]{:S(2)}, u32[]{:S(2)}) %all-to-all-start) | async-done | bytes 262176 | tf_op jit(solution)/shard_map/all_to_all | solution.py:340
  40.9 9.5 %bag_gather.5 = (bf16[32,64,128]{2,1,0:T(8,128)(2,1)S(1)}, f32[32776,128]{1,0:T(8,128)S(1)}) custom-call(s32[1]{0:T(128)} %bitcast.y_ref, s32[65536]{0:T(1024)S(1)} %bitcast.24, bf16[32768,128]{1,0:T(8,128)(2,1)} %refs_0_), custom_call_target="tpu_custom_call" | custom-call | tf_op jit(solution)/shard_map/bag_gather/pallas_call | solution.py:202
  50.5 6.3 %bag_gather.7 = bf16[32,64,128]{2,1,0:T(8,128)(2,1)S(1)} custom-call(s32[1]{0:T(128)} %bitcast.y_ref, s32[65536]{0:T(1024)S(1)} %bitcast.25, f32[32776,128]{1,0:T(8,128)S(1)} %get-tuple-element.23.refs_0_), custom_call_target="tpu_custom_call" | custom-call | tf_op jit(solution)/shard_map/bag_gather/pallas_call | solution.py:202
  56.9 1.9 %collective-permute-start.4 = (bf16[32,64,128]{2,1,0:T(8,128)(2,1)S(1)}, bf16[32,64,128]{2,1,0:T(8,128)(2,1)S(1)}, u32[]{:S(2)}, u32[]{:S(2)}) collective-permute-start(bf16[32,64,128]{2,1,0:T(8,128)(2,1)S(1)} %get-tuple-element.24), channel_id=1, source_target_pairs={{0,2},{1,3},{2,0},{3,1},{4,6},{5,7},{6,4},{7,5},{8,10},{9,11},{10,... | collective-permute-start | bytes 1572872 | tf_op jit(solution)/shard_map/ppermute | solution.py:332
  58.8 3.4 %bag_gather.8 = bf16[16,64,128]{2,1,0:T(8,128)(2,1)S(1)} custom-call(s32[1]{0:T(128)} %bitcast.y_ref, s32[65536]{0:T(1024)S(1)} %bitcast.26, f32[32776,128]{1,0:T(8,128)S(1)} %get-tuple-element.23.refs_0_), custom_call_target="tpu_custom_call" | custom-call | tf_op jit(solution)/shard_map/bag_gather/pallas_call | solution.py:202
  62.2 3.4 %bag_gather.9 = bf16[16,64,128]{2,1,0:T(8,128)(2,1)S(1)} custom-call(s32[1]{0:T(128)} %bitcast.y_ref, s32[65536]{0:T(1024)S(1)} %bitcast.27, f32[32776,128]{1,0:T(8,128)S(1)} %get-tuple-element.23.refs_0_), custom_call_target="tpu_custom_call" | custom-call | tf_op jit(solution)/shard_map/bag_gather/pallas_call | solution.py:202
  65.6 1.1 collective-permute-start.5
  66.9 6.1 %bag_gather.6.part_0 = bf16[32,64,128]{2,1,0:T(8,128)(2,1)S(1)} custom-call(s32[1]{0:T(128)} %bitcast.y_ref, s32[65536]{0:T(1024)S(1)} %bitcast.28, f32[32776,128]{1,0:T(8,128)S(1)} %get-tuple-element.23.refs_0_), custom_call_target="tpu_custom_call" | custom-call | tf_op jit(solution)/shard_map/bag_gather/pallas_call | solution.py:202
  72.9 3.2 %collective-permute-done.5.part_3 = bf16[16,64,128]{2,1,0:T(8,128)(2,1)S(1)} collective-permute-done((bf16[16,64,128]{2,1,0:T(8,128)(2,1)S(1)}, bf16[16,64,128]{2,1,0:T(8,128)(2,1)S(1)}, u32[]{:S(2)}, u32[]{:S(2)}) %collective-permute-start.5) | collective-permute-done | bytes 262176 | tf_op jit(solution)/shard_map/ppermute | solution.py:332
  76.2 5.6 %collective-permute-done.6.part_3b = bf16[16,64,128]{2,1,0:T(8,128)(2,1)S(1)} collective-permute-done((bf16[16,64,128]{2,1,0:T(8,128)(2,1)S(1)}, bf16[16,64,128]{2,1,0:T(8,128)(2,1)S(1)}, u32[]{:S(2)}, u32[]{:S(2)}) %collective-permute-start.6) | collective-permute-done | bytes 262176 | tf_op jit(solution)/shard_map/ppermute | solution.py:332
  82.7 18.1 %all_to_all.20.pooled_ref = bf16[16,128,128]{2,1,0:T(8,128)(2,1)S(1)} all-to-all(bf16[16,128,128]{2,1,0:T(8,128)(2,1)S(1)} %bitcast.29), channel_id=1, replica_groups={{0,4,8,12,16,20,24,28,32,36,40,44,48,52,56,60},{1,5,9,13,17,21,25,29,33..., dimensions={0} | all-to-all | bytes 1048576 | tf_op jit(solution)/shard_map/all_to_all | solution.py:356
  102.0 1.4 %collective-permute-start.8 = (bf16[64,2048]{1,0:T(8,128)(2,1)S(1)}, bf16[64,2048]{1,0:T(8,128)(2,1)S(1)}, u32[]{:S(2)}, u32[]{:S(2)}) collective-permute-start(bf16[64,2048]{1,0:T(8,128)(2,1)S(1)} %get-tuple-element.39), channel_id=1, source_target_pairs={{0,3},{1,2},{2,1},{3,0},{4,7},{5,6},{6,5},{7,4},{8,11},{9,10},{10,... | collective-permute-start | bytes 786440 | tf_op jit(solution)/shard_map/ppermute | solution.py:362
  103.5 5.8 %all_to_all.21.both_ref = bf16[2,128,2048]{2,1,0:T(8,128)(2,1)S(1)} all-to-all(bf16[2,128,2048]{2,1,0:T(8,128)(2,1)S(1)} %broadcast_in_dim.4), channel_id=1, replica_groups=mesh['section'=2,'dev'=64] {'section'}, dimensions={0} | all-to-all | bytes 2097152 | tf_op jit(solution)/shard_map/all_to_all | solution.py:313
  109.3 3.9 %dense_near.1 = (f32[1,128]{1,0:T(1,128)S(1)}, bf16[4096,1024]{1,0:T(8,128)(2,1)S(1)}) custom-call(bf16[2,128,2048]{2,1,0:T(8,128)(2,1)S(1)} %all_to_all.21.both_ref, bf16[4096,1024]{1,0:T(8,128)(2,1)} %all-gather.2.cloned.1.call-done.w_ref, f32[1,1024]{1,0:T(1,128)S(1)} %bitcast.32, f32[1,1024]{1,0:T(1,128)S(1)} %bitcast.30), custom_call_target="tpu_custom_call" | custom-call | tf_op jit(solution)/shard_map/dense_near/pallas_call | solution.py:301
  114.8 4.5 %all_to_all.22.both_ref = bf16[2,128,2048]{2,1,0:T(8,128)(2,1)S(1)} all-to-all(bf16[2,128,2048]{2,1,0:T(8,128)(2,1)S(1)} %broadcast_in_dim.5), channel_id=1, replica_groups=mesh['section'=2,'dev'=64] {'section'}, dimensions={0} | all-to-all | bytes 2097152 | tf_op jit(solution)/shard_map/all_to_all | solution.py:313
  119.4 1.4 %dense_far.1 = f32[1,128]{1,0:T(1,128)S(1)} custom-call(bf16[2,128,2048]{2,1,0:T(8,128)(2,1)S(1)} %all_to_all.22.both_ref, bf16[4096,1024]{1,0:T(8,128)(2,1)S(1)} %get-tuple-element.34.w_ref, f32[1,1024]{1,0:T(1,128)S(1)} %bitcast.33, f32[1,1024]{1,0:T(1,128)S(1)} %bitcast.31), custom_call_target="tpu_custom_call" | custom-call | tf_op jit(solution)/shard_map/dense_far/pallas_call | solution.py:301
  120.8 1.1 collective-permute-start.12
  121.9 2.2 %collective-permute-start.13 = (f32[64]{0:T(128)S(1)}, f32[64]{0:T(128)S(1)}, u32[]{:S(2)}, u32[]{:S(2)}) collective-permute-start(f32[64]{0:T(128)S(1)} %get-tuple-element.44), channel_id=1, source_target_pairs={{0,67},{1,66},{2,65},{3,64},{4,71},{5,70},{6,69},{7,68},{8,75},{9,... | collective-permute-start | bytes 776 | tf_op jit(solution)/shard_map/ppermute | solution.py:370
  124.0 1.5 %collective-permute-start.11 = (f32[64]{0:T(128)S(1)}, f32[64]{0:T(128)S(1)}, u32[]{:S(2)}, u32[]{:S(2)}) collective-permute-start(f32[64]{0:T(128)S(1)} %get-tuple-element.43), channel_id=1, source_target_pairs={{0,65},{1,64},{2,67},{3,66},{4,69},{5,68},{6,71},{7,70},{8,73},{9,... | collective-permute-start | bytes 776 | tf_op jit(solution)/shard_map/ppermute | solution.py:370
  (41 shorter events, 9.5 us)
Async XLA Ops:
  6.5 102.8 %all-gather.2.cloned.1.call-start = ((), (), s32[]{:S(2)}) async-start(), calls=%async_computation.4 | async-start | bytes 8912896 | tf_op jit(solution)/shard_map/all_gather | solution.py:338
  7.5 9.1 %collective-permute-start = (bf16[64,1024]{1,0:T(8,128)(2,1)S(1)}, bf16[64,1024]{1,0:T(8,128)(2,1)S(1)}, u32[]{:S(2)}, u32[]{:S(2)}) collective-permute-start(bf16[64,1024]{1,0:T(8,128)(2,1)S(1)} %get-tuple-element.41), channel_id=1, source_target_pairs={{0,1},{1,2},{2,3},{3,0},{4,5},{5,6},{6,7},{7,4},{8,9},{9,10},{10,1... | collective-permute-start | bytes 393224 | tf_op jit(solution)/shard_map/ppermute | solution.py:332
  9.7 8.3 %collective-permute-start.1 = (bf16[64,1024]{1,0:T(8,128)(2,1)S(1)}, bf16[64,1024]{1,0:T(8,128)(2,1)S(1)}, u32[]{:S(2)}, u32[]{:S(2)}) collective-permute-start(bf16[64,1024]{1,0:T(8,128)(2,1)S(1)} %get-tuple-element.25), channel_id=1, source_target_pairs={{0,2},{1,3},{2,0},{3,1},{4,6},{5,7},{6,4},{7,5},{8,10},{9,11},{10,... | collective-permute-start | bytes 393224 | tf_op jit(solution)/shard_map/ppermute | solution.py:332
  12.3 5.7 %collective-permute-start.2 = (bf16[64,1024]{1,0:T(8,128)(2,1)S(1)}, bf16[64,1024]{1,0:T(8,128)(2,1)S(1)}, u32[]{:S(2)}, u32[]{:S(2)}) collective-permute-start(bf16[64,1024]{1,0:T(8,128)(2,1)S(1)} %get-tuple-element.41), channel_id=1, source_target_pairs={{0,3},{1,0},{2,1},{3,2},{4,7},{5,4},{6,5},{7,6},{8,11},{9,8},{10,9... | collective-permute-start | bytes 393224 | tf_op jit(solution)/shard_map/ppermute | solution.py:332
  19.1 21.7 %all-to-all-start = ((s32[128,4,128]{2,1,0:T(4,128)}), s32[128,4,128]{2,1,0:T(4,128)S(1)}, u32[]{:S(2)}, u32[]{:S(2)}) async-start(s32[128,4,128]{2,1,0:T(4,128)} %bitcast.2), calls=%async_computation | async-start | bytes 524288 | tf_op jit(solution)/shard_map/all_to_all | solution.py:340
  56.8 25.0 %collective-permute-start.3 = (bf16[32,64,128]{2,1,0:T(8,128)(2,1)S(1)}, bf16[32,64,128]{2,1,0:T(8,128)(2,1)S(1)}, u32[]{:S(2)}, u32[]{:S(2)}) collective-permute-start(bf16[32,64,128]{2,1,0:T(8,128)(2,1)S(1)} %bag_gather.7), channel_id=1, source_target_pairs={{0,1},{1,2},{2,3},{3,0},{4,5},{5,6},{6,7},{7,4},{8,9},{9,10},{10,1... | collective-permute-start | bytes 1572872 | tf_op jit(solution)/shard_map/ppermute | solution.py:332
  56.9 24.9 %collective-permute-start.4 = (bf16[32,64,128]{2,1,0:T(8,128)(2,1)S(1)}, bf16[32,64,128]{2,1,0:T(8,128)(2,1)S(1)}, u32[]{:S(2)}, u32[]{:S(2)}) collective-permute-start(bf16[32,64,128]{2,1,0:T(8,128)(2,1)S(1)} %get-tuple-element.24), channel_id=1, source_target_pairs={{0,2},{1,3},{2,0},{3,1},{4,6},{5,7},{6,4},{7,5},{8,10},{9,11},{10,... | collective-permute-start | bytes 1572872 | tf_op jit(solution)/shard_map/ppermute | solution.py:332
  65.5 37.8 %copy-start = (bf16[2048]{0:T(1024)(128)(2,1)S(1)}, bf16[2048]{0:T(1024)(128)(2,1)}, u32[]{:S(2)}) copy-start(bf16[2048]{0:T(1024)(128)(2,1)} %param.11) | copy-start | bytes 12292
  65.6 37.8 %copy-start.1 = (bf16[2048]{0:T(1024)(128)(2,1)S(1)}, bf16[2048]{0:T(1024)(128)(2,1)}, u32[]{:S(2)}) copy-start(bf16[2048]{0:T(1024)(128)(2,1)} %param.10) | copy-start | bytes 12292
  65.6 10.6 %collective-permute-start.5 = (bf16[16,64,128]{2,1,0:T(8,128)(2,1)S(1)}, bf16[16,64,128]{2,1,0:T(8,128)(2,1)S(1)}, u32[]{:S(2)}, u32[]{:S(2)}) collective-permute-start(bf16[16,64,128]{2,1,0:T(8,128)(2,1)S(1)} %bag_gather.8), channel_id=1, source_target_pairs={{0,3},{1,0},{2,1},{3,2},{4,7},{5,4},{6,5},{7,6},{8,11},{9,8},{10,9... | collective-permute-start | bytes 786440 | tf_op jit(solution)/shard_map/ppermute | solution.py:332
  66.6 15.2 %collective-permute-start.6 = (bf16[16,64,128]{2,1,0:T(8,128)(2,1)S(1)}, bf16[16,64,128]{2,1,0:T(8,128)(2,1)S(1)}, u32[]{:S(2)}, u32[]{:S(2)}) collective-permute-start(bf16[16,64,128]{2,1,0:T(8,128)(2,1)S(1)} %bag_gather.9), channel_id=1, source_target_pairs={{0,3},{1,0},{2,1},{3,2},{4,7},{5,4},{6,5},{7,6},{8,11},{9,8},{10,9... | collective-permute-start | bytes 786440 | tf_op jit(solution)/shard_map/ppermute | solution.py:332
  101.0 12.9 %collective-permute-start.7 = (bf16[64,2048]{1,0:T(8,128)(2,1)S(1)}, bf16[64,2048]{1,0:T(8,128)(2,1)S(1)}, u32[]{:S(2)}, u32[]{:S(2)}) collective-permute-start(bf16[64,2048]{1,0:T(8,128)(2,1)S(1)} %get-tuple-element.40), channel_id=1, source_target_pairs={{0,1},{1,0},{2,3},{3,2},{4,5},{5,4},{6,7},{7,6},{8,9},{9,8},{10,11... | collective-permute-start | bytes 786440 | tf_op jit(solution)/shard_map/ppermute | solution.py:362
  102.0 11.9 %collective-permute-start.8 = (bf16[64,2048]{1,0:T(8,128)(2,1)S(1)}, bf16[64,2048]{1,0:T(8,128)(2,1)S(1)}, u32[]{:S(2)}, u32[]{:S(2)}) collective-permute-start(bf16[64,2048]{1,0:T(8,128)(2,1)S(1)} %get-tuple-element.39), channel_id=1, source_target_pairs={{0,3},{1,2},{2,1},{3,0},{4,7},{5,6},{6,5},{7,4},{8,11},{9,10},{10,... | collective-permute-start | bytes 786440 | tf_op jit(solution)/shard_map/ppermute | solution.py:362
  113.2 1.5 %collective-permute-start.9 = (f32[128]{0:T(128)S(1)}, f32[128]{0:T(128)S(1)}, u32[]{:S(2)}, u32[]{:S(2)}) collective-permute-start(f32[128]{0:T(128)S(1)} %bitcast.34), channel_id=1, source_target_pairs={{0,64},{1,65},{2,66},{3,67},{4,68},{5,69},{6,70},{7,71},{8,72},{9,... | collective-permute-start | bytes 1544 | tf_op jit(solution)/shard_map/ppermute | solution.py:370
  120.8 4.7 %collective-permute-start.12 = (f32[64]{0:T(128)S(1)}, f32[64]{0:T(128)S(1)}, u32[]{:S(2)}, u32[]{:S(2)}) collective-permute-start(f32[64]{0:T(128)S(1)} %get-tuple-element.44), channel_id=1, source_target_pairs={{0,3},{1,2},{2,1},{3,0},{4,7},{5,6},{6,5},{7,4},{8,11},{9,10},{10,... | collective-permute-start | bytes 776 | tf_op jit(solution)/shard_map/ppermute | solution.py:370
  121.9 4.2 %collective-permute-start.13 = (f32[64]{0:T(128)S(1)}, f32[64]{0:T(128)S(1)}, u32[]{:S(2)}, u32[]{:S(2)}) collective-permute-start(f32[64]{0:T(128)S(1)} %get-tuple-element.44), channel_id=1, source_target_pairs={{0,67},{1,66},{2,65},{3,64},{4,71},{5,70},{6,69},{7,68},{8,75},{9,... | collective-permute-start | bytes 776 | tf_op jit(solution)/shard_map/ppermute | solution.py:370
  124.0 2.4 %collective-permute-start.10 = (f32[64]{0:T(128)S(1)}, f32[64]{0:T(128)S(1)}, u32[]{:S(2)}, u32[]{:S(2)}) collective-permute-start(f32[64]{0:T(128)S(1)} %get-tuple-element.43), channel_id=1, source_target_pairs={{0,1},{1,0},{2,3},{3,2},{4,5},{5,4},{6,7},{7,6},{8,9},{9,8},{10,11... | collective-permute-start | bytes 776 | tf_op jit(solution)/shard_map/ppermute | solution.py:370
  124.0 3.0 %collective-permute-start.11 = (f32[64]{0:T(128)S(1)}, f32[64]{0:T(128)S(1)}, u32[]{:S(2)}, u32[]{:S(2)}) collective-permute-start(f32[64]{0:T(128)S(1)} %get-tuple-element.43), channel_id=1, source_target_pairs={{0,65},{1,64},{2,67},{3,66},{4,69},{5,68},{6,71},{7,70},{8,73},{9,... | collective-permute-start | bytes 776 | tf_op jit(solution)/shard_map/ppermute | solution.py:370
Sparse Core Ops, SparseCore 0:
  19.2 75.1 all-gather.1

commit v12 on v11

--- a/solution.py
+++ b/solution.py
@@ -369,11 +369,11 @@
         pairs = [(s * n_dev + d, (s ^ core) * n_dev + way[d]) for s in range(n_sec) for d in range(n_dev)]
         return lax.ppermute(x, both_axes, pairs)
 
+    far, near = lax.optimization_barrier((far, near))
     near_2 = moved(near, 1, range(n_dev))
-    far, near, near_2 = lax.optimization_barrier((far, near, near_2))
-    far_part = dense(swap(jnp.concatenate(far), "section"), kept, bias, scale, False).reshape(2, CHUNK)
-    back = [moved(far_part[h], core, ways[h]) for h in range(2) for core in range(2)]
-    return (near + near_2) + jnp.concatenate([back[0] + back[1], back[2] + back[3]])
+    far_part = dense(swap(jnp.concatenate(far), "section"), kept, bias, scale, False).reshape(-1)
+    far_part = (far_part + moved(far_part, 1, range(n_dev))).reshape(2, CHUNK)
+    return (near + near_2) + jnp.concatenate([moved(far_part[h], 0, ways[h]) for h in range(2)])
 
 
 def solution(mesh):

time: 135 us -> 132 us (0.978)
  starting transfers between devices: 27.9 us -> 24.2 us
    ppermute x5 -> x4, starting transfers between devices: 5.36 us -> 1.65 us  [moved(): return lax.ppermute(x, both_axes, pairs)]
    ppermute x5 -> x4, waiting for transfers between devices: 2.32 us -> 3.27 us  [moved(): return lax.ppermute(x, both_axes, pairs)]
  transfers between devices with their start and end apart: 16 -> 15, of which waited for: 8 -> 6; matrix products, arithmetic and copies ran while one was open for 0% -> 0% of each run, Pallas kernels for 27% -> 28%
where the time goes in v12:
time: 132 us
  Pallas kernels  38.1 us (29%)
  blocking collectives  28.5 us (22%)
  waiting for transfers between devices  24.3 us (18%)
  starting transfers between devices  24.2 us (18%)
  between operations  13.6 us (10%)
  other arithmetic  1.71 us (1%)
  local copies, waits for them, and re-layouts  1.38 us (1%)
    pallas_call x5, Pallas kernels, gather(): pl.pallas_call(functools.partial(gather_body, unroll=unroll, widen=widen,...  28.6 us
    all_to_all x1, blocking collectives, body(): lax.all_to_all(pooled, 'dev', 0, 0, axis_index_groups=levels, tiled=True)  18.1 us
    all_to_all x1, starting transfers between devices, body(): lax.all_to_all(lists.reshape(n_sec * n_dev, 4, 128), both_axes, 0, 0, til...  10.9 us
    all_to_all x1, waiting for transfers between devices, body(): lax.all_to_all(lists.reshape(n_sec * n_dev, 4, 128), both_axes, 0, 0, til...  10.8 us
    all_to_all x2, blocking collectives, swap(): lax.all_to_all(jnp.broadcast_to(x[None], (2, *x.shape)), axis, 0, 0, tile...  10.4 us
    ppermute x7, waiting for transfers between devices, along(): lax.ppermute(x, 'dev', [(d, d // ring * ring + (d + k) % ring) for d in r...  10.3 us
    ppermute x7, starting transfers between devices, along(): lax.ppermute(x, 'dev', [(d, d // ring * ring + (d + k) % ring) for d in r...  9.18 us
    pallas_call x2, Pallas kernels, dense(): pl.pallas_call(functools.partial(dense_body, stream=stream), out_shape=(o...  5.23 us
  transfers between devices with their start and end apart: 15, of which 6 were waited for; matrix products, arithmetic and copies ran while one was open for 0% of the time, Pallas kernels for 28%

profile of v12, /device:TPU:1, one launch (start us, length us, event | category | flops | bytes accessed | tf_op | source)
XLA Modules:
  0.0 131.8 jit_solution(17985053852719673900)
XLA Ops:
  7.5 2.2 %collective-permute-start = (bf16[64,1024]{1,0:T(8,128)(2,1)S(1)}, bf16[64,1024]{1,0:T(8,128)(2,1)S(1)}, u32[]{:S(2)}, u32[]{:S(2)}) collective-permute-start(bf16[64,1024]{1,0:T(8,128)(2,1)S(1)} %get-tuple-element.39), channel_id=1, source_target_pairs={{0,1},{1,2},{2,3},{3,0},{4,5},{5,6},{6,7},{7,4},{8,9},{9,10},{10,1... | collective-permute-start | bytes 393224 | tf_op jit(solution)/shard_map/ppermute | solution.py:332
  9.7 2.6 %collective-permute-start.1 = (bf16[64,1024]{1,0:T(8,128)(2,1)S(1)}, bf16[64,1024]{1,0:T(8,128)(2,1)S(1)}, u32[]{:S(2)}, u32[]{:S(2)}) collective-permute-start(bf16[64,1024]{1,0:T(8,128)(2,1)S(1)} %get-tuple-element.24), channel_id=1, source_target_pairs={{0,2},{1,3},{2,0},{3,1},{4,6},{5,7},{6,4},{7,5},{8,10},{9,11},{10,... | collective-permute-start | bytes 393224 | tf_op jit(solution)/shard_map/ppermute | solution.py:332
  12.3 1.1 collective-permute-start.2
  13.4 3.2 %bag_lists.1 = s32[512,128]{1,0:T(8,128)} custom-call(s32[32,8,64]{2,1,0:T(8,128)} %bitcast.36, s32[32]{0:T(128)} %pool_ref.1), custom_call_target="tpu_custom_call" | custom-call | tf_op jit(solution)/shard_map/bag_lists/pallas_call | solution.py:109
  16.6 1.4 %collective-permute-done.1 = bf16[64,1024]{1,0:T(8,128)(2,1)S(1)} collective-permute-done((bf16[64,1024]{1,0:T(8,128)(2,1)S(1)}, bf16[64,1024]{1,0:T(8,128)(2,1)S(1)}, u32[]{:S(2)}, u32[]{:S(2)}) %collective-permute-start.1) | collective-permute-done | bytes 131104 | tf_op jit(solution)/shard_map/ppermute | solution.py:332
  19.1 10.9 %all-to-all-start = ((s32[128,4,128]{2,1,0:T(4,128)}), s32[128,4,128]{2,1,0:T(4,128)S(1)}, u32[]{:S(2)}, u32[]{:S(2)}) async-start(s32[128,4,128]{2,1,0:T(4,128)} %bitcast.2), calls=%async_computation | async-start | bytes 524288 | tf_op jit(solution)/shard_map/all_to_all | solution.py:340
  30.0 10.8 %all-to-all-done.lists_ref = s32[128,4,128]{2,1,0:T(4,128)S(1)} async-done(((s32[128,4,128]{2,1,0:T(4,128)}), s32[128,4,128]{2,1,0:T(4,128)S(1)}, u32[]{:S(2)}, u32[]{:S(2)}) %all-to-all-start) | async-done | bytes 262176 | tf_op jit(solution)/shard_map/all_to_all | solution.py:340
  40.9 9.5 %bag_gather.5 = (bf16[32,64,128]{2,1,0:T(8,128)(2,1)S(1)}, f32[32776,128]{1,0:T(8,128)S(1)}) custom-call(s32[1]{0:T(128)} %bitcast.y_ref, s32[65536]{0:T(1024)S(1)} %bitcast.22, bf16[32768,128]{1,0:T(8,128)(2,1)} %refs_0_), custom_call_target="tpu_custom_call" | custom-call | tf_op jit(solution)/shard_map/bag_gather/pallas_call | solution.py:202
  50.5 6.3 %bag_gather.7 = bf16[32,64,128]{2,1,0:T(8,128)(2,1)S(1)} custom-call(s32[1]{0:T(128)} %bitcast.y_ref, s32[65536]{0:T(1024)S(1)} %bitcast.23, f32[32776,128]{1,0:T(8,128)S(1)} %get-tuple-element.22.refs_0_), custom_call_target="tpu_custom_call" | custom-call | tf_op jit(solution)/shard_map/bag_gather/pallas_call | solution.py:202
  56.9 1.9 %collective-permute-start.4 = (bf16[32,64,128]{2,1,0:T(8,128)(2,1)S(1)}, bf16[32,64,128]{2,1,0:T(8,128)(2,1)S(1)}, u32[]{:S(2)}, u32[]{:S(2)}) collective-permute-start(bf16[32,64,128]{2,1,0:T(8,128)(2,1)S(1)} %get-tuple-element.23), channel_id=1, source_target_pairs={{0,2},{1,3},{2,0},{3,1},{4,6},{5,7},{6,4},{7,5},{8,10},{9,11},{10,... | collective-permute-start | bytes 1572872 | tf_op jit(solution)/shard_map/ppermute | solution.py:332
  58.8 3.4 %bag_gather.8 = bf16[16,64,128]{2,1,0:T(8,128)(2,1)S(1)} custom-call(s32[1]{0:T(128)} %bitcast.y_ref, s32[65536]{0:T(1024)S(1)} %bitcast.24, f32[32776,128]{1,0:T(8,128)S(1)} %get-tuple-element.22.refs_0_), custom_call_target="tpu_custom_call" | custom-call | tf_op jit(solution)/shard_map/bag_gather/pallas_call | solution.py:202
  62.2 3.4 %bag_gather.9 = bf16[16,64,128]{2,1,0:T(8,128)(2,1)S(1)} custom-call(s32[1]{0:T(128)} %bitcast.y_ref, s32[65536]{0:T(1024)S(1)} %bitcast.25, f32[32776,128]{1,0:T(8,128)S(1)} %get-tuple-element.22.refs_0_), custom_call_target="tpu_custom_call" | custom-call | tf_op jit(solution)/shard_map/bag_gather/pallas_call | solution.py:202
  65.6 1.1 collective-permute-start.5
  66.9 6.1 %bag_gather.6.part_0 = bf16[32,64,128]{2,1,0:T(8,128)(2,1)S(1)} custom-call(s32[1]{0:T(128)} %bitcast.y_ref, s32[65536]{0:T(1024)S(1)} %bitcast.26, f32[32776,128]{1,0:T(8,128)S(1)} %get-tuple-element.22.refs_0_), custom_call_target="tpu_custom_call" | custom-call | tf_op jit(solution)/shard_map/bag_gather/pallas_call | solution.py:202
  72.9 3.2 %collective-permute-done.5.part_3 = bf16[16,64,128]{2,1,0:T(8,128)(2,1)S(1)} collective-permute-done((bf16[16,64,128]{2,1,0:T(8,128)(2,1)S(1)}, bf16[16,64,128]{2,1,0:T(8,128)(2,1)S(1)}, u32[]{:S(2)}, u32[]{:S(2)}) %collective-permute-start.5) | collective-permute-done | bytes 262176 | tf_op jit(solution)/shard_map/ppermute | solution.py:332
  76.2 5.6 %collective-permute-done.6.part_3b = bf16[16,64,128]{2,1,0:T(8,128)(2,1)S(1)} collective-permute-done((bf16[16,64,128]{2,1,0:T(8,128)(2,1)S(1)}, bf16[16,64,128]{2,1,0:T(8,128)(2,1)S(1)}, u32[]{:S(2)}, u32[]{:S(2)}) %collective-permute-start.6) | collective-permute-done | bytes 262176 | tf_op jit(solution)/shard_map/ppermute | solution.py:332
  82.7 18.1 %all_to_all.20.pooled_ref = bf16[16,128,128]{2,1,0:T(8,128)(2,1)S(1)} all-to-all(bf16[16,128,128]{2,1,0:T(8,128)(2,1)S(1)} %bitcast.27), channel_id=1, replica_groups={{0,4,8,12,16,20,24,28,32,36,40,44,48,52,56,60},{1,5,9,13,17,21,25,29,33..., dimensions={0} | all-to-all | bytes 1048576 | tf_op jit(solution)/shard_map/all_to_all | solution.py:356
  101.9 1.4 %collective-permute-start.8 = (bf16[64,2048]{1,0:T(8,128)(2,1)S(1)}, bf16[64,2048]{1,0:T(8,128)(2,1)S(1)}, u32[]{:S(2)}, u32[]{:S(2)}) collective-permute-start(bf16[64,2048]{1,0:T(8,128)(2,1)S(1)} %get-tuple-element.37), channel_id=1, source_target_pairs={{0,3},{1,2},{2,1},{3,0},{4,7},{5,6},{6,5},{7,4},{8,11},{9,10},{10,... | collective-permute-start | bytes 786440 | tf_op jit(solution)/shard_map/ppermute | solution.py:362
  103.5 5.8 %all_to_all.21.both_ref = bf16[2,128,2048]{2,1,0:T(8,128)(2,1)S(1)} all-to-all(bf16[2,128,2048]{2,1,0:T(8,128)(2,1)S(1)} %broadcast_in_dim.4), channel_id=1, replica_groups=mesh['section'=2,'dev'=64] {'section'}, dimensions={0} | all-to-all | bytes 2097152 | tf_op jit(solution)/shard_map/all_to_all | solution.py:313
  109.3 3.9 %dense_near.1 = (f32[1,128]{1,0:T(1,128)S(1)}, bf16[4096,1024]{1,0:T(8,128)(2,1)S(1)}) custom-call(bf16[2,128,2048]{2,1,0:T(8,128)(2,1)S(1)} %all_to_all.21.both_ref, bf16[4096,1024]{1,0:T(8,128)(2,1)} %all-gather.2.cloned.1.call-done.w_ref, f32[1,1024]{1,0:T(1,128)S(1)} %bitcast.30, f32[1,1024]{1,0:T(1,128)S(1)} %bitcast.28), custom_call_target="tpu_custom_call" | custom-call | tf_op jit(solution)/shard_map/dense_near/pallas_call | solution.py:301
  113.4 4.6 %all_to_all.22.both_ref = bf16[2,128,2048]{2,1,0:T(8,128)(2,1)S(1)} all-to-all(bf16[2,128,2048]{2,1,0:T(8,128)(2,1)S(1)} %broadcast_in_dim.5), channel_id=1, replica_groups=mesh['section'=2,'dev'=64] {'section'}, dimensions={0} | all-to-all | bytes 2097152 | tf_op jit(solution)/shard_map/all_to_all | solution.py:313
  118.0 1.4 %dense_far.1 = f32[1,128]{1,0:T(1,128)S(1)} custom-call(bf16[2,128,2048]{2,1,0:T(8,128)(2,1)S(1)} %all_to_all.22.both_ref, bf16[4096,1024]{1,0:T(8,128)(2,1)S(1)} %get-tuple-element.32.w_ref, f32[1,1024]{1,0:T(1,128)S(1)} %bitcast.31, f32[1,1024]{1,0:T(1,128)S(1)} %bitcast.29), custom_call_target="tpu_custom_call" | custom-call | tf_op jit(solution)/shard_map/dense_far/pallas_call | solution.py:301
  120.7 1.1 collective-permute-start.12
  121.7 2.6 %collective-permute-done.12 = f32[64]{0:T(128)S(1)} collective-permute-done((f32[64]{0:T(128)S(1)}, f32[64]{0:T(128)S(1)}, u32[]{:S(2)}, u32[]{:S(2)}) %collective-permute-start.12) | collective-permute-done | bytes 288 | tf_op jit(solution)/shard_map/ppermute | solution.py:370
  (38 shorter events, 6.8 us)
Async XLA Ops:
  6.5 102.8 %all-gather.2.cloned.1.call-start = ((), (), s32[]{:S(2)}) async-start(), calls=%async_computation.4 | async-start | bytes 8912896 | tf_op jit(solution)/shard_map/all_gather | solution.py:338
  7.5 9.1 %collective-permute-start = (bf16[64,1024]{1,0:T(8,128)(2,1)S(1)}, bf16[64,1024]{1,0:T(8,128)(2,1)S(1)}, u32[]{:S(2)}, u32[]{:S(2)}) collective-permute-start(bf16[64,1024]{1,0:T(8,128)(2,1)S(1)} %get-tuple-element.39), channel_id=1, source_target_pairs={{0,1},{1,2},{2,3},{3,0},{4,5},{5,6},{6,7},{7,4},{8,9},{9,10},{10,1... | collective-permute-start | bytes 393224 | tf_op jit(solution)/shard_map/ppermute | solution.py:332
  9.7 8.3 %collective-permute-start.1 = (bf16[64,1024]{1,0:T(8,128)(2,1)S(1)}, bf16[64,1024]{1,0:T(8,128)(2,1)S(1)}, u32[]{:S(2)}, u32[]{:S(2)}) collective-permute-start(bf16[64,1024]{1,0:T(8,128)(2,1)S(1)} %get-tuple-element.24), channel_id=1, source_target_pairs={{0,2},{1,3},{2,0},{3,1},{4,6},{5,7},{6,4},{7,5},{8,10},{9,11},{10,... | collective-permute-start | bytes 393224 | tf_op jit(solution)/shard_map/ppermute | solution.py:332
  12.3 5.7 %collective-permute-start.2 = (bf16[64,1024]{1,0:T(8,128)(2,1)S(1)}, bf16[64,1024]{1,0:T(8,128)(2,1)S(1)}, u32[]{:S(2)}, u32[]{:S(2)}) collective-permute-start(bf16[64,1024]{1,0:T(8,128)(2,1)S(1)} %get-tuple-element.39), channel_id=1, source_target_pairs={{0,3},{1,0},{2,1},{3,2},{4,7},{5,4},{6,5},{7,6},{8,11},{9,8},{10,9... | collective-permute-start | bytes 393224 | tf_op jit(solution)/shard_map/ppermute | solution.py:332
  19.1 21.7 %all-to-all-start = ((s32[128,4,128]{2,1,0:T(4,128)}), s32[128,4,128]{2,1,0:T(4,128)S(1)}, u32[]{:S(2)}, u32[]{:S(2)}) async-start(s32[128,4,128]{2,1,0:T(4,128)} %bitcast.2), calls=%async_computation | async-start | bytes 524288 | tf_op jit(solution)/shard_map/all_to_all | solution.py:340
  56.8 25.0 %collective-permute-start.3 = (bf16[32,64,128]{2,1,0:T(8,128)(2,1)S(1)}, bf16[32,64,128]{2,1,0:T(8,128)(2,1)S(1)}, u32[]{:S(2)}, u32[]{:S(2)}) collective-permute-start(bf16[32,64,128]{2,1,0:T(8,128)(2,1)S(1)} %bag_gather.7), channel_id=1, source_target_pairs={{0,1},{1,2},{2,3},{3,0},{4,5},{5,6},{6,7},{7,4},{8,9},{9,10},{10,1... | collective-permute-start | bytes 1572872 | tf_op jit(solution)/shard_map/ppermute | solution.py:332
  56.9 24.9 %collective-permute-start.4 = (bf16[32,64,128]{2,1,0:T(8,128)(2,1)S(1)}, bf16[32,64,128]{2,1,0:T(8,128)(2,1)S(1)}, u32[]{:S(2)}, u32[]{:S(2)}) collective-permute-start(bf16[32,64,128]{2,1,0:T(8,128)(2,1)S(1)} %get-tuple-element.23), channel_id=1, source_target_pairs={{0,2},{1,3},{2,0},{3,1},{4,6},{5,7},{6,4},{7,5},{8,10},{9,11},{10,... | collective-permute-start | bytes 1572872 | tf_op jit(solution)/shard_map/ppermute | solution.py:332
  65.5 37.8 %copy-start = (bf16[2048]{0:T(1024)(128)(2,1)S(1)}, bf16[2048]{0:T(1024)(128)(2,1)}, u32[]{:S(2)}) copy-start(bf16[2048]{0:T(1024)(128)(2,1)} %param.11) | copy-start | bytes 12292
  65.5 37.8 %copy-start.1 = (bf16[2048]{0:T(1024)(128)(2,1)S(1)}, bf16[2048]{0:T(1024)(128)(2,1)}, u32[]{:S(2)}) copy-start(bf16[2048]{0:T(1024)(128)(2,1)} %param.10) | copy-start | bytes 12292
  65.6 10.6 %collective-permute-start.5 = (bf16[16,64,128]{2,1,0:T(8,128)(2,1)S(1)}, bf16[16,64,128]{2,1,0:T(8,128)(2,1)S(1)}, u32[]{:S(2)}, u32[]{:S(2)}) collective-permute-start(bf16[16,64,128]{2,1,0:T(8,128)(2,1)S(1)} %bag_gather.8), channel_id=1, source_target_pairs={{0,3},{1,0},{2,1},{3,2},{4,7},{5,4},{6,5},{7,6},{8,11},{9,8},{10,9... | collective-permute-start | bytes 786440 | tf_op jit(solution)/shard_map/ppermute | solution.py:332
  66.6 15.1 %collective-permute-start.6 = (bf16[16,64,128]{2,1,0:T(8,128)(2,1)S(1)}, bf16[16,64,128]{2,1,0:T(8,128)(2,1)S(1)}, u32[]{:S(2)}, u32[]{:S(2)}) collective-permute-start(bf16[16,64,128]{2,1,0:T(8,128)(2,1)S(1)} %bag_gather.9), channel_id=1, source_target_pairs={{0,3},{1,0},{2,1},{3,2},{4,7},{5,4},{6,5},{7,6},{8,11},{9,8},{10,9... | collective-permute-start | bytes 786440 | tf_op jit(solution)/shard_map/ppermute | solution.py:332
  100.9 12.3 %collective-permute-start.7 = (bf16[64,2048]{1,0:T(8,128)(2,1)S(1)}, bf16[64,2048]{1,0:T(8,128)(2,1)S(1)}, u32[]{:S(2)}, u32[]{:S(2)}) collective-permute-start(bf16[64,2048]{1,0:T(8,128)(2,1)S(1)} %get-tuple-element.38), channel_id=1, source_target_pairs={{0,1},{1,0},{2,3},{3,2},{4,5},{5,4},{6,7},{7,6},{8,9},{9,8},{10,11... | collective-permute-start | bytes 786440 | tf_op jit(solution)/shard_map/ppermute | solution.py:362
  101.9 11.3 %collective-permute-start.8 = (bf16[64,2048]{1,0:T(8,128)(2,1)S(1)}, bf16[64,2048]{1,0:T(8,128)(2,1)S(1)}, u32[]{:S(2)}, u32[]{:S(2)}) collective-permute-start(bf16[64,2048]{1,0:T(8,128)(2,1)S(1)} %get-tuple-element.37), channel_id=1, source_target_pairs={{0,3},{1,2},{2,1},{3,0},{4,7},{5,6},{6,5},{7,4},{8,11},{9,10},{10,... | collective-permute-start | bytes 786440 | tf_op jit(solution)/shard_map/ppermute | solution.py:362
  119.3 1.3 collective-permute-start.10
  119.8 2.0 %collective-permute-start.9 = (f32[128]{0:T(128)S(1)}, f32[128]{0:T(128)S(1)}, u32[]{:S(2)}, u32[]{:S(2)}) collective-permute-start(f32[128]{0:T(128)S(1)} %bitcast.33), channel_id=1, source_target_pairs={{0,64},{1,65},{2,66},{3,67},{4,68},{5,69},{6,70},{7,71},{8,72},{9,... | collective-permute-start | bytes 1544 | tf_op jit(solution)/shard_map/ppermute | solution.py:370
  120.7 3.6 %collective-permute-start.12 = (f32[64]{0:T(128)S(1)}, f32[64]{0:T(128)S(1)}, u32[]{:S(2)}, u32[]{:S(2)}) collective-permute-start(f32[64]{0:T(128)S(1)} %get-tuple-element.42), channel_id=1, source_target_pairs={{0,3},{1,2},{2,1},{3,0},{4,7},{5,6},{6,5},{7,4},{8,11},{9,10},{10,... | collective-permute-start | bytes 776 | tf_op jit(solution)/shard_map/ppermute | solution.py:370
  121.7 2.6 %collective-permute-start.11 = (f32[64]{0:T(128)S(1)}, f32[64]{0:T(128)S(1)}, u32[]{:S(2)}, u32[]{:S(2)}) collective-permute-start(f32[64]{0:T(128)S(1)} %get-tuple-element.41), channel_id=1, source_target_pairs={{0,1},{1,0},{2,3},{3,2},{4,5},{5,4},{6,7},{7,6},{8,9},{9,8},{10,11... | collective-permute-start | bytes 776 | tf_op jit(solution)/shard_map/ppermute | solution.py:370
Sparse Core Ops, SparseCore 0:
  19.2 75.1 all-gather.1

commit v13 on v12

--- a/solution.py
+++ b/solution.py
@@ -265,33 +265,37 @@
     )(pltpu.with_memory_space_constraint(pooled, pltpu.VMEM))
 
 
-def dense_body(both_ref, w_ref, bias_ref, scale_ref, *refs, stream):
+def dense_body(section_ref, own_ref, other_ref, w_ref, bias_ref, scale_ref, *refs, stream):
+    section = section_ref[0]
+    wide = own_ref.shape[1]
+    per = wide // WBLK
+    blocks = []
+    for i in range(2 * per):
+        side = section if i < per else 1 - section
+        blocks.append(pl.ds(pl.multiple_of(side * wide + i % per * WBLK, WBLK), WBLK))
     if stream:
         out_ref, kept, acc, sem = refs
-        blocks = [pl.ds(b * WBLK, WBLK) for b in range(kept.shape[0] // WBLK)]
         copies = [pltpu.make_async_copy(w_ref.at[b], kept.at[b], sem.at[i]) for i, b in enumerate(blocks)]
         for copy in copies:
             copy.start()
     else:
         out_ref, acc = refs
         kept = w_ref
-        blocks = [pl.ds(b * WBLK, WBLK) for b in range(kept.shape[0] // WBLK)]
-    wide = both_ref.shape[2]
     for i, block in enumerate(blocks):
         if stream:
             copies[i].wait()
-        at = i * WBLK
-        x = both_ref[at // wide, :, at % wide : at % wide + WBLK]
+        at = i % per * WBLK
+        x = (own_ref if i < per else other_ref)[:, at : at + WBLK]
         prod = jnp.dot(x, kept[block, :], preferred_element_type=jnp.float32)
-        acc[...] = prod if i == 0 else acc[...] + prod
+        acc[...] = acc[...] + prod if i else prod
     part = jnp.maximum(acc[...] + bias_ref[...], 0.0) * scale_ref[...]
     lanes = sum(part[:, 128 * i : 128 * i + 128] for i in range(part.shape[1] // 128))
     out_ref[...] = jnp.sum(lanes.T, axis=0, keepdims=True)
 
 
-def dense(both, weights, bias, scale, stream):
+def dense(section, own, other, weights, bias, scale, stream):
     vmem = pl.BlockSpec(memory_space=pltpu.VMEM)
-    samples = both.shape[1]
+    samples = own.shape[0]
     rows, units = weights.shape
     out = pltpu.VMEM((1, samples), jnp.float32)
     scratch = [pltpu.VMEM((samples, units), jnp.float32)]
@@ -301,21 +305,32 @@
     return pl.pallas_call(
         functools.partial(dense_body, stream=stream),
         out_shape=(out, pltpu.VMEM(weights.shape, weights.dtype)) if stream else out,
-        in_specs=[vmem, pl.BlockSpec(memory_space=pltpu.HBM) if stream else vmem, vmem, vmem],
+        in_specs=[
+            pl.BlockSpec(memory_space=pltpu.SMEM),
+            vmem,
+            vmem,
+            pl.BlockSpec(memory_space=pltpu.HBM) if stream else vmem,
+            vmem,
+            vmem,
+        ],
         out_specs=(vmem, vmem) if stream else vmem,
         scratch_shapes=scratch,
         compiler_params=pltpu.CompilerParams(vmem_limit_bytes=8 * 2**20),
         name="dense_near" if stream else "dense_far",
-    )(pltpu.with_memory_space_constraint(both, pltpu.VMEM), weights, bias, scale)
-
-
-def swap(x, axis):
-    return lax.all_to_all(jnp.broadcast_to(x[None], (2, *x.shape)), axis, 0, 0, tiled=True)
+    )(
+        section,
+        pltpu.with_memory_space_constraint(own, pltpu.VMEM),
+        pltpu.with_memory_space_constraint(other, pltpu.VMEM),
+        weights,
+        bias,
+        scale,
+    )
 
 
 def body(indices, pool_len, tables, w_first, b_first, w_out):
     n_dev = lax.axis_size("dev")
     n_sec = lax.axis_size("section")
+    section = lax.axis_index("section")
     dev = lax.axis_index("dev")
     lists = prep(jnp.transpose(indices, (1, 2, 0)), pool_len)
     ring = 4
@@ -362,16 +377,22 @@
         lax.ppermute(features[h * CHUNK : (h + 1) * CHUNK], "dev", list(enumerate(ways[h]))) for h in range(2)
     ]
     bias, scale = bias.reshape(1, part), scale.reshape(1, part)
-    near, kept = dense(swap(features, "section"), whole, bias, scale, True)
+    core = section.reshape(1)
+
+    def crossed(x):
+        return lax.ppermute(x, "section", [(0, 1), (1, 0)])
+
+    near, kept = dense(core, features, crossed(features), whole, bias, scale, True)
     near = near.reshape(-1)
 
-    def moved(x, core, way):
-        pairs = [(s * n_dev + d, (s ^ core) * n_dev + way[d]) for s in range(n_sec) for d in range(n_dev)]
+    def moved(x, turn, way):
+        pairs = [(s * n_dev + d, (s ^ turn) * n_dev + way[d]) for s in range(n_sec) for d in range(n_dev)]
         return lax.ppermute(x, both_axes, pairs)
 
     far, near = lax.optimization_barrier((far, near))
     near_2 = moved(near, 1, range(n_dev))
-    far_part = dense(swap(jnp.concatenate(far), "section"), kept, bias, scale, False).reshape(-1)
+    far = jnp.concatenate(far)
+    far_part = dense(core, far, crossed(far), kept, bias, scale, False).reshape(-1)
     far_part = (far_part + moved(far_part, 1, range(n_dev))).reshape(2, CHUNK)
     return (near + near_2) + jnp.concatenate([moved(far_part[h], 0, ways[h]) for h in range(2)])
 

time: 132 us -> 129 us (0.977)
  blocking collectives: 28.5 us -> 18.2 us
  waiting for transfers between devices: 24.3 us -> 28.8 us
  starting transfers between devices: 24.2 us -> 27.3 us
    all_to_all x2 -> x0, blocking collectives: 10.4 us -> none  [swap(): lax.all_to_all(jnp.broadcast_to(x[None], (2, *x.shape)), axis, 0, 0, tile...]
    ppermute x2, waiting for transfers between devices: 0.01 us -> 3.2 us  [body(): lax.ppermute(features[h * CHUNK:(h + 1) * CHUNK], 'dev', list(enumerate(w...]
    ppermute x0 -> x2, starting transfers between devices: none -> 2.03 us  [crossed(): return lax.ppermute(x, 'section', [(0, 1), (1, 0)])]
    ppermute x0 -> x2, waiting for transfers between devices: none -> 1.54 us  [crossed(): return lax.ppermute(x, 'section', [(0, 1), (1, 0)])]
  transfers between devices with their start and end apart: 15 -> 17, of which waited for: 6 -> 10; matrix products, arithmetic and copies ran while one was open for 0% -> 0% of each run, Pallas kernels for 28% -> 29%
where the time goes in v13:
time: 129 us
  Pallas kernels  38.1 us (30%)
  waiting for transfers between devices  28.8 us (22%)
  starting transfers between devices  27.3 us (21%)
  blocking collectives  18.2 us (14%)
  between operations  13.6 us (11%)
  other arithmetic  1.68 us (1%)
    pallas_call x5, Pallas kernels, gather(): pl.pallas_call(functools.partial(gather_body, unroll=unroll, widen=widen,...  28.6 us
    all_to_all x1, blocking collectives, body(): lax.all_to_all(pooled, 'dev', 0, 0, axis_index_groups=levels, tiled=True)  18.2 us
    all_to_all x1, starting transfers between devices, body(): lax.all_to_all(lists.reshape(n_sec * n_dev, 4, 128), both_axes, 0, 0, til...  10.9 us
    all_to_all x1, waiting for transfers between devices, body(): lax.all_to_all(lists.reshape(n_sec * n_dev, 4, 128), both_axes, 0, 0, til...  10.7 us
    ppermute x7, waiting for transfers between devices, along(): lax.ppermute(x, 'dev', [(d, d // ring * ring + (d + k) % ring) for d in r...  10.2 us
    ppermute x7, starting transfers between devices, along(): lax.ppermute(x, 'dev', [(d, d // ring * ring + (d + k) % ring) for d in r...  9.2 us
    pallas_call x2, Pallas kernels, dense(): pl.pallas_call(functools.partial(dense_body, stream=stream), out_shape=(o...  5.24 us
    pallas_call x1, Pallas kernels, prep(): pl.pallas_call(prep_body, out_shape=pltpu.VMEM((128 * 4, 128), jnp.int32)...  3.26 us
  transfers between devices with their start and end apart: 17, of which 10 were waited for; matrix products, arithmetic and copies ran while one was open for 0% of the time, Pallas kernels for 29%

profile of v13, /device:TPU:1, one launch (start us, length us, event | category | flops | bytes accessed | tf_op | source)
XLA Modules:
  0.0 128.9 jit_solution(10302311540917787789)
XLA Ops:
  7.5 2.2 %collective-permute-start = (bf16[64,1024]{1,0:T(8,128)(2,1)S(1)}, bf16[64,1024]{1,0:T(8,128)(2,1)S(1)}, u32[]{:S(2)}, u32[]{:S(2)}) collective-permute-start(bf16[64,1024]{1,0:T(8,128)(2,1)S(1)} %get-tuple-element.39), channel_id=1, source_target_pairs={{0,1},{1,2},{2,3},{3,0},{4,5},{5,6},{6,7},{7,4},{8,9},{9,10},{10,1... | collective-permute-start | bytes 393224 | tf_op jit(solution)/shard_map/ppermute | solution.py:347
  9.7 2.6 %collective-permute-start.1 = (bf16[64,1024]{1,0:T(8,128)(2,1)S(1)}, bf16[64,1024]{1,0:T(8,128)(2,1)S(1)}, u32[]{:S(2)}, u32[]{:S(2)}) collective-permute-start(bf16[64,1024]{1,0:T(8,128)(2,1)S(1)} %get-tuple-element.24), channel_id=1, source_target_pairs={{0,2},{1,3},{2,0},{3,1},{4,6},{5,7},{6,4},{7,5},{8,10},{9,11},{10,... | collective-permute-start | bytes 393224 | tf_op jit(solution)/shard_map/ppermute | solution.py:347
  13.4 3.3 %bag_lists.1 = s32[512,128]{1,0:T(8,128)} custom-call(s32[32,8,64]{2,1,0:T(8,128)} %bitcast.37, s32[32]{0:T(128)} %pool_ref.1), custom_call_target="tpu_custom_call" | custom-call | tf_op jit(solution)/shard_map/bag_lists/pallas_call | solution.py:109
  16.7 1.4 %collective-permute-done.1 = bf16[64,1024]{1,0:T(8,128)(2,1)S(1)} collective-permute-done((bf16[64,1024]{1,0:T(8,128)(2,1)S(1)}, bf16[64,1024]{1,0:T(8,128)(2,1)S(1)}, u32[]{:S(2)}, u32[]{:S(2)}) %collective-permute-start.1) | collective-permute-done | bytes 131104 | tf_op jit(solution)/shard_map/ppermute | solution.py:347
  19.1 10.9 %all-to-all-start = ((s32[128,4,128]{2,1,0:T(4,128)}), s32[128,4,128]{2,1,0:T(4,128)S(1)}, u32[]{:S(2)}, u32[]{:S(2)}) async-start(s32[128,4,128]{2,1,0:T(4,128)} %bitcast.2), calls=%async_computation | async-start | bytes 524288 | tf_op jit(solution)/shard_map/all_to_all | solution.py:355
  30.0 10.7 %all-to-all-done.lists_ref = s32[128,4,128]{2,1,0:T(4,128)S(1)} async-done(((s32[128,4,128]{2,1,0:T(4,128)}), s32[128,4,128]{2,1,0:T(4,128)S(1)}, u32[]{:S(2)}, u32[]{:S(2)}) %all-to-all-start) | async-done | bytes 262176 | tf_op jit(solution)/shard_map/all_to_all | solution.py:355
  40.9 9.5 %bag_gather.5 = (bf16[32,64,128]{2,1,0:T(8,128)(2,1)S(1)}, f32[32776,128]{1,0:T(8,128)S(1)}) custom-call(s32[1]{0:T(128)} %bitcast.y_ref, s32[65536]{0:T(1024)S(1)} %bitcast.23, bf16[32768,128]{1,0:T(8,128)(2,1)} %refs_0_), custom_call_target="tpu_custom_call" | custom-call | tf_op jit(solution)/shard_map/bag_gather/pallas_call | solution.py:202
  50.4 6.3 %bag_gather.7 = bf16[32,64,128]{2,1,0:T(8,128)(2,1)S(1)} custom-call(s32[1]{0:T(128)} %bitcast.y_ref, s32[65536]{0:T(1024)S(1)} %bitcast.24, f32[32776,128]{1,0:T(8,128)S(1)} %get-tuple-element.22.refs_0_), custom_call_target="tpu_custom_call" | custom-call | tf_op jit(solution)/shard_map/bag_gather/pallas_call | solution.py:202
  56.9 1.9 %collective-permute-start.4 = (bf16[32,64,128]{2,1,0:T(8,128)(2,1)S(1)}, bf16[32,64,128]{2,1,0:T(8,128)(2,1)S(1)}, u32[]{:S(2)}, u32[]{:S(2)}) collective-permute-start(bf16[32,64,128]{2,1,0:T(8,128)(2,1)S(1)} %get-tuple-element.23), channel_id=1, source_target_pairs={{0,2},{1,3},{2,0},{3,1},{4,6},{5,7},{6,4},{7,5},{8,10},{9,11},{10,... | collective-permute-start | bytes 1572872 | tf_op jit(solution)/shard_map/ppermute | solution.py:347
  58.8 3.4 %bag_gather.8 = bf16[16,64,128]{2,1,0:T(8,128)(2,1)S(1)} custom-call(s32[1]{0:T(128)} %bitcast.y_ref, s32[65536]{0:T(1024)S(1)} %bitcast.25, f32[32776,128]{1,0:T(8,128)S(1)} %get-tuple-element.22.refs_0_), custom_call_target="tpu_custom_call" | custom-call | tf_op jit(solution)/shard_map/bag_gather/pallas_call | solution.py:202
  62.2 3.4 %bag_gather.9 = bf16[16,64,128]{2,1,0:T(8,128)(2,1)S(1)} custom-call(s32[1]{0:T(128)} %bitcast.y_ref, s32[65536]{0:T(1024)S(1)} %bitcast.26, f32[32776,128]{1,0:T(8,128)S(1)} %get-tuple-element.22.refs_0_), custom_call_target="tpu_custom_call" | custom-call | tf_op jit(solution)/shard_map/bag_gather/pallas_call | solution.py:202
  66.8 6.1 %bag_gather.6.part_0 = bf16[32,64,128]{2,1,0:T(8,128)(2,1)S(1)} custom-call(s32[1]{0:T(128)} %bitcast.y_ref, s32[65536]{0:T(1024)S(1)} %bitcast.27, f32[32776,128]{1,0:T(8,128)S(1)} %get-tuple-element.22.refs_0_), custom_call_target="tpu_custom_call" | custom-call | tf_op jit(solution)/shard_map/bag_gather/pallas_call | solution.py:202
  72.9 3.2 %collective-permute-done.5.part_3 = bf16[16,64,128]{2,1,0:T(8,128)(2,1)S(1)} collective-permute-done((bf16[16,64,128]{2,1,0:T(8,128)(2,1)S(1)}, bf16[16,64,128]{2,1,0:T(8,128)(2,1)S(1)}, u32[]{:S(2)}, u32[]{:S(2)}) %collective-permute-start.5) | collective-permute-done | bytes 262176 | tf_op jit(solution)/shard_map/ppermute | solution.py:347
  76.1 5.6 %collective-permute-done.6.part_3b = bf16[16,64,128]{2,1,0:T(8,128)(2,1)S(1)} collective-permute-done((bf16[16,64,128]{2,1,0:T(8,128)(2,1)S(1)}, bf16[16,64,128]{2,1,0:T(8,128)(2,1)S(1)}, u32[]{:S(2)}, u32[]{:S(2)}) %collective-permute-start.6) | collective-permute-done | bytes 262176 | tf_op jit(solution)/shard_map/ppermute | solution.py:347
  82.6 18.2 %all_to_all.10.pooled_ref = bf16[16,128,128]{2,1,0:T(8,128)(2,1)S(1)} all-to-all(bf16[16,128,128]{2,1,0:T(8,128)(2,1)S(1)} %bitcast.28), channel_id=1, replica_groups={{0,4,8,12,16,20,24,28,32,36,40,44,48,52,56,60},{1,5,9,13,17,21,25,29,33..., dimensions={0} | all-to-all | bytes 1048576 | tf_op jit(solution)/shard_map/all_to_all | solution.py:371
  101.6 1.3 collective-permute-start.7
  102.9 1.6 %collective-permute-start.8 = (bf16[64,2048]{1,0:T(8,128)(2,1)S(1)}, bf16[64,2048]{1,0:T(8,128)(2,1)S(1)}, u32[]{:S(2)}, u32[]{:S(2)}) collective-permute-start(bf16[64,2048]{1,0:T(8,128)(2,1)S(1)} %get-tuple-element.37), channel_id=1, source_target_pairs={{0,3},{1,2},{2,1},{3,0},{4,7},{5,6},{6,5},{7,4},{8,11},{9,10},{10,... | collective-permute-start | bytes 786440 | tf_op jit(solution)/shard_map/ppermute | solution.py:377
  104.6 3.9 %dense_near.1 = (f32[1,128]{1,0:T(1,128)S(1)}, bf16[4096,1024]{1,0:T(8,128)(2,1)S(1)}) custom-call(s32[1]{0:T(128)} %bitcast.5.section_ref, bf16[128,2048]{1,0:T(8,128)(2,1)S(1)} %feature_rows.1.own_ref, bf16[128,2048]{1,0:T(8,128)(2,1)S(1)} %collective-permute-done.9.other_ref, bf16[4096,1024]{1,0:T(8,128)(2,1)} %all-gather.2.cloned.1.call-done.w_ref, ...), custom_call_target="tpu_custom_call" | custom-call | tf_op jit(solution)/shard_map/dense_near/pallas_call | solution.py:305
  109.5 2.1 %collective-permute-done.8 = bf16[64,2048]{1,0:T(8,128)(2,1)S(1)} collective-permute-done((bf16[64,2048]{1,0:T(8,128)(2,1)S(1)}, bf16[64,2048]{1,0:T(8,128)(2,1)S(1)}, u32[]{:S(2)}, u32[]{:S(2)}) %collective-permute-start.8) | collective-permute-done | bytes 262176 | tf_op jit(solution)/shard_map/ppermute | solution.py:377
  111.7 1.4 %collective-permute-start.11 = (bf16[128,2048]{1,0:T(8,128)(2,1)S(1)}, bf16[128,2048]{1,0:T(8,128)(2,1)S(1)}, u32[]{:S(2)}, u32[]{:S(2)}) collective-permute-start(bf16[128,2048]{1,0:T(8,128)(2,1)S(1)} %constant_dynamic-update-slice_fusion.own_ref), channel_id=1, source_target_pairs={{0,64},{64,0},{1,65},{65,1},{2,66},{66,2},{3,67},{67,3},{4,68},{68... | collective-permute-start | bytes 1572872 | tf_op jit(solution)/shard_map/ppermute | solution.py:383
  113.1 1.5 %collective-permute-done.11.other_ref = bf16[128,2048]{1,0:T(8,128)(2,1)S(1)} collective-permute-done((bf16[128,2048]{1,0:T(8,128)(2,1)S(1)}, bf16[128,2048]{1,0:T(8,128)(2,1)S(1)}, u32[]{:S(2)}, u32[]{:S(2)}) %collective-permute-start.11) | collective-permute-done | bytes 524320 | tf_op jit(solution)/shard_map/ppermute | solution.py:383
  114.7 1.4 %dense_far.1 = f32[1,128]{1,0:T(1,128)S(1)} custom-call(s32[1]{0:T(128)} %bitcast.5.section_ref, bf16[128,2048]{1,0:T(8,128)(2,1)S(1)} %constant_dynamic-update-slice_fusion.own_ref, bf16[128,2048]{1,0:T(8,128)(2,1)S(1)} %collective-permute-done.11.other_ref, bf16[4096,1024]{1,0:T(8,128)(2,1)S(1)} %get-tuple-element.32.w_ref, f32[1,1024]{1,0:T(1,128)S(1)} %bitcast.32, ...), custom_call_target="tpu_custom_call" | custom-call | tf_op jit(solution)/shard_map/dense_far/pallas_call | solution.py:305
  117.4 1.6 %collective-permute-start.14 = (f32[64]{0:T(128)S(1)}, f32[64]{0:T(128)S(1)}, u32[]{:S(2)}, u32[]{:S(2)}) collective-permute-start(f32[64]{0:T(128)S(1)} %get-tuple-element.42), channel_id=1, source_target_pairs={{0,3},{1,2},{2,1},{3,0},{4,7},{5,6},{6,5},{7,4},{8,11},{9,10},{10,... | collective-permute-start | bytes 776 | tf_op jit(solution)/shard_map/ppermute | solution.py:390
  119.0 2.0 %collective-permute-done.14 = f32[64]{0:T(128)S(1)} collective-permute-done((f32[64]{0:T(128)S(1)}, f32[64]{0:T(128)S(1)}, u32[]{:S(2)}, u32[]{:S(2)}) %collective-permute-start.14) | collective-permute-done | bytes 288 | tf_op jit(solution)/shard_map/ppermute | solution.py:390
  (39 shorter events, 9.8 us)
Async XLA Ops:
  6.5 98.0 %all-gather.2.cloned.1.call-start = ((), (), s32[]{:S(2)}) async-start(), calls=%async_computation.2 | async-start | bytes 8912896 | tf_op jit(solution)/shard_map/all_gather | solution.py:353
  7.5 9.1 %collective-permute-start = (bf16[64,1024]{1,0:T(8,128)(2,1)S(1)}, bf16[64,1024]{1,0:T(8,128)(2,1)S(1)}, u32[]{:S(2)}, u32[]{:S(2)}) collective-permute-start(bf16[64,1024]{1,0:T(8,128)(2,1)S(1)} %get-tuple-element.39), channel_id=1, source_target_pairs={{0,1},{1,2},{2,3},{3,0},{4,5},{5,6},{6,7},{7,4},{8,9},{9,10},{10,1... | collective-permute-start | bytes 393224 | tf_op jit(solution)/shard_map/ppermute | solution.py:347
  9.7 8.3 %collective-permute-start.1 = (bf16[64,1024]{1,0:T(8,128)(2,1)S(1)}, bf16[64,1024]{1,0:T(8,128)(2,1)S(1)}, u32[]{:S(2)}, u32[]{:S(2)}) collective-permute-start(bf16[64,1024]{1,0:T(8,128)(2,1)S(1)} %get-tuple-element.24), channel_id=1, source_target_pairs={{0,2},{1,3},{2,0},{3,1},{4,6},{5,7},{6,4},{7,5},{8,10},{9,11},{10,... | collective-permute-start | bytes 393224 | tf_op jit(solution)/shard_map/ppermute | solution.py:347
  12.3 5.7 %collective-permute-start.2 = (bf16[64,1024]{1,0:T(8,128)(2,1)S(1)}, bf16[64,1024]{1,0:T(8,128)(2,1)S(1)}, u32[]{:S(2)}, u32[]{:S(2)}) collective-permute-start(bf16[64,1024]{1,0:T(8,128)(2,1)S(1)} %get-tuple-element.39), channel_id=1, source_target_pairs={{0,3},{1,0},{2,1},{3,2},{4,7},{5,4},{6,5},{7,6},{8,11},{9,8},{10,9... | collective-permute-start | bytes 393224 | tf_op jit(solution)/shard_map/ppermute | solution.py:347
  19.1 21.7 %all-to-all-start = ((s32[128,4,128]{2,1,0:T(4,128)}), s32[128,4,128]{2,1,0:T(4,128)S(1)}, u32[]{:S(2)}, u32[]{:S(2)}) async-start(s32[128,4,128]{2,1,0:T(4,128)} %bitcast.2), calls=%async_computation | async-start | bytes 524288 | tf_op jit(solution)/shard_map/all_to_all | solution.py:355
  56.7 25.0 %collective-permute-start.3 = (bf16[32,64,128]{2,1,0:T(8,128)(2,1)S(1)}, bf16[32,64,128]{2,1,0:T(8,128)(2,1)S(1)}, u32[]{:S(2)}, u32[]{:S(2)}) collective-permute-start(bf16[32,64,128]{2,1,0:T(8,128)(2,1)S(1)} %bag_gather.7), channel_id=1, source_target_pairs={{0,1},{1,2},{2,3},{3,0},{4,5},{5,6},{6,7},{7,4},{8,9},{9,10},{10,1... | collective-permute-start | bytes 1572872 | tf_op jit(solution)/shard_map/ppermute | solution.py:347
  56.9 24.8 %collective-permute-start.4 = (bf16[32,64,128]{2,1,0:T(8,128)(2,1)S(1)}, bf16[32,64,128]{2,1,0:T(8,128)(2,1)S(1)}, u32[]{:S(2)}, u32[]{:S(2)}) collective-permute-start(bf16[32,64,128]{2,1,0:T(8,128)(2,1)S(1)} %get-tuple-element.23), channel_id=1, source_target_pairs={{0,2},{1,3},{2,0},{3,1},{4,6},{5,7},{6,4},{7,5},{8,10},{9,11},{10,... | collective-permute-start | bytes 1572872 | tf_op jit(solution)/shard_map/ppermute | solution.py:347
  65.5 39.0 %copy-start = (bf16[2048]{0:T(1024)(128)(2,1)S(1)}, bf16[2048]{0:T(1024)(128)(2,1)}, u32[]{:S(2)}) copy-start(bf16[2048]{0:T(1024)(128)(2,1)} %param.11) | copy-start | bytes 12292
  65.6 39.0 %copy-start.1 = (bf16[2048]{0:T(1024)(128)(2,1)S(1)}, bf16[2048]{0:T(1024)(128)(2,1)}, u32[]{:S(2)}) copy-start(bf16[2048]{0:T(1024)(128)(2,1)} %param.10) | copy-start | bytes 12292
  65.6 10.5 %collective-permute-start.5 = (bf16[16,64,128]{2,1,0:T(8,128)(2,1)S(1)}, bf16[16,64,128]{2,1,0:T(8,128)(2,1)S(1)}, u32[]{:S(2)}, u32[]{:S(2)}) collective-permute-start(bf16[16,64,128]{2,1,0:T(8,128)(2,1)S(1)} %bag_gather.8), channel_id=1, source_target_pairs={{0,3},{1,0},{2,1},{3,2},{4,7},{5,4},{6,5},{7,6},{8,11},{9,8},{10,9... | collective-permute-start | bytes 786440 | tf_op jit(solution)/shard_map/ppermute | solution.py:347
  66.6 15.0 %collective-permute-start.6 = (bf16[16,64,128]{2,1,0:T(8,128)(2,1)S(1)}, bf16[16,64,128]{2,1,0:T(8,128)(2,1)S(1)}, u32[]{:S(2)}, u32[]{:S(2)}) collective-permute-start(bf16[16,64,128]{2,1,0:T(8,128)(2,1)S(1)} %bag_gather.9), channel_id=1, source_target_pairs={{0,3},{1,0},{2,1},{3,2},{4,7},{5,4},{6,5},{7,6},{8,11},{9,8},{10,9... | collective-permute-start | bytes 786440 | tf_op jit(solution)/shard_map/ppermute | solution.py:347
  100.9 3.6 %collective-permute-start.9 = (bf16[128,2048]{1,0:T(8,128)(2,1)S(1)}, bf16[128,2048]{1,0:T(8,128)(2,1)S(1)}, u32[]{:S(2)}, u32[]{:S(2)}) collective-permute-start(bf16[128,2048]{1,0:T(8,128)(2,1)S(1)} %feature_rows.1.own_ref), channel_id=1, source_target_pairs={{0,64},{64,0},{1,65},{65,1},{2,66},{66,2},{3,67},{67,3},{4,68},{68... | collective-permute-start | bytes 1572872 | tf_op jit(solution)/shard_map/ppermute | solution.py:383
  101.6 7.9 %collective-permute-start.7 = (bf16[64,2048]{1,0:T(8,128)(2,1)S(1)}, bf16[64,2048]{1,0:T(8,128)(2,1)S(1)}, u32[]{:S(2)}, u32[]{:S(2)}) collective-permute-start(bf16[64,2048]{1,0:T(8,128)(2,1)S(1)} %get-tuple-element.38), channel_id=1, source_target_pairs={{0,1},{1,0},{2,3},{3,2},{4,5},{5,4},{6,7},{7,6},{8,9},{9,8},{10,11... | collective-permute-start | bytes 786440 | tf_op jit(solution)/shard_map/ppermute | solution.py:377
  102.9 8.8 %collective-permute-start.8 = (bf16[64,2048]{1,0:T(8,128)(2,1)S(1)}, bf16[64,2048]{1,0:T(8,128)(2,1)S(1)}, u32[]{:S(2)}, u32[]{:S(2)}) collective-permute-start(bf16[64,2048]{1,0:T(8,128)(2,1)S(1)} %get-tuple-element.37), channel_id=1, source_target_pairs={{0,3},{1,2},{2,1},{3,0},{4,7},{5,6},{6,5},{7,4},{8,11},{9,10},{10,... | collective-permute-start | bytes 786440 | tf_op jit(solution)/shard_map/ppermute | solution.py:377
  111.7 3.0 %collective-permute-start.11 = (bf16[128,2048]{1,0:T(8,128)(2,1)S(1)}, bf16[128,2048]{1,0:T(8,128)(2,1)S(1)}, u32[]{:S(2)}, u32[]{:S(2)}) collective-permute-start(bf16[128,2048]{1,0:T(8,128)(2,1)S(1)} %constant_dynamic-update-slice_fusion.own_ref), channel_id=1, source_target_pairs={{0,64},{64,0},{1,65},{65,1},{2,66},{66,2},{3,67},{67,3},{4,68},{68... | collective-permute-start | bytes 1572872 | tf_op jit(solution)/shard_map/ppermute | solution.py:383
  116.0 1.3 collective-permute-start.12
  116.5 2.5 %collective-permute-start.10 = (f32[128]{0:T(128)S(1)}, f32[128]{0:T(128)S(1)}, u32[]{:S(2)}, u32[]{:S(2)}) collective-permute-start(f32[128]{0:T(128)S(1)} %bitcast.34), channel_id=1, source_target_pairs={{0,64},{1,65},{2,66},{3,67},{4,68},{5,69},{6,70},{7,71},{8,72},{9,... | collective-permute-start | bytes 1544 | tf_op jit(solution)/shard_map/ppermute | solution.py:390
  117.4 3.6 %collective-permute-start.14 = (f32[64]{0:T(128)S(1)}, f32[64]{0:T(128)S(1)}, u32[]{:S(2)}, u32[]{:S(2)}) collective-permute-start(f32[64]{0:T(128)S(1)} %get-tuple-element.42), channel_id=1, source_target_pairs={{0,3},{1,2},{2,1},{3,0},{4,7},{5,6},{6,5},{7,4},{8,11},{9,10},{10,... | collective-permute-start | bytes 776 | tf_op jit(solution)/shard_map/ppermute | solution.py:390
  119.0 2.4 %collective-permute-start.13 = (f32[64]{0:T(128)S(1)}, f32[64]{0:T(128)S(1)}, u32[]{:S(2)}, u32[]{:S(2)}) collective-permute-start(f32[64]{0:T(128)S(1)} %get-tuple-element.41), channel_id=1, source_target_pairs={{0,1},{1,0},{2,3},{3,2},{4,5},{5,4},{6,7},{7,6},{8,9},{9,8},{10,11... | collective-permute-start | bytes 776 | tf_op jit(solution)/shard_map/ppermute | solution.py:390
Sparse Core Ops, SparseCore 0:
  19.2 75.1 all-gather.1

commit v14 on v13

--- a/solution.py
+++ b/solution.py
@@ -373,16 +373,16 @@
     bias = lax.dynamic_slice(b_first, (q * part,), (part,)).astype(jnp.float32)
     scale = lax.dynamic_slice(w_out, (q * part,), (part,)).astype(jnp.float32)
     ways = [[d // ring * ring + (d + (1 if d % 2 == h else ring - 1)) % ring for d in range(n_dev)] for h in range(2)]
-    far = [
-        lax.ppermute(features[h * CHUNK : (h + 1) * CHUNK], "dev", list(enumerate(ways[h]))) for h in range(2)
-    ]
+    far = [features[h * CHUNK : (h + 1) * CHUNK] for h in range(2)]
+    far = [lax.ppermute(far[h], "dev", list(enumerate(ways[h]))) for h in range(2)]
     bias, scale = bias.reshape(1, part), scale.reshape(1, part)
     core = section.reshape(1)
 
     def crossed(x):
         return lax.ppermute(x, "section", [(0, 1), (1, 0)])
 
-    near, kept = dense(core, features, crossed(features), whole, bias, scale, True)
+    other = crossed(features)
+    near, kept = dense(core, features, other, whole, bias, scale, True)
     near = near.reshape(-1)
 
     def moved(x, turn, way):

time: 129 us -> 129 us (level)
  no operation moved by 1% of the time
where the time goes in v14:
time: 129 us
  Pallas kernels  38.1 us (30%)
  waiting for transfers between devices  28.8 us (22%)
  starting transfers between devices  27.3 us (21%)
  blocking collectives  18.2 us (14%)
  between operations  13.6 us (11%)
  other arithmetic  1.68 us (1%)
    pallas_call x5, Pallas kernels, gather(): pl.pallas_call(functools.partial(gather_body, unroll=unroll, widen=widen,...  28.6 us
    all_to_all x1, blocking collectives, body(): lax.all_to_all(pooled, 'dev', 0, 0, axis_index_groups=levels, tiled=True)  18.2 us
    all_to_all x1, starting transfers between devices, body(): lax.all_to_all(lists.reshape(n_sec * n_dev, 4, 128), both_axes, 0, 0, til...  10.9 us
    all_to_all x1, waiting for transfers between devices, body(): lax.all_to_all(lists.reshape(n_sec * n_dev, 4, 128), both_axes, 0, 0, til...  10.7 us
    ppermute x7, waiting for transfers between devices, along(): lax.ppermute(x, 'dev', [(d, d // ring * ring + (d + k) % ring) for d in r...  10.2 us
    ppermute x7, starting transfers between devices, along(): lax.ppermute(x, 'dev', [(d, d // ring * ring + (d + k) % ring) for d in r...  9.2 us
    pallas_call x2, Pallas kernels, dense(): pl.pallas_call(functools.partial(dense_body, stream=stream), out_shape=(o...  5.24 us
    pallas_call x1, Pallas kernels, prep(): pl.pallas_call(prep_body, out_shape=pltpu.VMEM((128 * 4, 128), jnp.int32)...  3.26 us
  transfers between devices with their start and end apart: 17, of which 10 were waited for; matrix products, arithmetic and copies ran while one was open for 0% of the time, Pallas kernels for 29%

profile of v14, /device:TPU:1, one launch (start us, length us, event | category | flops | bytes accessed | tf_op | source)
XLA Modules:
  0.0 128.9 jit_solution(10302311540917787789)
XLA Ops:
  7.5 2.2 %collective-permute-start = (bf16[64,1024]{1,0:T(8,128)(2,1)S(1)}, bf16[64,1024]{1,0:T(8,128)(2,1)S(1)}, u32[]{:S(2)}, u32[]{:S(2)}) collective-permute-start(bf16[64,1024]{1,0:T(8,128)(2,1)S(1)} %get-tuple-element.39), channel_id=1, source_target_pairs={{0,1},{1,2},{2,3},{3,0},{4,5},{5,6},{6,7},{7,4},{8,9},{9,10},{10,1... | collective-permute-start | bytes 393224 | tf_op jit(solution)/shard_map/ppermute | solution.py:347
  9.7 2.6 %collective-permute-start.1 = (bf16[64,1024]{1,0:T(8,128)(2,1)S(1)}, bf16[64,1024]{1,0:T(8,128)(2,1)S(1)}, u32[]{:S(2)}, u32[]{:S(2)}) collective-permute-start(bf16[64,1024]{1,0:T(8,128)(2,1)S(1)} %get-tuple-element.24), channel_id=1, source_target_pairs={{0,2},{1,3},{2,0},{3,1},{4,6},{5,7},{6,4},{7,5},{8,10},{9,11},{10,... | collective-permute-start | bytes 393224 | tf_op jit(solution)/shard_map/ppermute | solution.py:347
  13.4 3.3 %bag_lists.1 = s32[512,128]{1,0:T(8,128)} custom-call(s32[32,8,64]{2,1,0:T(8,128)} %bitcast.37, s32[32]{0:T(128)} %pool_ref.1), custom_call_target="tpu_custom_call" | custom-call | tf_op jit(solution)/shard_map/bag_lists/pallas_call | solution.py:109
  16.7 1.4 %collective-permute-done.1 = bf16[64,1024]{1,0:T(8,128)(2,1)S(1)} collective-permute-done((bf16[64,1024]{1,0:T(8,128)(2,1)S(1)}, bf16[64,1024]{1,0:T(8,128)(2,1)S(1)}, u32[]{:S(2)}, u32[]{:S(2)}) %collective-permute-start.1) | collective-permute-done | bytes 131104 | tf_op jit(solution)/shard_map/ppermute | solution.py:347
  19.1 10.9 %all-to-all-start = ((s32[128,4,128]{2,1,0:T(4,128)}), s32[128,4,128]{2,1,0:T(4,128)S(1)}, u32[]{:S(2)}, u32[]{:S(2)}) async-start(s32[128,4,128]{2,1,0:T(4,128)} %bitcast.2), calls=%async_computation | async-start | bytes 524288 | tf_op jit(solution)/shard_map/all_to_all | solution.py:355
  30.0 10.7 %all-to-all-done.lists_ref = s32[128,4,128]{2,1,0:T(4,128)S(1)} async-done(((s32[128,4,128]{2,1,0:T(4,128)}), s32[128,4,128]{2,1,0:T(4,128)S(1)}, u32[]{:S(2)}, u32[]{:S(2)}) %all-to-all-start) | async-done | bytes 262176 | tf_op jit(solution)/shard_map/all_to_all | solution.py:355
  40.9 9.5 %bag_gather.5 = (bf16[32,64,128]{2,1,0:T(8,128)(2,1)S(1)}, f32[32776,128]{1,0:T(8,128)S(1)}) custom-call(s32[1]{0:T(128)} %bitcast.y_ref, s32[65536]{0:T(1024)S(1)} %bitcast.23, bf16[32768,128]{1,0:T(8,128)(2,1)} %refs_0_), custom_call_target="tpu_custom_call" | custom-call | tf_op jit(solution)/shard_map/bag_gather/pallas_call | solution.py:202
  50.4 6.3 %bag_gather.7 = bf16[32,64,128]{2,1,0:T(8,128)(2,1)S(1)} custom-call(s32[1]{0:T(128)} %bitcast.y_ref, s32[65536]{0:T(1024)S(1)} %bitcast.24, f32[32776,128]{1,0:T(8,128)S(1)} %get-tuple-element.22.refs_0_), custom_call_target="tpu_custom_call" | custom-call | tf_op jit(solution)/shard_map/bag_gather/pallas_call | solution.py:202
  56.9 1.9 %collective-permute-start.4 = (bf16[32,64,128]{2,1,0:T(8,128)(2,1)S(1)}, bf16[32,64,128]{2,1,0:T(8,128)(2,1)S(1)}, u32[]{:S(2)}, u32[]{:S(2)}) collective-permute-start(bf16[32,64,128]{2,1,0:T(8,128)(2,1)S(1)} %get-tuple-element.23), channel_id=1, source_target_pairs={{0,2},{1,3},{2,0},{3,1},{4,6},{5,7},{6,4},{7,5},{8,10},{9,11},{10,... | collective-permute-start | bytes 1572872 | tf_op jit(solution)/shard_map/ppermute | solution.py:347
  58.8 3.4 %bag_gather.8 = bf16[16,64,128]{2,1,0:T(8,128)(2,1)S(1)} custom-call(s32[1]{0:T(128)} %bitcast.y_ref, s32[65536]{0:T(1024)S(1)} %bitcast.25, f32[32776,128]{1,0:T(8,128)S(1)} %get-tuple-element.22.refs_0_), custom_call_target="tpu_custom_call" | custom-call | tf_op jit(solution)/shard_map/bag_gather/pallas_call | solution.py:202
  62.2 3.4 %bag_gather.9 = bf16[16,64,128]{2,1,0:T(8,128)(2,1)S(1)} custom-call(s32[1]{0:T(128)} %bitcast.y_ref, s32[65536]{0:T(1024)S(1)} %bitcast.26, f32[32776,128]{1,0:T(8,128)S(1)} %get-tuple-element.22.refs_0_), custom_call_target="tpu_custom_call" | custom-call | tf_op jit(solution)/shard_map/bag_gather/pallas_call | solution.py:202
  66.8 6.1 %bag_gather.6.part_0 = bf16[32,64,128]{2,1,0:T(8,128)(2,1)S(1)} custom-call(s32[1]{0:T(128)} %bitcast.y_ref, s32[65536]{0:T(1024)S(1)} %bitcast.27, f32[32776,128]{1,0:T(8,128)S(1)} %get-tuple-element.22.refs_0_), custom_call_target="tpu_custom_call" | custom-call | tf_op jit(solution)/shard_map/bag_gather/pallas_call | solution.py:202
  72.9 3.2 %collective-permute-done.5.part_3 = bf16[16,64,128]{2,1,0:T(8,128)(2,1)S(1)} collective-permute-done((bf16[16,64,128]{2,1,0:T(8,128)(2,1)S(1)}, bf16[16,64,128]{2,1,0:T(8,128)(2,1)S(1)}, u32[]{:S(2)}, u32[]{:S(2)}) %collective-permute-start.5) | collective-permute-done | bytes 262176 | tf_op jit(solution)/shard_map/ppermute | solution.py:347
  76.1 5.6 %collective-permute-done.6.part_3b = bf16[16,64,128]{2,1,0:T(8,128)(2,1)S(1)} collective-permute-done((bf16[16,64,128]{2,1,0:T(8,128)(2,1)S(1)}, bf16[16,64,128]{2,1,0:T(8,128)(2,1)S(1)}, u32[]{:S(2)}, u32[]{:S(2)}) %collective-permute-start.6) | collective-permute-done | bytes 262176 | tf_op jit(solution)/shard_map/ppermute | solution.py:347
  82.6 18.2 %all_to_all.10.pooled_ref = bf16[16,128,128]{2,1,0:T(8,128)(2,1)S(1)} all-to-all(bf16[16,128,128]{2,1,0:T(8,128)(2,1)S(1)} %bitcast.28), channel_id=1, replica_groups={{0,4,8,12,16,20,24,28,32,36,40,44,48,52,56,60},{1,5,9,13,17,21,25,29,33..., dimensions={0} | all-to-all | bytes 1048576 | tf_op jit(solution)/shard_map/all_to_all | solution.py:371
  101.6 1.3 collective-permute-start.7
  102.9 1.6 %collective-permute-start.8 = (bf16[64,2048]{1,0:T(8,128)(2,1)S(1)}, bf16[64,2048]{1,0:T(8,128)(2,1)S(1)}, u32[]{:S(2)}, u32[]{:S(2)}) collective-permute-start(bf16[64,2048]{1,0:T(8,128)(2,1)S(1)} %get-tuple-element.37), channel_id=1, source_target_pairs={{0,3},{1,2},{2,1},{3,0},{4,7},{5,6},{6,5},{7,4},{8,11},{9,10},{10,... | collective-permute-start | bytes 786440 | tf_op jit(solution)/shard_map/ppermute | solution.py:377
  104.6 3.9 %dense_near.1 = (f32[1,128]{1,0:T(1,128)S(1)}, bf16[4096,1024]{1,0:T(8,128)(2,1)S(1)}) custom-call(s32[1]{0:T(128)} %bitcast.5.section_ref, bf16[128,2048]{1,0:T(8,128)(2,1)S(1)} %feature_rows.1.own_ref, bf16[128,2048]{1,0:T(8,128)(2,1)S(1)} %collective-permute-done.9.other_ref, bf16[4096,1024]{1,0:T(8,128)(2,1)} %all-gather.2.cloned.1.call-done.w_ref, ...), custom_call_target="tpu_custom_call" | custom-call | tf_op jit(solution)/shard_map/dense_near/pallas_call | solution.py:305
  109.5 2.1 %collective-permute-done.8 = bf16[64,2048]{1,0:T(8,128)(2,1)S(1)} collective-permute-done((bf16[64,2048]{1,0:T(8,128)(2,1)S(1)}, bf16[64,2048]{1,0:T(8,128)(2,1)S(1)}, u32[]{:S(2)}, u32[]{:S(2)}) %collective-permute-start.8) | collective-permute-done | bytes 262176 | tf_op jit(solution)/shard_map/ppermute | solution.py:377
  111.7 1.4 %collective-permute-start.11 = (bf16[128,2048]{1,0:T(8,128)(2,1)S(1)}, bf16[128,2048]{1,0:T(8,128)(2,1)S(1)}, u32[]{:S(2)}, u32[]{:S(2)}) collective-permute-start(bf16[128,2048]{1,0:T(8,128)(2,1)S(1)} %constant_dynamic-update-slice_fusion.own_ref), channel_id=1, source_target_pairs={{0,64},{64,0},{1,65},{65,1},{2,66},{66,2},{3,67},{67,3},{4,68},{68... | collective-permute-start | bytes 1572872 | tf_op jit(solution)/shard_map/ppermute | solution.py:382
  113.1 1.5 %collective-permute-done.11.other_ref = bf16[128,2048]{1,0:T(8,128)(2,1)S(1)} collective-permute-done((bf16[128,2048]{1,0:T(8,128)(2,1)S(1)}, bf16[128,2048]{1,0:T(8,128)(2,1)S(1)}, u32[]{:S(2)}, u32[]{:S(2)}) %collective-permute-start.11) | collective-permute-done | bytes 524320 | tf_op jit(solution)/shard_map/ppermute | solution.py:382
  114.7 1.4 %dense_far.1 = f32[1,128]{1,0:T(1,128)S(1)} custom-call(s32[1]{0:T(128)} %bitcast.5.section_ref, bf16[128,2048]{1,0:T(8,128)(2,1)S(1)} %constant_dynamic-update-slice_fusion.own_ref, bf16[128,2048]{1,0:T(8,128)(2,1)S(1)} %collective-permute-done.11.other_ref, bf16[4096,1024]{1,0:T(8,128)(2,1)S(1)} %get-tuple-element.32.w_ref, f32[1,1024]{1,0:T(1,128)S(1)} %bitcast.32, ...), custom_call_target="tpu_custom_call" | custom-call | tf_op jit(solution)/shard_map/dense_far/pallas_call | solution.py:305
  117.4 1.6 %collective-permute-start.14 = (f32[64]{0:T(128)S(1)}, f32[64]{0:T(128)S(1)}, u32[]{:S(2)}, u32[]{:S(2)}) collective-permute-start(f32[64]{0:T(128)S(1)} %get-tuple-element.42), channel_id=1, source_target_pairs={{0,3},{1,2},{2,1},{3,0},{4,7},{5,6},{6,5},{7,4},{8,11},{9,10},{10,... | collective-permute-start | bytes 776 | tf_op jit(solution)/shard_map/ppermute | solution.py:390
  119.0 2.0 %collective-permute-done.14 = f32[64]{0:T(128)S(1)} collective-permute-done((f32[64]{0:T(128)S(1)}, f32[64]{0:T(128)S(1)}, u32[]{:S(2)}, u32[]{:S(2)}) %collective-permute-start.14) | collective-permute-done | bytes 288 | tf_op jit(solution)/shard_map/ppermute | solution.py:390
  (39 shorter events, 9.8 us)
Async XLA Ops:
  6.5 98.0 %all-gather.2.cloned.1.call-start = ((), (), s32[]{:S(2)}) async-start(), calls=%async_computation.2 | async-start | bytes 8912896 | tf_op jit(solution)/shard_map/all_gather | solution.py:353
  7.5 9.1 %collective-permute-start = (bf16[64,1024]{1,0:T(8,128)(2,1)S(1)}, bf16[64,1024]{1,0:T(8,128)(2,1)S(1)}, u32[]{:S(2)}, u32[]{:S(2)}) collective-permute-start(bf16[64,1024]{1,0:T(8,128)(2,1)S(1)} %get-tuple-element.39), channel_id=1, source_target_pairs={{0,1},{1,2},{2,3},{3,0},{4,5},{5,6},{6,7},{7,4},{8,9},{9,10},{10,1... | collective-permute-start | bytes 393224 | tf_op jit(solution)/shard_map/ppermute | solution.py:347
  9.7 8.3 %collective-permute-start.1 = (bf16[64,1024]{1,0:T(8,128)(2,1)S(1)}, bf16[64,1024]{1,0:T(8,128)(2,1)S(1)}, u32[]{:S(2)}, u32[]{:S(2)}) collective-permute-start(bf16[64,1024]{1,0:T(8,128)(2,1)S(1)} %get-tuple-element.24), channel_id=1, source_target_pairs={{0,2},{1,3},{2,0},{3,1},{4,6},{5,7},{6,4},{7,5},{8,10},{9,11},{10,... | collective-permute-start | bytes 393224 | tf_op jit(solution)/shard_map/ppermute | solution.py:347
  12.3 5.7 %collective-permute-start.2 = (bf16[64,1024]{1,0:T(8,128)(2,1)S(1)}, bf16[64,1024]{1,0:T(8,128)(2,1)S(1)}, u32[]{:S(2)}, u32[]{:S(2)}) collective-permute-start(bf16[64,1024]{1,0:T(8,128)(2,1)S(1)} %get-tuple-element.39), channel_id=1, source_target_pairs={{0,3},{1,0},{2,1},{3,2},{4,7},{5,4},{6,5},{7,6},{8,11},{9,8},{10,9... | collective-permute-start | bytes 393224 | tf_op jit(solution)/shard_map/ppermute | solution.py:347
  19.1 21.7 %all-to-all-start = ((s32[128,4,128]{2,1,0:T(4,128)}), s32[128,4,128]{2,1,0:T(4,128)S(1)}, u32[]{:S(2)}, u32[]{:S(2)}) async-start(s32[128,4,128]{2,1,0:T(4,128)} %bitcast.2), calls=%async_computation | async-start | bytes 524288 | tf_op jit(solution)/shard_map/all_to_all | solution.py:355
  56.7 25.0 %collective-permute-start.3 = (bf16[32,64,128]{2,1,0:T(8,128)(2,1)S(1)}, bf16[32,64,128]{2,1,0:T(8,128)(2,1)S(1)}, u32[]{:S(2)}, u32[]{:S(2)}) collective-permute-start(bf16[32,64,128]{2,1,0:T(8,128)(2,1)S(1)} %bag_gather.7), channel_id=1, source_target_pairs={{0,1},{1,2},{2,3},{3,0},{4,5},{5,6},{6,7},{7,4},{8,9},{9,10},{10,1... | collective-permute-start | bytes 1572872 | tf_op jit(solution)/shard_map/ppermute | solution.py:347
  56.9 24.8 %collective-permute-start.4 = (bf16[32,64,128]{2,1,0:T(8,128)(2,1)S(1)}, bf16[32,64,128]{2,1,0:T(8,128)(2,1)S(1)}, u32[]{:S(2)}, u32[]{:S(2)}) collective-permute-start(bf16[32,64,128]{2,1,0:T(8,128)(2,1)S(1)} %get-tuple-element.23), channel_id=1, source_target_pairs={{0,2},{1,3},{2,0},{3,1},{4,6},{5,7},{6,4},{7,5},{8,10},{9,11},{10,... | collective-permute-start | bytes 1572872 | tf_op jit(solution)/shard_map/ppermute | solution.py:347
  65.5 39.0 %copy-start = (bf16[2048]{0:T(1024)(128)(2,1)S(1)}, bf16[2048]{0:T(1024)(128)(2,1)}, u32[]{:S(2)}) copy-start(bf16[2048]{0:T(1024)(128)(2,1)} %param.11) | copy-start | bytes 12292
  65.6 39.0 %copy-start.1 = (bf16[2048]{0:T(1024)(128)(2,1)S(1)}, bf16[2048]{0:T(1024)(128)(2,1)}, u32[]{:S(2)}) copy-start(bf16[2048]{0:T(1024)(128)(2,1)} %param.10) | copy-start | bytes 12292
  65.6 10.5 %collective-permute-start.5 = (bf16[16,64,128]{2,1,0:T(8,128)(2,1)S(1)}, bf16[16,64,128]{2,1,0:T(8,128)(2,1)S(1)}, u32[]{:S(2)}, u32[]{:S(2)}) collective-permute-start(bf16[16,64,128]{2,1,0:T(8,128)(2,1)S(1)} %bag_gather.8), channel_id=1, source_target_pairs={{0,3},{1,0},{2,1},{3,2},{4,7},{5,4},{6,5},{7,6},{8,11},{9,8},{10,9... | collective-permute-start | bytes 786440 | tf_op jit(solution)/shard_map/ppermute | solution.py:347
  66.6 15.0 %collective-permute-start.6 = (bf16[16,64,128]{2,1,0:T(8,128)(2,1)S(1)}, bf16[16,64,128]{2,1,0:T(8,128)(2,1)S(1)}, u32[]{:S(2)}, u32[]{:S(2)}) collective-permute-start(bf16[16,64,128]{2,1,0:T(8,128)(2,1)S(1)} %bag_gather.9), channel_id=1, source_target_pairs={{0,3},{1,0},{2,1},{3,2},{4,7},{5,4},{6,5},{7,6},{8,11},{9,8},{10,9... | collective-permute-start | bytes 786440 | tf_op jit(solution)/shard_map/ppermute | solution.py:347
  100.9 3.6 %collective-permute-start.9 = (bf16[128,2048]{1,0:T(8,128)(2,1)S(1)}, bf16[128,2048]{1,0:T(8,128)(2,1)S(1)}, u32[]{:S(2)}, u32[]{:S(2)}) collective-permute-start(bf16[128,2048]{1,0:T(8,128)(2,1)S(1)} %feature_rows.1.own_ref), channel_id=1, source_target_pairs={{0,64},{64,0},{1,65},{65,1},{2,66},{66,2},{3,67},{67,3},{4,68},{68... | collective-permute-start | bytes 1572872 | tf_op jit(solution)/shard_map/ppermute | solution.py:382
  101.6 7.9 %collective-permute-start.7 = (bf16[64,2048]{1,0:T(8,128)(2,1)S(1)}, bf16[64,2048]{1,0:T(8,128)(2,1)S(1)}, u32[]{:S(2)}, u32[]{:S(2)}) collective-permute-start(bf16[64,2048]{1,0:T(8,128)(2,1)S(1)} %get-tuple-element.38), channel_id=1, source_target_pairs={{0,1},{1,0},{2,3},{3,2},{4,5},{5,4},{6,7},{7,6},{8,9},{9,8},{10,11... | collective-permute-start | bytes 786440 | tf_op jit(solution)/shard_map/ppermute | solution.py:377
  102.9 8.8 %collective-permute-start.8 = (bf16[64,2048]{1,0:T(8,128)(2,1)S(1)}, bf16[64,2048]{1,0:T(8,128)(2,1)S(1)}, u32[]{:S(2)}, u32[]{:S(2)}) collective-permute-start(bf16[64,2048]{1,0:T(8,128)(2,1)S(1)} %get-tuple-element.37), channel_id=1, source_target_pairs={{0,3},{1,2},{2,1},{3,0},{4,7},{5,6},{6,5},{7,4},{8,11},{9,10},{10,... | collective-permute-start | bytes 786440 | tf_op jit(solution)/shard_map/ppermute | solution.py:377
  111.7 3.0 %collective-permute-start.11 = (bf16[128,2048]{1,0:T(8,128)(2,1)S(1)}, bf16[128,2048]{1,0:T(8,128)(2,1)S(1)}, u32[]{:S(2)}, u32[]{:S(2)}) collective-permute-start(bf16[128,2048]{1,0:T(8,128)(2,1)S(1)} %constant_dynamic-update-slice_fusion.own_ref), channel_id=1, source_target_pairs={{0,64},{64,0},{1,65},{65,1},{2,66},{66,2},{3,67},{67,3},{4,68},{68... | collective-permute-start | bytes 1572872 | tf_op jit(solution)/shard_map/ppermute | solution.py:382
  116.0 1.3 collective-permute-start.12
  116.5 2.5 %collective-permute-start.10 = (f32[128]{0:T(128)S(1)}, f32[128]{0:T(128)S(1)}, u32[]{:S(2)}, u32[]{:S(2)}) collective-permute-start(f32[128]{0:T(128)S(1)} %bitcast.34), channel_id=1, source_target_pairs={{0,64},{1,65},{2,66},{3,67},{4,68},{5,69},{6,70},{7,71},{8,72},{9,... | collective-permute-start | bytes 1544 | tf_op jit(solution)/shard_map/ppermute | solution.py:390
  117.4 3.6 %collective-permute-start.14 = (f32[64]{0:T(128)S(1)}, f32[64]{0:T(128)S(1)}, u32[]{:S(2)}, u32[]{:S(2)}) collective-permute-start(f32[64]{0:T(128)S(1)} %get-tuple-element.42), channel_id=1, source_target_pairs={{0,3},{1,2},{2,1},{3,0},{4,7},{5,6},{6,5},{7,4},{8,11},{9,10},{10,... | collective-permute-start | bytes 776 | tf_op jit(solution)/shard_map/ppermute | solution.py:390
  119.0 2.4 %collective-permute-start.13 = (f32[64]{0:T(128)S(1)}, f32[64]{0:T(128)S(1)}, u32[]{:S(2)}, u32[]{:S(2)}) collective-permute-start(f32[64]{0:T(128)S(1)} %get-tuple-element.41), channel_id=1, source_target_pairs={{0,1},{1,0},{2,3},{3,2},{4,5},{5,4},{6,7},{7,6},{8,9},{9,8},{10,11... | collective-permute-start | bytes 776 | tf_op jit(solution)/shard_map/ppermute | solution.py:390
Sparse Core Ops, SparseCore 0:
  19.2 75.1 all-gather.1
